TPU v7x, 32 devices: a whole 2x2x4 slice. The times are simulated.
32 devices in a mesh: shard: 4 (over y, x), ctx: 8 (over z, core).
Axes of the slice: x: 2, y: 2, z: 4, core: 2. Of those that a mesh axis runs over, the one named last changes fastest.
Arguments:
- tokens: bfloat16 [8, 1024, 1280], P('shard', 'ctx'), may hold values from -6 to 6
- cotangent: bfloat16 [8, 1024, 1280], P('shard', 'ctx'), may hold values from -6 to 6
- positions: int32 [8, 1024], P('shard'), may hold values from 0 to 1023, as said below
- lengths: int32 [8], P('shard'), may hold values from 256 to 1024, as said below
- attn_gain: bfloat16 [1280], P('shard'), may hold values from 0.5 to 1.5
- w_query: bfloat16 [1280, 1280], P('shard'), may hold values from -0.15625 to 0.15625
- w_key: bfloat16 [1280, 320], P('shard'), may hold values from -0.15625 to 0.15625
- w_value: bfloat16 [1280, 320], P('shard'), may hold values from -0.15625 to 0.15625
- w_out: bfloat16 [1280, 1280], P('shard'), may hold values from -3 to 3
- mlp_gain: bfloat16 [1280], P('shard'), may hold values from 0.5 to 1.5
- w_gate: bfloat16 [1280, 3584], P(None, 'shard'), may hold values from -0.15625 to 0.15625
- w_up: bfloat16 [1280, 3584], P(None, 'shard'), may hold values from -0.15625 to 0.15625
- w_down: bfloat16 [3584, 1280], P('shard'), may hold values from -0.09375 to 0.09375
Outputs:
- output: bfloat16 [8, 1024, 1280], P('shard', 'ctx')
- d_tokens: bfloat16 [8, 1024, 1280], P('shard', 'ctx')
- d_attn_gain: float32 [1280], P('shard')
- d_w_query: float32 [1280, 1280], P('shard')
- d_w_key: float32 [1280, 320], P('shard')
- d_w_value: float32 [1280, 320], P('shard')
- d_w_out: float32 [1280, 1280], P('shard')
- d_mlp_gain: float32 [1280], P('shard')
- d_w_gate: float32 [1280, 3584], P(None, 'shard')
- d_w_up: float32 [1280, 3584], P(None, 'shard')
- d_w_down: float32 [3584, 1280], P('shard')
Inputs may be any that keep to these rules, and one draw needn't show every extreme that they name: In every sequence each position 0 to 1023 stands in exactly one slot; the 128 slots of one index of ctx hold two runs of 64 consecutive positions in rising order, run number a first and run number 2 * 8 - 1 - a second, with a drawn for each sequence and index. `lengths`: some sequence has length 1024 in every draw.
All inputs are finite; a program needn't handle non-finite values.
Results may differ from a plain program's by a relative error of at most 0.024.
Values may be sent and summed in bfloat16 or wider, within the bound.
A program may use at most 256 MiB of HBM per device.

v0:
```python
import math

import jax
import jax.numpy as jnp
from jax import lax
from jax.sharding import PartitionSpec as P

HQ = 20
HK = 5
HD = 64


EPSILON = 1e-05
NEGATIVE = -1e30
ROPE_BASE = 10000.0


def rope_parts(places):
    half_dim = HD // 2
    frequency = ROPE_BASE ** (-jnp.arange(half_dim, dtype=jnp.float32) * 2.0 / HD)
    angles = places.astype(jnp.float32)[..., None] * frequency
    return (jnp.cos(angles), jnp.sin(angles))


def rotate(values, cosine, sine_part):
    half_dim = values.shape[-1] // 2
    first_half = values[..., :half_dim]
    second_half = values[..., half_dim:]
    cosine_b = cosine[..., None, :]
    sine_b = sine_part[..., None, :]
    return jnp.concatenate(
        [
            first_half * cosine_b - second_half * sine_b,
            second_half * cosine_b + first_half * sine_b,
        ],
        -1,
    )


def row_norm(hidden, gain_vec):
    inv_scale = lax.rsqrt(jnp.mean(hidden * hidden, -1, keepdims=True) + EPSILON)
    return (hidden * inv_scale * gain_vec, inv_scale)


def norm_back(grad_norm, hidden, inv_scale, gain_vec):
    scaled = grad_norm * gain_vec
    grad_gain = jnp.sum(grad_norm * hidden * inv_scale, 0)
    grad_hidden = inv_scale * scaled - hidden * inv_scale**3 * jnp.mean(
        scaled * hidden, -1, keepdims=True
    )
    return (grad_hidden, grad_gain)


def product(left_side, right_side):
    return jnp.dot(left_side, right_side, preferred_element_type=jnp.float32)


def product_tn(left_side, right_side):
    return jnp.einsum("ra,rb->ab", left_side, right_side, preferred_element_type=jnp.float32)


def product_nt(left_side, right_side):
    return jnp.einsum("ra,ba->rb", left_side, right_side, preferred_element_type=jnp.float32)


def gate_back(grad_inner, gate_proj, up_proj):
    sigmoid_gate = jax.nn.sigmoid(gate_proj)
    grad_gate = (
        grad_inner * up_proj * sigmoid_gate * (1.0 + gate_proj * (1.0 - sigmoid_gate))
    ).astype(jnp.bfloat16)
    grad_up = (grad_inner * gate_proj * sigmoid_gate).astype(jnp.bfloat16)
    return (grad_gate, grad_up)


def block_scores(query_rot, key_piece, query_places, key_places, seq_lengths):
    micro_count, span_rows = (key_piece.shape[0], key_piece.shape[1])
    key_heads = key_piece.reshape(micro_count, span_rows, HK, HD)
    scores = jnp.einsum(
        "mqhgd,mkhd->mhgqk", query_rot, key_heads, preferred_element_type=jnp.float32
    ) * (1.0 / math.sqrt(HD))
    allowed = (key_places[:, None, :] <= query_places[:, :, None]) & (
        key_places < seq_lengths[:, None]
    )[:, None, :]
    return (scores, allowed[:, None, None])


def over_blocks(span_rows, block_rows, step_fn, carried):
    sub_rows = math.gcd(span_rows, block_rows)

    def one_step(fold_state, block_index):
        return (step_fn(fold_state, block_index * sub_rows, sub_rows), None)

    final_state, unused = lax.scan(one_step, carried, jnp.arange(span_rows // sub_rows))
    return final_state


def per_device(
    tokens,
    cotangent,
    positions,
    lengths,
    attn_gain,
    w_query,
    w_key,
    w_value,
    w_out,
    mlp_gain,
    w_gate,
    w_up,
    w_down,
):
    micro_count, stretch_len, model_width = tokens.shape
    ctx_count = lax.axis_size("ctx")
    full_len = stretch_len * ctx_count
    row_count = micro_count * stretch_len
    query_width = HQ * HD
    kv_width = HK * HD
    group_size = HQ // HK
    factor = 1.0 / math.sqrt(HD)
    block_rows = stretch_len * math.gcd(ctx_count, max(1, 512 // stretch_len))
    rank_ctx = lax.axis_index("ctx")
    query_places = lax.dynamic_slice_in_dim(positions, rank_ctx * stretch_len, stretch_len, 1)
    valid_rows = (query_places < lengths[:, None]).astype(jnp.float32).reshape(row_count, 1)
    cosine, sine_part = rope_parts(query_places.reshape(row_count))
    gain_one, gain_two, query_all, key_all, value_all, out_all = (
        lax.all_gather(attn_gain, "shard", axis=0, tiled=True),
        lax.all_gather(mlp_gain, "shard", axis=0, tiled=True),
        lax.all_gather(w_query, "shard", axis=0, tiled=True),
        lax.all_gather(w_key, "shard", axis=0, tiled=True),
        lax.all_gather(w_value, "shard", axis=0, tiled=True),
        lax.all_gather(w_out, "shard", axis=0, tiled=True),
    )
    hidden = tokens.reshape(row_count, model_width).astype(jnp.float32)
    normed_one, inv_one = row_norm(hidden, gain_one.astype(jnp.float32))
    norm_one = normed_one.astype(jnp.bfloat16)
    queries = product(norm_one, query_all)
    key_proj = product(norm_one, key_all)
    value_low = (
        product(norm_one, value_all)
        .astype(jnp.bfloat16)
        .reshape(micro_count, stretch_len, kv_width)
    )
    query_rot = (
        rotate(queries.reshape(row_count, HQ, HD), cosine, sine_part)
        .astype(jnp.bfloat16)
        .reshape(micro_count, stretch_len, HK, group_size, HD)
    )
    key_rot = (
        rotate(key_proj.reshape(row_count, HK, HD), cosine, sine_part)
        .astype(jnp.bfloat16)
        .reshape(micro_count, stretch_len, kv_width)
    )

    def attend_rows(fold_state, key_piece, value_piece, first_row):
        run_max, run_sum, run_acc = fold_state
        span_rows = key_piece.shape[1]
        key_places = lax.dynamic_slice_in_dim(positions, first_row, span_rows, 1)
        scores, allowed = block_scores(query_rot, key_piece, query_places, key_places, lengths)
        masked = jnp.where(allowed, scores, NEGATIVE)
        new_max = jnp.maximum(run_max, jnp.max(masked, -1))
        weights = jnp.where(allowed, jnp.exp(masked - new_max[..., None]), 0.0)
        factor_old = jnp.exp(run_max - new_max)
        new_sum = run_sum * factor_old + jnp.sum(weights, -1)
        update = jnp.einsum(
            "mhgqk,mkhd->mqhgd",
            weights.astype(jnp.bfloat16),
            value_piece.reshape(micro_count, span_rows, HK, HD),
            preferred_element_type=jnp.float32,
        )
        rescale = jnp.transpose(factor_old, (0, 3, 1, 2))[..., None]
        return (new_max, new_sum, run_acc * rescale + update)

    initial = (
        jnp.full((micro_count, HK, group_size, stretch_len), NEGATIVE, jnp.float32),
        jnp.zeros((micro_count, HK, group_size, stretch_len), jnp.float32),
        jnp.zeros((micro_count, stretch_len, HK, group_size, HD), jnp.float32),
    )
    key_piece = lax.all_gather(key_rot, "ctx", axis=1, tiled=True)
    value_piece = lax.all_gather(value_low, "ctx", axis=1, tiled=True)

    def step_fn(inner_state, offset, sub_rows):
        key_sub = lax.dynamic_slice_in_dim(key_piece, offset, sub_rows, 1)
        value_sub = lax.dynamic_slice_in_dim(value_piece, offset, sub_rows, 1)
        return attend_rows(inner_state, key_sub, value_sub, offset)

    run_max, run_sum, run_acc = over_blocks(key_piece.shape[1], block_rows, step_fn, initial)
    log_sum = run_max + jnp.log(run_sum)
    attended = run_acc / jnp.transpose(run_sum, (0, 3, 1, 2))[..., None]
    attn_low = attended.reshape(row_count, query_width).astype(jnp.bfloat16)
    middle = hidden + product(attn_low, out_all)
    gain_two_f = gain_two.astype(jnp.float32)
    normed_two, inv_two = row_norm(middle, gain_two_f)
    norm_two = normed_two.astype(jnp.bfloat16)
    gate_all, up_all, down_all = (
        lax.all_gather(w_gate, "shard", axis=1, tiled=True),
        lax.all_gather(w_up, "shard", axis=1, tiled=True),
        lax.all_gather(w_down, "shard", axis=0, tiled=True),
    )
    gate_proj = product(norm_two, gate_all)
    up_proj = product(norm_two, up_all)
    inner_act = (jax.nn.silu(gate_proj) * up_proj).astype(jnp.bfloat16)
    mlp_out = product(inner_act, down_all)
    result = (middle + mlp_out).astype(jnp.bfloat16).reshape(micro_count, stretch_len, model_width)
    gain_one, gain_two, query_all, key_all, value_all, out_all = (
        lax.all_gather(attn_gain, "shard", axis=0, tiled=True),
        lax.all_gather(mlp_gain, "shard", axis=0, tiled=True),
        lax.all_gather(w_query, "shard", axis=0, tiled=True),
        lax.all_gather(w_key, "shard", axis=0, tiled=True),
        lax.all_gather(w_value, "shard", axis=0, tiled=True),
        lax.all_gather(w_out, "shard", axis=0, tiled=True),
    )
    gain_two_f = gain_two.astype(jnp.float32)
    grad_out = cotangent.reshape(row_count, model_width).astype(jnp.float32) * valid_rows
    grad_low = grad_out.astype(jnp.bfloat16)
    gate_all, up_all, down_all = (
        lax.all_gather(w_gate, "shard", axis=1, tiled=True),
        lax.all_gather(w_up, "shard", axis=1, tiled=True),
        lax.all_gather(w_down, "shard", axis=0, tiled=True),
    )
    grad_wdown = product_tn(inner_act, grad_low)
    grad_inner = product_nt(grad_low, down_all)
    grad_gate, grad_up = gate_back(grad_inner, gate_proj, up_proj)
    grad_wgate = product_tn(norm_two, grad_gate)
    grad_wup = product_tn(norm_two, grad_up)
    grad_norm_two = product_nt(grad_gate, gate_all) + product_nt(grad_up, up_all)
    grad_mid_norm, grad_gain_two = norm_back(grad_norm_two, middle, inv_two, gain_two_f)
    grad_middle = grad_out + grad_mid_norm
    grad_proj = grad_middle.astype(jnp.bfloat16)
    grad_wout = product_tn(attn_low, grad_proj)
    grad_attn = (
        product_nt(grad_proj, out_all)
        .astype(jnp.bfloat16)
        .reshape(micro_count, stretch_len, HK, group_size, HD)
    )
    row_delta = jnp.transpose(jnp.sum(grad_attn.astype(jnp.float32) * attended, -1), (0, 2, 3, 1))
    key_full, value_full = (
        lax.all_gather(key_rot, "ctx", axis=1, tiled=True),
        lax.all_gather(value_low, "ctx", axis=1, tiled=True),
    )

    def grad_block(key_piece, value_piece, first_row):
        span_rows = key_piece.shape[1]
        key_places = lax.dynamic_slice_in_dim(positions, first_row, span_rows, 1)
        scores, allowed = block_scores(query_rot, key_piece, query_places, key_places, lengths)
        softmax = jnp.where(allowed, jnp.exp(scores - log_sum[..., None]), 0.0)
        grad_soft = jnp.einsum(
            "mqhgd,mkhd->mhgqk",
            grad_attn,
            value_piece.reshape(micro_count, span_rows, HK, HD),
            preferred_element_type=jnp.float32,
        )
        grad_score = (softmax * (grad_soft - row_delta[..., None])).astype(jnp.bfloat16)
        return (softmax, grad_score)

    def query_step(grad_acc, offset, sub_rows):
        key_piece = lax.dynamic_slice_in_dim(key_full, offset, sub_rows, 1)
        value_piece = lax.dynamic_slice_in_dim(value_full, offset, sub_rows, 1)
        softmax, grad_score = grad_block(key_piece, value_piece, offset)
        return grad_acc + jnp.einsum(
            "mhgqk,mkhd->mqhgd",
            grad_score,
            key_piece.reshape(micro_count, sub_rows, HK, HD),
            preferred_element_type=jnp.float32,
        )

    grad_qrot = (
        over_blocks(
            full_len,
            block_rows,
            query_step,
            jnp.zeros((micro_count, stretch_len, HK, group_size, HD), jnp.float32),
        )
        * factor
    )
    span_rows = stretch_len * lax.axis_size("ctx")
    sub_rows = math.gcd(span_rows, block_rows)

    def one_piece(block_index):
        offset = block_index * sub_rows
        key_piece = lax.dynamic_slice_in_dim(key_full, offset, sub_rows, 1)
        value_piece = lax.dynamic_slice_in_dim(value_full, offset, sub_rows, 1)
        softmax, grad_score = grad_block(key_piece, value_piece, offset)
        grad_val = jnp.einsum(
            "mhgqk,mqhgd->kmhd",
            softmax.astype(jnp.bfloat16),
            grad_attn,
            preferred_element_type=jnp.float32,
        )
        grad_key = (
            jnp.einsum(
                "mhgqk,mqhgd->kmhd", grad_score, query_rot, preferred_element_type=jnp.float32
            )
            * factor
        )
        return jnp.concatenate(
            [
                grad_key.reshape(sub_rows, micro_count, kv_width),
                grad_val.reshape(sub_rows, micro_count, kv_width),
            ],
            -1,
        )

    stacked = lax.map(one_piece, jnp.arange(span_rows // sub_rows))
    grad_kv = lax.psum_scatter(
        stacked.reshape(span_rows, micro_count, 2 * kv_width).astype(jnp.bfloat16),
        "ctx",
        scatter_dimension=0,
        tiled=True,
    ).astype(jnp.float32)
    grad_kv = jnp.transpose(grad_kv, (1, 0, 2)).reshape(row_count, 2 * kv_width)
    grad_queries = (
        rotate(grad_qrot.reshape(row_count, HQ, HD), cosine, -sine_part)
        .reshape(row_count, query_width)
        .astype(jnp.bfloat16)
    )
    grad_keys = (
        rotate(grad_kv[:, :kv_width].reshape(row_count, HK, HD), cosine, -sine_part)
        .reshape(row_count, kv_width)
        .astype(jnp.bfloat16)
    )
    grad_values = grad_kv[:, kv_width:].astype(jnp.bfloat16)
    grad_wquery = product_tn(norm_one, grad_queries)
    grad_wkey = product_tn(norm_one, grad_keys)
    grad_wvalue = product_tn(norm_one, grad_values)
    grad_norm_one = (
        product_nt(grad_queries, query_all)
        + product_nt(grad_keys, key_all)
        + product_nt(grad_values, value_all)
    )
    grad_hidden, grad_gain_one = norm_back(
        grad_norm_one, hidden, inv_one, gain_one.astype(jnp.float32)
    )
    grad_input = (
        (grad_middle + grad_hidden)
        .astype(jnp.bfloat16)
        .reshape(micro_count, stretch_len, model_width)
    )
    (
        share_gain_one,
        share_wquery,
        share_wkey,
        share_wvalue,
        share_wout,
        share_gain_two,
        share_wgate,
        share_wup,
        share_wdown,
    ) = (
        lax.psum_scatter(
            grad_gain_one.astype(jnp.bfloat16), "shard", scatter_dimension=0, tiled=True
        ).astype(jnp.float32),
        lax.psum_scatter(
            grad_wquery.astype(jnp.bfloat16), "shard", scatter_dimension=0, tiled=True
        ).astype(jnp.float32),
        lax.psum_scatter(
            grad_wkey.astype(jnp.bfloat16), "shard", scatter_dimension=0, tiled=True
        ).astype(jnp.float32),
        lax.psum_scatter(
            grad_wvalue.astype(jnp.bfloat16), "shard", scatter_dimension=0, tiled=True
        ).astype(jnp.float32),
        lax.psum_scatter(
            grad_wout.astype(jnp.bfloat16), "shard", scatter_dimension=0, tiled=True
        ).astype(jnp.float32),
        lax.psum_scatter(
            grad_gain_two.astype(jnp.bfloat16), "shard", scatter_dimension=0, tiled=True
        ).astype(jnp.float32),
        lax.psum_scatter(
            grad_wgate.astype(jnp.bfloat16), "shard", scatter_dimension=1, tiled=True
        ).astype(jnp.float32),
        lax.psum_scatter(
            grad_wup.astype(jnp.bfloat16), "shard", scatter_dimension=1, tiled=True
        ).astype(jnp.float32),
        lax.psum_scatter(
            grad_wdown.astype(jnp.bfloat16), "shard", scatter_dimension=0, tiled=True
        ).astype(jnp.float32),
    )
    totals = (
        lax.psum(share_gain_one.astype(jnp.bfloat16), "ctx").astype(jnp.float32),
        lax.psum(share_wquery.astype(jnp.bfloat16), "ctx").astype(jnp.float32),
        lax.psum(share_wkey.astype(jnp.bfloat16), "ctx").astype(jnp.float32),
        lax.psum(share_wvalue.astype(jnp.bfloat16), "ctx").astype(jnp.float32),
        lax.psum(share_wout.astype(jnp.bfloat16), "ctx").astype(jnp.float32),
        lax.psum(share_gain_two.astype(jnp.bfloat16), "ctx").astype(jnp.float32),
        lax.psum(share_wgate.astype(jnp.bfloat16), "ctx").astype(jnp.float32),
        lax.psum(share_wup.astype(jnp.bfloat16), "ctx").astype(jnp.float32),
        lax.psum(share_wdown.astype(jnp.bfloat16), "ctx").astype(jnp.float32),
    )
    return (
        result,
        grad_input,
        totals[0],
        totals[1],
        totals[2],
        totals[3],
        totals[4],
        totals[5],
        totals[6],
        totals[7],
        totals[8],
    )


def solution(mesh):
    return jax.shard_map(
        per_device,
        mesh=mesh,
        in_specs=(
            P("shard", "ctx", None),
            P("shard", "ctx", None),
            P("shard", None),
            P("shard"),
            P("shard"),
            P("shard", None),
            P("shard", None),
            P("shard", None),
            P("shard", None),
            P("shard"),
            P(None, "shard"),
            P(None, "shard"),
            P("shard", None),
        ),
        out_specs=(
            P("shard", "ctx", None),
            P("shard", "ctx", None),
            P("shard"),
            P("shard", None),
            P("shard", None),
            P("shard", None),
            P("shard", None),
            P("shard"),
            P(None, "shard"),
            P(None, "shard"),
            P("shard", None),
        ),
        check_vma=False,
    )
```

profile of v0, /device:TPU:0, one launch (start us, length us, event | category | flops | bytes accessed | tf_op | source)
XLA Modules:
  0.0 1232.8 jit_solution(15737660514148302673)
XLA Ops:
  11.8 11.5 all-reduce.7
  23.4 16.6 %all_gather.45 = bf16[1280,320]{1,0:T(8,128)(2,1)S(1)} all-gather(bf16[320,320]{1,0:T(8,128)(2,1)} %param.25), channel_id=1, replica_groups=mesh['shard'=4,'ctx'=8] {'shard'}, dimensions={0}, use_global_device_ids=true | all-gather | bytes 1024000 | tf_op jit(solution)/shard_map/all_gather | solution.py:129
  43.3 22.3 %all_gather.48 = bf16[1280,320]{1,0:T(8,128)(2,1)S(1)} all-gather(bf16[320,320]{1,0:T(8,128)(2,1)} %param.26), channel_id=1, replica_groups=mesh['shard'=4,'ctx'=8] {'shard'}, dimensions={0}, use_global_device_ids=true | all-gather | bytes 1024000 | tf_op jit(solution)/shard_map/all_gather | solution.py:130
  71.0 5.9 copy.65
  76.9 3.0 fusion.89
  80.4 17.9 %all-gather.8.cloned.1.call-done = bf16[2,1024,320]{1,2,0:T(8,128)(2,1)} async-done(((bf16[2,128,320]{1,2,0:T(8,128)(2,1)}), bf16[2,1024,320]{1,2,0:T(8,128)(2,1)}) %all-gather.8.cloned.1.call-update) | async-done | bytes 1310736 | tf_op jit(solution)/shard_map/all_gather | solution.py:178
  98.3 26.9 %all-gather.12.cloned.1.call-done = bf16[2,1024,320]{1,2,0:T(8,128)(2,1)} async-done(((bf16[2,128,320]{1,2,0:T(8,128)(2,1)}), bf16[2,1024,320]{1,2,0:T(8,128)(2,1)}) %all-gather.12.cloned.1.call-update) | async-done | bytes 1310736 | tf_op jit(solution)/shard_map/all_gather | solution.py:179
  125.3 40.2 %while.37 = (s32[]{:T(128)}, f32[2,5,4,128]{3,2,1,0:T(4,128)S(1)}, f32[2,5,4,128]{3,2,1,0:T(4,128)S(1)}, f32[2,128,5,4,64]{1,4,3,2,0:T(8,128)}, s32[2]{0:T(128)S...) while((s32[]{:T(128)}, f32[2,5,4,128]{3,2,1,0:T(4,128)S(1)}, ...), condition=%wide.region_4.5_spmd.clone, body=%wide.region_1.4_spmd.clone.sunk | while | flops 706444288 | bytes 81476864 | solution.py:93
  128.3 5.6 fusion.187
  134.0 7.0 fusion.189
  141.2 3.6 fusion.191
  147.9 5.6 fusion.187
  153.5 6.8 fusion.189
  160.5 4.7 fusion.191
  165.5 4.1 fusion.84
  171.0 3.3 multiply_reduce_fusion.3
  174.5 92.2 %all-gather.16.cloned.1.call-done = bf16[1280,3584]{1,0:T(8,128)(2,1)} async-done(((bf16[1280,896]{1,0:T(8,128)(2,1)}), bf16[1280,3584]{1,0:T(8,128)(2,1)}) %all-gather.16.cloned.1.call-update) | async-done | bytes 9175056 | tf_op jit(solution)/shard_map/all_gather | solution.py:195
  266.7 8.0 fusion.90
  274.7 87.8 %all-gather.18.cloned.1.call-done = bf16[1280,3584]{1,0:T(8,128)(2,1)} async-done(((bf16[1280,896]{1,0:T(8,128)(2,1)}), bf16[1280,3584]{1,0:T(8,128)(2,1)}) %all-gather.18.cloned.1.call-update) | async-done | bytes 9175056 | tf_op jit(solution)/shard_map/all_gather | solution.py:196
  362.5 8.0 fusion.91
  370.4 87.9 %all-gather.20.cloned.1.call-done = bf16[3584,1280]{1,0:T(8,128)(2,1)} async-done(((bf16[896,1280]{1,0:T(8,128)(2,1)}), bf16[3584,1280]{1,0:T(8,128)(2,1)}) %all-gather.20.cloned.1.call-update) | async-done | bytes 9175056 | tf_op jit(solution)/shard_map/all_gather | solution.py:197
  458.4 12.0 multiply_convert_fusion
  470.4 7.6 fusion.92
  478.0 3.3 multiply_reduce_fusion
  486.2 2.0 multiply_reduce_fusion.1
  488.3 49.6 %while.36 = (s32[]{:T(128)}, bf16[2,512,2,640]{3,1,0,2:T(8,128)(2,1)}, s32[2]{0:T(128)S(1)}, s32[2,1024]{1,0:T(2,128)S(1)}, s32[2,128]{1,0:T(2,128)S(1)}, /*inde...) while((s32[]{:T(128)}, ...), condition=%wide.region_11.12_spmd, body=%wide.region_10.11_spmd.sunk | while | flops 1371931648 | bytes 97463624 | solution.py:303
  498.3 2.0 constant_dynamic-slice_fusion.17
  500.3 1.6 fusion.180
  502.3 3.9 fusion.181
  506.2 8.6 fusion.182
  518.7 2.1 constant_dynamic-slice_fusion.17
  522.8 3.9 fusion.181
  526.7 8.6 fusion.182
  539.0 7.5 convolution_convert_fusion.2
  546.5 12.8 %copy.91 = bf16[1280,3584]{0,1:T(8,128)(2,1)} copy(bf16[1280,3584]{1,0:T(8,128)(2,1)} %convolution_convert_fusion.2) | data formatting | bytes 18350080
  559.4 7.7 convolution_convert_fusion.1
  567.1 13.0 %copy.93 = bf16[1280,3584]{0,1:T(8,128)(2,1)} copy(bf16[1280,3584]{1,0:T(8,128)(2,1)} %convolution_convert_fusion.1) | data formatting | bytes 18350080
  580.2 36.6 %while.38 = (s32[]{:T(128)}, f32[2,128,5,4,64]{1,4,3,2,0:T(8,128)}, s32[2]{0:T(128)S(1)}, bf16[2,1024,320]{1,2,0:T(8,128)(2,1)S(1)}, s32[2,1024]{1,0:T(2,128)S(1...) while((s32[]{:T(128)}, f32[2,128,5,4,64]{1,4,3,2,0:T(8,128)}, ...), condition=%wide.region_9.10_spmd.clone, body=%wide.region_8.9_spmd.clone.sunk | while | flops 1023280128 | bytes 29809904 | solution.py:93
  582.6 5.7 fusion.198
  588.7 9.7 fusion.199
  600.8 5.4 fusion.198
  606.7 10.1 fusion.199
  621.4 2.8 convolution_convert_fusion.4
  625.7 2.7 convolution_convert_fusion.3
  631.3 2.6 convolution_convert_fusion.5
  634.2 7.6 convolution_convert_fusion
  641.9 29.2 %reduce-scatter.25.cloned.1.call-done = bf16[896,1280]{1,0:T(8,128)(2,1)} async-done(((bf16[3584,1280]{1,0:T(8,128)(2,1)}), bf16[896,1280]{1,0:T(8,128)(2,1)}) %reduce-scatter.25.cloned.1.call-update) | async-done | bytes 2293776
  671.1 4.3 copy.92
  675.4 91.5 %reduce-scatter.27.cloned.1.call-done = bf16[896,1280]{1,0:T(8,128)(2,1)} async-done(((bf16[3584,1280]{1,0:T(8,128)(2,1)}), bf16[896,1280]{1,0:T(8,128)(2,1)}) %reduce-scatter.27.cloned.1.call-update) | async-done | bytes 2293776
  766.9 4.3 copy.94
  771.3 44.3 %reduce-scatter.15.cloned.1.call-done = bf16[320,1280]{1,0:T(8,128)(2,1)} async-done(((bf16[1280,1280]{1,0:T(8,128)(2,1)}), bf16[320,1280]{1,0:T(8,128)(2,1)}) %reduce-scatter.15.cloned.1.call-update) | async-done | bytes 819216 | tf_op jit(solution)/shard_map/reduce_scatter | solution.py:352
  815.6 48.5 %reduce-scatter.21.cloned.1.call-done = bf16[320,1280]{1,0:T(8,128)(2,1)} async-done(((bf16[1280,1280]{1,0:T(8,128)(2,1)}), bf16[320,1280]{1,0:T(8,128)(2,1)}) %reduce-scatter.21.cloned.1.call-update) | async-done | bytes 819216 | tf_op jit(solution)/shard_map/reduce_scatter | solution.py:361
  864.0 31.0 %reduce-scatter.17.cloned.1.call-done = bf16[320,320]{1,0:T(8,128)(2,1)} async-done(((bf16[1280,320]{1,0:T(8,128)(2,1)}), bf16[320,320]{1,0:T(8,128)(2,1)}) %reduce-scatter.17.cloned.1.call-update) | async-done | bytes 204816 | tf_op jit(solution)/shard_map/reduce_scatter | solution.py:355
  895.0 30.3 %reduce-scatter.19.cloned.1.call-done = bf16[320,320]{1,0:T(8,128)(2,1)} async-done(((bf16[1280,320]{1,0:T(8,128)(2,1)}), bf16[320,320]{1,0:T(8,128)(2,1)}) %reduce-scatter.19.cloned.1.call-update) | async-done | bytes 204816 | tf_op jit(solution)/shard_map/reduce_scatter | solution.py:358
  925.4 95.8 %reduce-scatter.23.cloned.1.call-done = bf16[896,1280]{1,0:T(8,128)(2,1)} async-done(((bf16[3584,1280]{1,0:T(8,128)(2,1)}), bf16[896,1280]{1,0:T(8,128)(2,1)}) %reduce-scatter.23.cloned.1.call-update) | async-done | bytes 2293776 | tf_op jit(solution)/shard_map/reduce_scatter | solution.py:373
  1021.9 3.1 fusion.93
  1025.1 7.1 fusion.57
  1034.4 9.1 all-reduce.6
  1043.7 15.4 %all-reduce.4 = (bf16[320]{0:T(512)(128)(2,1)S(1)}, bf16[320]{0:T(512)(128)(2,1)S(1)}) all-reduce(bf16[320]{0:T(512)(128)(2,1)S(1)} %dynamic-slice.3, bf16[320]{0:T(512)(128)(2,1)S(1)} %dynamic-slice.5), channel_id=1, replica_groups=mesh['shard'=4,'ctx'=8] {'ctx'}, use_global_device_ids=true, to_apply=%region_16.17 | all-reduce | flops 640 | bytes 2560 | tf_op jit(solution)/shard_map/psum | solution.py:378
  1061.5 151.3 %all-reduce.10.cloned.1.call-done = (bf16[320,1280]{1,0:T(8,128)(2,1)}, bf16[320,320]{1,0:T(8,128)(2,1)}, bf16[320,320]{1,0:T(8,128)(2,1)}, bf16[320,1280]{1,0:T...) async-done(((bf16[320,1280]{1,0:T(8,128)(2,1)}, bf16[320,320]{1,0:T(8,128)(2,1)}, bf16[320,320]{1,0:T(8,128)(2,1)}, ...) | async-done | bytes 8929296 | tf_op jit(solution)/shard_map/psum | solution.py:379
  1212.8 2.5 convert_element_type.248
  1218.2 2.4 convert_element_type.258
  1220.8 2.4 convert_element_type.260
  1223.3 2.5 convert_element_type.262
  (249 shorter events, 55.9 us)
Async XLA Ops:
  7.2 33.5 %copy-start.4 = (bf16[2,128,1280]{2,1,0:T(8,128)(2,1)S(1)}, bf16[2,128,1280]{2,1,0:T(8,128)(2,1)}, u32[]{:S(2)}) copy-start(bf16[2,128,1280]{2,1,0:T(8,128)(2,1)} %param.19) | copy-start | bytes 1966084
  7.2 63.8 %all-gather.10.cloned.1.call-start = ((), (), s32[]{:S(2)}) async-start(), calls=%async_computation.9 | async-start | bytes 4096000 | tf_op jit(solution)/shard_map/all_gather | solution.py:128
  7.9 32.9 %copy-start.36 = (s32[2,1024]{1,0:T(2,128)S(1)}, s32[2,1024]{1,0:T(2,128)}, u32[]{:S(2)}) copy-start(s32[2,1024]{1,0:T(2,128)} %param.21) | copy-start | bytes 24580
  7.9 32.9 %copy-start.42 = (s32[2]{0:T(128)S(1)}, s32[2]{0:T(128)}, u32[]{:S(2)}) copy-start(s32[2]{0:T(128)} %param.22) | copy-start | bytes 28
  7.9 90.4 %all-gather.8.cloned.1.call-start = ((), (), s32[]{:S(2)}) async-start(), calls=%async_computation.8 | async-start | bytes 1474560 | tf_op jit(solution)/shard_map/all_gather | solution.py:178
  23.4 42.3 %copy-start.40 = (f32[1280]{0:T(1024)}, f32[1280]{0:T(1024)S(1)}, u32[]{:S(2)}) copy-start(f32[1280]{0:T(1024)S(1)} %convert_element_type.216) | copy-start | bytes 15364
  40.0 2.4 copy-start.11
  40.9 1.6 copy-start.45
  41.0 24.7 %copy-start.43 = (f32[256]{0:T(256)}, f32[256]{0:T(256)S(1)}, u32[]{:S(2)}) copy-start(f32[256]{0:T(256)S(1)} %get-tuple-element.479) | copy-start | bytes 3076
  41.8 38.1 %copy-start.33 = (f32[256,32]{0,1:T(8,128)}, f32[256,32]{0,1:T(8,128)S(1)}, u32[]{:S(2)}) copy-start(f32[256,32]{0,1:T(8,128)S(1)} %get-tuple-element.476) | copy-start | bytes 98308
  42.0 34.9 %copy-start.7 = (bf16[2,128,1280]{2,1,0:T(8,128)(2,1)}, bf16[2,128,1280]{2,1,0:T(8,128)(2,1)S(1)}, u32[]{:S(2)}) copy-start(bf16[2,128,1280]{2,1,0:T(8,128)(2,1)S(1)} %fusion.62) | copy-start | bytes 1966084
  43.3 82.0 %all-gather.12.cloned.1.call-start = ((), (), s32[]{:S(2)}) async-start(), calls=%async_computation.10 | async-start | bytes 1474560 | tf_op jit(solution)/shard_map/all_gather | solution.py:179
  68.1 102.8 %all-gather.14.cloned.1.call-start = ((), (), s32[]{:S(2)}) async-start(), calls=%async_computation.11 | async-start | bytes 4096000 | tf_op jit(solution)/shard_map/all_gather | solution.py:131
  68.7 198.0 %all-gather.16.cloned.1.call-start = ((), (), s32[]{:S(2)}) async-start(), calls=%async_computation.12 | async-start | bytes 11468800 | tf_op jit(solution)/shard_map/all_gather | solution.py:195
  69.3 1.4 copy-start.25
  69.3 293.1 %all-gather.18.cloned.1.call-start = ((), (), s32[]{:S(2)}) async-start(), calls=%async_computation.13 | async-start | bytes 11468800 | tf_op jit(solution)/shard_map/all_gather | solution.py:196
  69.9 388.5 %all-gather.20.cloned.1.call-start = ((), (), s32[]{:S(2)}) async-start(), calls=%async_computation.14 | async-start | bytes 11468800 | tf_op jit(solution)/shard_map/all_gather | solution.py:197
  70.6 557.9 %reduce-scatter.13.cloned.1.call-start = ((), (), s32[]{:S(2)}) async-start(), calls=%async_computation.15 | async-start | bytes 2949120 | tf_op jit(solution)/shard_map/reduce_scatter | solution.py:304
  70.9 387.4 %copy-start.22 = (bf16[256,1280]{1,0:T(8,128)(2,1)}, bf16[256,1280]{1,0:T(8,128)(2,1)S(1)}, u32[]{:S(2)}) copy-start(bf16[256,1280]{1,0:T(8,128)(2,1)S(1)} %fusion.59) | copy-start | bytes 1966084
  134.0 7.2 copy-start
  153.5 7.0 copy-start
  174.2 307.1 %copy-start.19 = (f32[256,1280]{1,0:T(8,128)}, f32[256,1280]{1,0:T(8,128)S(1)}, u32[]{:S(2)}) copy-start(f32[256,1280]{1,0:T(8,128)S(1)} %get-tuple-element.484) | copy-start | bytes 3932164
  174.5 188.0 %copy-start.15 = (bf16[256,1280]{1,0:T(8,128)(2,1)}, bf16[256,1280]{1,0:T(8,128)(2,1)S(1)}, u32[]{:S(2)}) copy-start(bf16[256,1280]{1,0:T(8,128)(2,1)S(1)} %multiply_convert_fusion.3) | copy-start | bytes 1966084
  470.4 7.6 copy-start.31
  470.4 7.6 copy-start.30
  470.4 7.6 copy-start.48
  478.0 3.4 copy-start.26
  481.3 2.4 copy-start.49
  485.2 3.1 copy-start.2
  501.9 4.3 copy-start.1
  502.3 3.9 copy-start.6
  515.7 1.8 copy-start.3
  522.3 4.3 copy-start.1
  522.8 3.9 copy-start.6
  536.1 1.8 copy-start.3
  538.0 133.2 %reduce-scatter.25.cloned.1.call-start = ((), (), s32[]{:S(2)}) async-start(), calls=%async_computation.21 | async-start | bytes 11468800
  559.4 207.6 %reduce-scatter.27.cloned.1.call-start = ((), (), s32[]{:S(2)}) async-start(), calls=%async_computation.22 | async-start | bytes 11468800
  580.1 235.4 %reduce-scatter.15.cloned.1.call-start = ((), (), s32[]{:S(2)}) async-start(), calls=%async_computation.16 | async-start | bytes 4096000 | tf_op jit(solution)/shard_map/reduce_scatter | solution.py:352
  619.3 1.1 copy-start.34
  619.3 1.1 copy-start.37
  620.3 1.1 copy-start.8
  624.2 1.3 copy-start.10
  624.2 1.5 copy-start.24
  624.2 239.8 %reduce-scatter.21.cloned.1.call-start = ((), (), s32[]{:S(2)}) async-start(), calls=%async_computation.19 | async-start | bytes 4096000 | tf_op jit(solution)/shard_map/reduce_scatter | solution.py:361
  628.5 266.6 %reduce-scatter.17.cloned.1.call-start = ((), (), s32[]{:S(2)}) async-start(), calls=%async_computation.17 | async-start | bytes 1228800 | tf_op jit(solution)/shard_map/reduce_scatter | solution.py:355
  629.6 1.7 copy-start.18
  631.2 3.0 copy-start.23
  631.3 294.1 %reduce-scatter.19.cloned.1.call-start = ((), (), s32[]{:S(2)}) async-start(), calls=%async_computation.18 | async-start | bytes 1228800 | tf_op jit(solution)/shard_map/reduce_scatter | solution.py:358
  633.9 387.3 %reduce-scatter.23.cloned.1.call-start = ((), (), s32[]{:S(2)}) async-start(), calls=%async_computation.20 | async-start | bytes 11468800 | tf_op jit(solution)/shard_map/reduce_scatter | solution.py:373
  641.9 570.9 %all-reduce.10.cloned.1.call-start = ((), (), s32[]{:S(2)}) async-start(), calls=%async_computation.23 | async-start | bytes 18022400 | tf_op jit(solution)/shard_map/psum | solution.py:379
  1021.9 3.2 copy-start.20
  1021.9 3.2 copy-start.21
  1025.1 7.1 copy-start.12
  1032.2 1.1 copy-start.5
  1032.2 1.4 copy-start.14
  1032.2 1.5 copy-start.32
  1032.2 1.5 copy-start.41
  1032.2 1.5 copy-start.44
  1212.8 2.5 copy-start.39
  1212.8 3.3 copy-start.38
  1212.8 4.2 copy-start.35
  1215.3 2.9 copy-start.29
  1218.2 2.6 copy-start.28
  1220.8 2.6 copy-start.27
  (6 other events, 5.5 us)
Sparse Core Ops, SparseCore 0:
  9.8 60.5 all-gather.9
  72.6 25.6 all-gather.7
  100.5 24.7 all-gather.11
  127.0 43.9 all-gather.13
  172.7 94.0 all-gather.15
  268.4 94.0 all-gather.17
  364.3 94.0 all-gather.19
  538.1 37.7 reduce-scatter.12
  579.1 92.0 reduce-scatter.24
  674.2 92.7 reduce-scatter.26
  770.5 44.9 reduce-scatter.14
  819.0 44.9 reduce-scatter.20
  867.5 27.4 reduce-scatter.16
  897.9 27.4 reduce-scatter.18
  928.4 92.7 reduce-scatter.22
  1024.6 188.1 all-reduce.9
where the time goes:
time: 1240 us; the launch traced here: 1230 us
  waiting for transfers between devices  839 us (68%)
  matrix products  170 us (14%)
  local copies, waits for them, and re-layouts  76 us (6%)
  blocking collectives  75 us (6%)
  other arithmetic  42.3 us (3%)
  between operations  16.5 us (1%)
  loops' own time  13.2 us (1%)
    psum x1, waiting for transfers between devices, per_device(): lax.psum(share_wquery.astype(jnp.bfloat16), 'ctx').astype(jnp.float32)  151 us
    unnamed x18, waiting for transfers between devices  124 us
    reduce_scatter x1, waiting for transfers between devices, per_device(): lax.psum_scatter(grad_wdown.astype(jnp.bfloat16), 'shard', scatter_dimens...  95.8 us
    all_gather x1, waiting for transfers between devices, per_device(): lax.all_gather(w_gate, 'shard', axis=1, tiled=True)  92.2 us
    all_gather x1, waiting for transfers between devices, per_device(): lax.all_gather(w_down, 'shard', axis=0, tiled=True)  87.9 us
    all_gather x1, waiting for transfers between devices, per_device(): lax.all_gather(w_up, 'shard', axis=1, tiled=True)  87.8 us
    reduce_scatter x1, waiting for transfers between devices, per_device(): lax.psum_scatter(grad_wout.astype(jnp.bfloat16), 'shard', scatter_dimensi...  48.5 us
    unnamed x107, local copies, waits for them, and re-layouts  46.4 us
  transfers between devices with their start and end apart: 16, of which 14 were waited for; matrix products, arithmetic and copies ran while one was open for 16% of the time, Pallas kernels for 0%

commit v1 on v0

--- a/solution.py
+++ b/solution.py
@@ -3,6 +3,7 @@
 import jax
 import jax.numpy as jnp
 from jax import lax
+from jax.sharding import Mesh
 from jax.sharding import PartitionSpec as P
 
 HQ = 20
@@ -110,7 +111,7 @@
     w_down,
 ):
     micro_count, stretch_len, model_width = tokens.shape
-    ctx_count = lax.axis_size("ctx")
+    ctx_count = lax.axis_size("line") * lax.axis_size("core")
     full_len = stretch_len * ctx_count
     row_count = micro_count * stretch_len
     query_width = HQ * HD
@@ -118,25 +119,31 @@
     group_size = HQ // HK
     factor = 1.0 / math.sqrt(HD)
     block_rows = stretch_len * math.gcd(ctx_count, max(1, 512 // stretch_len))
-    rank_ctx = lax.axis_index("ctx")
+    rank_ctx = lax.axis_index("line") * lax.axis_size("core") + lax.axis_index("core")
     query_places = lax.dynamic_slice_in_dim(positions, rank_ctx * stretch_len, stretch_len, 1)
     valid_rows = (query_places < lengths[:, None]).astype(jnp.float32).reshape(row_count, 1)
     cosine, sine_part = rope_parts(query_places.reshape(row_count))
-    gain_one, gain_two, query_all, key_all, value_all, out_all = (
+    gain_one, gain_two = (
         lax.all_gather(attn_gain, "shard", axis=0, tiled=True),
         lax.all_gather(mlp_gain, "shard", axis=0, tiled=True),
-        lax.all_gather(w_query, "shard", axis=0, tiled=True),
-        lax.all_gather(w_key, "shard", axis=0, tiled=True),
-        lax.all_gather(w_value, "shard", axis=0, tiled=True),
-        lax.all_gather(w_out, "shard", axis=0, tiled=True),
-    )
+    )
+    qkv_local = jnp.concatenate([w_query, w_key, w_value], axis=1)
+    qkv_all = lax.all_gather(qkv_local, "shard", axis=0, tiled=True)
+    query_all = qkv_all[:, :query_width]
+    key_all = qkv_all[:, query_width : query_width + kv_width]
+    value_all = qkv_all[:, query_width + kv_width :]
+    out_all = lax.all_gather(w_out, "shard", axis=0, tiled=True)
+    grad_out = cotangent.reshape(row_count, model_width).astype(jnp.float32) * valid_rows
+    grad_low = grad_out.astype(jnp.bfloat16)
+    grad_low_all = lax.all_gather(grad_low, "shard", axis=0, tiled=True)
     hidden = tokens.reshape(row_count, model_width).astype(jnp.float32)
     normed_one, inv_one = row_norm(hidden, gain_one.astype(jnp.float32))
     norm_one = normed_one.astype(jnp.bfloat16)
-    queries = product(norm_one, query_all)
-    key_proj = product(norm_one, key_all)
+    qkv = product(norm_one, qkv_all)
+    queries = qkv[:, :query_width]
+    key_proj = qkv[:, query_width : query_width + kv_width]
     value_low = (
-        product(norm_one, value_all)
+        qkv[:, query_width + kv_width :]
         .astype(jnp.bfloat16)
         .reshape(micro_count, stretch_len, kv_width)
     )
@@ -175,8 +182,8 @@
         jnp.zeros((micro_count, HK, group_size, stretch_len), jnp.float32),
         jnp.zeros((micro_count, stretch_len, HK, group_size, HD), jnp.float32),
     )
-    key_piece = lax.all_gather(key_rot, "ctx", axis=1, tiled=True)
-    value_piece = lax.all_gather(value_low, "ctx", axis=1, tiled=True)
+    key_piece = lax.all_gather(key_rot, ("line", "core"), axis=1, tiled=True)
+    value_piece = lax.all_gather(value_low, ("line", "core"), axis=1, tiled=True)
 
     def step_fn(inner_state, offset, sub_rows):
         key_sub = lax.dynamic_slice_in_dim(key_piece, offset, sub_rows, 1)
@@ -191,38 +198,32 @@
     gain_two_f = gain_two.astype(jnp.float32)
     normed_two, inv_two = row_norm(middle, gain_two_f)
     norm_two = normed_two.astype(jnp.bfloat16)
-    gate_all, up_all, down_all = (
-        lax.all_gather(w_gate, "shard", axis=1, tiled=True),
-        lax.all_gather(w_up, "shard", axis=1, tiled=True),
-        lax.all_gather(w_down, "shard", axis=0, tiled=True),
-    )
-    gate_proj = product(norm_two, gate_all)
-    up_proj = product(norm_two, up_all)
+    norm_two_all = lax.all_gather(norm_two, "shard", axis=0, tiled=True)
+    gate_proj = product(norm_two_all, w_gate)
+    up_proj = product(norm_two_all, w_up)
     inner_act = (jax.nn.silu(gate_proj) * up_proj).astype(jnp.bfloat16)
-    mlp_out = product(inner_act, down_all)
+    grad_inner = product_nt(grad_low_all, w_down)
+    grad_gate, grad_up = gate_back(grad_inner, gate_proj, up_proj)
+    grad_norm_two = lax.psum_scatter(
+        (product_nt(grad_gate, w_gate) + product_nt(grad_up, w_up)).astype(jnp.bfloat16),
+        "shard",
+        scatter_dimension=0,
+        tiled=True,
+    ).astype(jnp.float32)
+    mlp_out = lax.psum_scatter(
+        product(inner_act, w_down).astype(jnp.bfloat16), "shard", scatter_dimension=0, tiled=True
+    ).astype(jnp.float32)
     result = (middle + mlp_out).astype(jnp.bfloat16).reshape(micro_count, stretch_len, model_width)
-    gain_one, gain_two, query_all, key_all, value_all, out_all = (
-        lax.all_gather(attn_gain, "shard", axis=0, tiled=True),
-        lax.all_gather(mlp_gain, "shard", axis=0, tiled=True),
-        lax.all_gather(w_query, "shard", axis=0, tiled=True),
-        lax.all_gather(w_key, "shard", axis=0, tiled=True),
-        lax.all_gather(w_value, "shard", axis=0, tiled=True),
-        lax.all_gather(w_out, "shard", axis=0, tiled=True),
-    )
-    gain_two_f = gain_two.astype(jnp.float32)
-    grad_out = cotangent.reshape(row_count, model_width).astype(jnp.float32) * valid_rows
-    grad_low = grad_out.astype(jnp.bfloat16)
-    gate_all, up_all, down_all = (
-        lax.all_gather(w_gate, "shard", axis=1, tiled=True),
-        lax.all_gather(w_up, "shard", axis=1, tiled=True),
-        lax.all_gather(w_down, "shard", axis=0, tiled=True),
-    )
-    grad_wdown = product_tn(inner_act, grad_low)
-    grad_inner = product_nt(grad_low, down_all)
-    grad_gate, grad_up = gate_back(grad_inner, gate_proj, up_proj)
-    grad_wgate = product_tn(norm_two, grad_gate)
-    grad_wup = product_tn(norm_two, grad_up)
-    grad_norm_two = product_nt(grad_gate, gate_all) + product_nt(grad_up, up_all)
+    grad_wdown = product_tn(inner_act, grad_low_all).astype(jnp.bfloat16)
+    grad_wgate = product_tn(norm_two_all, grad_gate).astype(jnp.bfloat16)
+    grad_wup = product_tn(norm_two_all, grad_up).astype(jnp.bfloat16)
+
+    def over_ctx(part):
+        share = lax.psum_scatter(part, "core", scatter_dimension=0, tiled=True)
+        share = lax.psum(share, "line")
+        return lax.all_gather(share, "core", axis=0, tiled=True)
+
+    total_wdown, total_wgate, total_wup = over_ctx(grad_wdown), over_ctx(grad_wgate), over_ctx(grad_wup)
     grad_mid_norm, grad_gain_two = norm_back(grad_norm_two, middle, inv_two, gain_two_f)
     grad_middle = grad_out + grad_mid_norm
     grad_proj = grad_middle.astype(jnp.bfloat16)
@@ -233,10 +234,7 @@
         .reshape(micro_count, stretch_len, HK, group_size, HD)
     )
     row_delta = jnp.transpose(jnp.sum(grad_attn.astype(jnp.float32) * attended, -1), (0, 2, 3, 1))
-    key_full, value_full = (
-        lax.all_gather(key_rot, "ctx", axis=1, tiled=True),
-        lax.all_gather(value_low, "ctx", axis=1, tiled=True),
-    )
+    key_full, value_full = key_piece, value_piece
 
     def grad_block(key_piece, value_piece, first_row):
         span_rows = key_piece.shape[1]
@@ -272,7 +270,7 @@
         )
         * factor
     )
-    span_rows = stretch_len * lax.axis_size("ctx")
+    span_rows = stretch_len * ctx_count
     sub_rows = math.gcd(span_rows, block_rows)
 
     def one_piece(block_index):
@@ -303,7 +301,7 @@
     stacked = lax.map(one_piece, jnp.arange(span_rows // sub_rows))
     grad_kv = lax.psum_scatter(
         stacked.reshape(span_rows, micro_count, 2 * kv_width).astype(jnp.bfloat16),
-        "ctx",
+        ("line", "core"),
         scatter_dimension=0,
         tiled=True,
     ).astype(jnp.float32)
@@ -319,14 +317,9 @@
         .astype(jnp.bfloat16)
     )
     grad_values = grad_kv[:, kv_width:].astype(jnp.bfloat16)
-    grad_wquery = product_tn(norm_one, grad_queries)
-    grad_wkey = product_tn(norm_one, grad_keys)
-    grad_wvalue = product_tn(norm_one, grad_values)
-    grad_norm_one = (
-        product_nt(grad_queries, query_all)
-        + product_nt(grad_keys, key_all)
-        + product_nt(grad_values, value_all)
-    )
+    grad_qkv = jnp.concatenate([grad_queries, grad_keys, grad_values], axis=1)
+    grad_wqkv = product_tn(norm_one, grad_qkv).astype(jnp.bfloat16)
+    grad_norm_one = product_nt(grad_qkv, qkv_all)
     grad_hidden, grad_gain_one = norm_back(
         grad_norm_one, hidden, inv_one, gain_one.astype(jnp.float32)
     )
@@ -335,78 +328,43 @@
         .astype(jnp.bfloat16)
         .reshape(micro_count, stretch_len, model_width)
     )
-    (
-        share_gain_one,
-        share_wquery,
-        share_wkey,
-        share_wvalue,
-        share_wout,
-        share_gain_two,
-        share_wgate,
-        share_wup,
-        share_wdown,
-    ) = (
-        lax.psum_scatter(
-            grad_gain_one.astype(jnp.bfloat16), "shard", scatter_dimension=0, tiled=True
-        ).astype(jnp.float32),
-        lax.psum_scatter(
-            grad_wquery.astype(jnp.bfloat16), "shard", scatter_dimension=0, tiled=True
-        ).astype(jnp.float32),
-        lax.psum_scatter(
-            grad_wkey.astype(jnp.bfloat16), "shard", scatter_dimension=0, tiled=True
-        ).astype(jnp.float32),
-        lax.psum_scatter(
-            grad_wvalue.astype(jnp.bfloat16), "shard", scatter_dimension=0, tiled=True
-        ).astype(jnp.float32),
-        lax.psum_scatter(
-            grad_wout.astype(jnp.bfloat16), "shard", scatter_dimension=0, tiled=True
-        ).astype(jnp.float32),
-        lax.psum_scatter(
-            grad_gain_two.astype(jnp.bfloat16), "shard", scatter_dimension=0, tiled=True
-        ).astype(jnp.float32),
-        lax.psum_scatter(
-            grad_wgate.astype(jnp.bfloat16), "shard", scatter_dimension=1, tiled=True
-        ).astype(jnp.float32),
-        lax.psum_scatter(
-            grad_wup.astype(jnp.bfloat16), "shard", scatter_dimension=1, tiled=True
-        ).astype(jnp.float32),
-        lax.psum_scatter(
-            grad_wdown.astype(jnp.bfloat16), "shard", scatter_dimension=0, tiled=True
-        ).astype(jnp.float32),
-    )
-    totals = (
-        lax.psum(share_gain_one.astype(jnp.bfloat16), "ctx").astype(jnp.float32),
-        lax.psum(share_wquery.astype(jnp.bfloat16), "ctx").astype(jnp.float32),
-        lax.psum(share_wkey.astype(jnp.bfloat16), "ctx").astype(jnp.float32),
-        lax.psum(share_wvalue.astype(jnp.bfloat16), "ctx").astype(jnp.float32),
-        lax.psum(share_wout.astype(jnp.bfloat16), "ctx").astype(jnp.float32),
-        lax.psum(share_gain_two.astype(jnp.bfloat16), "ctx").astype(jnp.float32),
-        lax.psum(share_wgate.astype(jnp.bfloat16), "ctx").astype(jnp.float32),
-        lax.psum(share_wup.astype(jnp.bfloat16), "ctx").astype(jnp.float32),
-        lax.psum(share_wdown.astype(jnp.bfloat16), "ctx").astype(jnp.float32),
-    )
+
+    def over_all(part):
+        share = lax.psum_scatter(part, "shard", scatter_dimension=0, tiled=True)
+        return over_ctx(share)
+
+    total_wout = over_all(grad_wout.astype(jnp.bfloat16))
+    total_wqkv = over_all(grad_wqkv)
+    gains = jnp.stack([grad_gain_one, grad_gain_two], axis=1).astype(jnp.bfloat16)
+    gains = lax.psum(gains, ("shard", "line", "core")).astype(jnp.float32)
+    span = attn_gain.shape[0]
+    gains = lax.dynamic_slice_in_dim(gains, lax.axis_index("shard") * span, span, 0)
+    f32 = jnp.float32
     return (
         result,
         grad_input,
-        totals[0],
-        totals[1],
-        totals[2],
-        totals[3],
-        totals[4],
-        totals[5],
-        totals[6],
-        totals[7],
-        totals[8],
+        gains[:, 0],
+        total_wqkv[:, :query_width].astype(f32),
+        total_wqkv[:, query_width : query_width + kv_width].astype(f32),
+        total_wqkv[:, query_width + kv_width :].astype(f32),
+        total_wout.astype(f32),
+        gains[:, 1],
+        total_wgate.astype(f32),
+        total_wup.astype(f32),
+        total_wdown.astype(f32),
     )
 
 
 def solution(mesh):
+    shards, ctx = mesh.devices.shape
+    inner = Mesh(mesh.devices.reshape(shards, ctx // 2, 2), ("shard", "line", "core"))
+    where = ("line", "core")
     return jax.shard_map(
         per_device,
-        mesh=mesh,
+        mesh=inner,
         in_specs=(
-            P("shard", "ctx", None),
-            P("shard", "ctx", None),
+            P("shard", where, None),
+            P("shard", where, None),
             P("shard", None),
             P("shard"),
             P("shard"),
@@ -420,8 +378,8 @@
             P("shard", None),
         ),
         out_specs=(
-            P("shard", "ctx", None),
-            P("shard", "ctx", None),
+            P("shard", where, None),
+            P("shard", where, None),
             P("shard"),
             P("shard", None),
             P("shard", None),

time: 1240 us -> 894 us (0.72)
  waiting for transfers between devices: 839 us -> 551 us
  blocking collectives: 75 us -> 53.2 us
  local copies, waits for them, and re-layouts: 76 us -> 58.4 us
  matrix products: 170 us -> 154 us
    all_gather x7 -> x10, waiting for transfers between devices: 314 us -> 173 us  [the longest x1 45.8 us: per_device(): qkv_all = lax.all_gather(qkv_local, 'shard', axis=0, tiled=True)]
    unnamed x18 -> x21, waiting for transfers between devices: 124 us -> 2.66 us
    reduce_scatter x5 -> x9, waiting for transfers between devices: 250 us -> 208 us  [the longest x2 69.2 us: over_all(): share = lax.psum_scatter(part, 'shard', scatter_dimension=0, tiled=True)]
    all_gather x2 -> x1, blocking collectives: 38.9 us -> 2.38 us  [over_ctx(): return lax.all_gather(share, 'core', axis=0, tiled=True)]
    unnamed x107 -> x89, local copies, waits for them, and re-layouts: 46.4 us -> 12.6 us
    psum x1, blocking collectives: 15.4 us -> 39.3 us  [per_device(): gains = lax.psum(gains, ('shard', 'line', 'core')).astype(jnp.float32)]
    psum x1, waiting for transfers between devices: 151 us -> 168 us  [over_ctx(): share = lax.psum(share, 'line')]
    dot_general x7 -> x5, matrix products: 32.4 us -> 25.9 us  [product_tn(): jnp.einsum('ra,rb->ab', left_side, right_side, preferred_element_type=jnp...]
  transfers between devices with their start and end apart: 16 -> 21, of which waited for: 14 -> 16; matrix products, arithmetic and copies ran while one was open for 16% -> 17% of each run, Pallas kernels for 0% -> 0%
where the time goes in v1:
time: 894 us; the launch traced here: 889 us
  waiting for transfers between devices  551 us (62%)
  matrix products  154 us (17%)
  local copies, waits for them, and re-layouts  58.4 us (7%)
  blocking collectives  53.2 us (6%)
  other arithmetic  50 us (6%)
  between operations  16.1 us (2%)
    psum x1, waiting for transfers between devices, over_ctx(): share = lax.psum(share, 'line')  168 us
    reduce_scatter x2, waiting for transfers between devices, over_all(): share = lax.psum_scatter(part, 'shard', scatter_dimension=0, tiled=True)  69.2 us
    reduce_scatter x5, waiting for transfers between devices, over_ctx(): share = lax.psum_scatter(part, 'core', scatter_dimension=0, tiled=True)  63.8 us
    all_gather x1, waiting for transfers between devices, per_device(): qkv_all = lax.all_gather(qkv_local, 'shard', axis=0, tiled=True)  45.8 us
    reduce_scatter x1, waiting for transfers between devices, per_device(): lax.psum_scatter(product(inner_act, w_down).astype(jnp.bfloat16), 'shard'...  41 us
    psum x1, blocking collectives, per_device(): gains = lax.psum(gains, ('shard', 'line', 'core')).astype(jnp.float32)  39.3 us
    all_gather x1, waiting for transfers between devices, per_device(): norm_two_all = lax.all_gather(norm_two, 'shard', axis=0, tiled=True)  37 us
    reduce_scatter x1, waiting for transfers between devices, per_device(): lax.psum_scatter((product_nt(grad_gate, w_gate) + product_nt(grad_up, w_u...  33.5 us
  transfers between devices with their start and end apart: 21, of which 16 were waited for; matrix products, arithmetic and copies ran while one was open for 17% of the time, Pallas kernels for 0%

profile of v1, /device:TPU:0, one launch (start us, length us, event | category | flops | bytes accessed | tf_op | source)
XLA Modules:
  0.0 889.0 jit_solution(6632849939000674957)
XLA Ops:
  7.3 3.5 concatenate.30
  12.7 11.5 %all-reduce.3 = (bf16[1280]{0:T(1024)(128)(2,1)S(1)}, bf16[1280]{0:T(1024)(128)(2,1)S(1)}) all-reduce(bf16[1280]{0:T(1024)(128)(2,1)S(1)} %dynamic-update-slice, bf16[1280]{0:T(1024)(128)(2,1)S(1)} %dynamic-update-slice.1), channel_id=1, replica_groups=mesh['shard'=4,'line'=4,'core'=2] {'shard'}, use_global_device_ids=true, to_apply=%add | all-reduce | flops 2560 | bytes 10240
  26.5 45.8 %all-gather.11.cloned.1.call-done = bf16[1280,1920]{1,0:T(8,128)(2,1)} async-done(((bf16[320,1920]{1,0:T(8,128)(2,1)}), bf16[1280,1920]{1,0:T(8,128)(2,1)}) %all-gather.11.cloned.1.call-update) | async-done | bytes 4915216 | tf_op jit(solution)/shard_map/all_gather | solution.py:131
  72.3 4.1 fusion.90
  81.6 2.5 slice.78
  84.1 2.8 copy.58
  89.6 16.0 %all-gather.13.cloned.1.call-done = bf16[2,1024,320]{1,0,2:T(2,128)(2,1)} async-done(((bf16[2,128,320]{1,0,2:T(2,128)(2,1)}), bf16[2,1024,320]{1,0,2:T(2,128)(2,1)}) %all-gather.13.cloned.1.call-update) | async-done | bytes 1310736 | tf_op jit(solution)/shard_map/all_gather | solution.py:185
  105.5 2.7 copy.60
  108.3 25.1 %all-gather.15.cloned.1.call-done = bf16[2,1024,320]{1,2,0:T(8,128)(2,1)} async-done(((bf16[2,128,320]{1,2,0:T(8,128)(2,1)}), bf16[2,1024,320]{1,2,0:T(8,128)(2,1)}) %all-gather.15.cloned.1.call-update) | async-done | bytes 1310736 | tf_op jit(solution)/shard_map/all_gather | solution.py:186
  133.4 22.7 %while.37 = (s32[]{:T(128)}, f32[2,5,4,128]{3,2,1,0:T(4,128)S(1)}, f32[2,5,4,128]{3,2,1,0:T(4,128)S(1)}, f32[2,128,5,4,64]{1,4,3,2,0:T(8,128)}, s32[2]{0:T(128)S...) while((s32[]{:T(128)}, f32[2,5,4,128]{3,2,1,0:T(4,128)S(1)}, ...), condition=%wide.region_4.5_spmd.clone, body=%wide.region_1.4_spmd.clone.sunk | while | flops 706444288 | bytes 50019616 | solution.py:94
  138.1 2.7 fusion.177
  140.8 2.9 fusion.179
  149.5 2.7 fusion.177
  152.2 2.8 fusion.179
  156.1 4.1 fusion.86
  160.3 18.9 %all-gather.17.cloned.1.call-done = bf16[1280,1280]{1,0:T(8,128)(2,1)} async-done(((bf16[320,1280]{1,0:T(8,128)(2,1)}), bf16[1280,1280]{1,0:T(8,128)(2,1)}) %all-gather.17.cloned.1.call-update) | async-done | bytes 3276816 | tf_op jit(solution)/shard_map/all_gather | solution.py:135
  179.1 3.4 multiply_reduce_fusion.1
  187.3 37.0 %all-gather.19.cloned.1.call-done = bf16[1024,1280]{1,0:T(8,128)(2,1)} async-done(((bf16[256,1280]{1,0:T(8,128)(2,1)}), bf16[1024,1280]{1,0:T(8,128)(2,1)}) %all-gather.19.cloned.1.call-update) | async-done | bytes 2621456 | tf_op jit(solution)/shard_map/all_gather | solution.py:201
  224.3 7.3 fusion.92
  231.6 4.7 fusion.91
  236.3 29.8 %all-gather.21.cloned.1.call-done = bf16[1024,1280]{1,0:T(8,128)(2,1)} async-done(((bf16[256,1280]{1,0:T(8,128)(2,1)}), bf16[1024,1280]{1,0:T(8,128)(2,1)}) %all-gather.21.cloned.1.call-update) | async-done | bytes 2621456 | tf_op jit(solution)/shard_map/all_gather | solution.py:138
  266.1 9.4 %multiply_convert_fusion = (bf16[1024,896]{1,0:T(8,128)(2,1)S(1)}, bf16[1024,896]{1,0:T(8,128)(2,1)S(1)}, bf16[1024,896]{1,0:T(8,128)(2,1)}) fusion(f32[1024,896]{1,0:T(8,128)} %fusion.91, f32[1024,896]{1,0:T(8,128)} %fusion.92, bf16[1024,1280]{1,0:T(8,128)(2,1)} %all-gather.21.cloned.1.call-done, bf16[896,1280]{1,0:T(8,128)(2,1)S(1)} %copy-done), kind=kOutput, calls=%fused_computation.70 | convolution fusion | flops 2363490304 | bytes 17760256 | tf_op jit(solution)/shard_map/ra,ba->rb/dot_general | solution.py:64
  275.6 2.9 fusion.93
  278.6 4.2 add_convert_fusion
  282.8 5.9 convolution_convert_fusion.2
  289.0 33.5 %reduce-scatter.13.cloned.1.call-done = bf16[256,1280]{1,0:T(8,128)(2,1)} async-done(((bf16[1024,1280]{1,0:T(8,128)(2,1)}), bf16[256,1280]{1,0:T(8,128)(2,1)}) %reduce-scatter.13.cloned.1.call-update) | async-done | bytes 655376 | tf_op jit(solution)/shard_map/reduce_scatter | solution.py:207
  324.6 41.0 %reduce-scatter.11.cloned.1.call-done = bf16[256,1280]{1,0:T(8,128)(2,1)} async-done(((bf16[1024,1280]{1,0:T(8,128)(2,1)}), bf16[256,1280]{1,0:T(8,128)(2,1)}) %reduce-scatter.11.cloned.1.call-update) | async-done | bytes 655376 | tf_op jit(solution)/shard_map/reduce_scatter | solution.py:213
  365.7 3.1 fusion.60
  376.0 55.9 %while.36 = (s32[]{:T(128)}, bf16[2,512,2,640]{3,1,0,2:T(8,128)(2,1)}, s32[2]{0:T(128)S(1)}, s32[2,1024]{1,0:T(2,128)S(1)}, s32[2,128]{1,0:T(2,128)S(1)}, /*inde...) while((s32[]{:T(128)}, ...), condition=%wide.region_13.14_spmd, body=%wide.region_12.13_spmd.sunk | while | flops 1371931648 | bytes 58142024 | solution.py:301
  379.7 5.6 fusion.168
  385.3 8.5 fusion.170
  393.8 6.0 fusion.169
  401.3 2.6 constant_dynamic-update-slice_fusion.2
  407.6 5.6 fusion.168
  413.2 8.5 fusion.170
  421.7 6.0 fusion.169
  429.2 2.6 constant_dynamic-update-slice_fusion.2
  432.9 4.0 convolution_convert_fusion
  437.1 38.6 %while.38 = (s32[]{:T(128)}, f32[2,128,5,4,64]{1,4,3,2,0:T(8,128)}, s32[2]{0:T(128)S(1)}, bf16[2,1024,320]{1,2,0:T(8,128)(2,1)S(1)}, s32[2,1024]{1,0:T(2,128)S(1...) while((s32[]{:T(128)}, f32[2,128,5,4,64]{1,4,3,2,0:T(8,128)}, ...), condition=%wide.region_11.12_spmd.clone, body=%wide.region_10.11_spmd.clone.sunk | while | flops 1023280128 | bytes 29809904 | solution.py:94
  440.9 5.6 fusion.186
  446.5 9.7 %fusion.187 = f32[2,128,5,4,64]{1,4,3,2,0:T(8,128)} fusion(bf16[2,512,5,64,1]{1,3,4,2,0:T(8,128)(2,1)S(1)} %bitcast.313, f32[2,5,512,128,4]{3,2,4,1,0:T(8,128)} %fusion.186, f32[2,5,4,128]{3,2,1,0:T(4,128)S(1)} %get-tuple-element.876, f32[2,5,4,128]{3,2,1,0:T(4,128)S(1)} %get-tuple-element.873, pred[2,128,512]{1,2,0:T(8,128)(4,1)S(1)} %compare_and_fusion.8, ...), kind=kOutput, calls=%fused_computation.58.clone.1 | convolution fusion | flops 687472640 | bytes 15245313 | tf_op jit(solution)/shard_map/while/body/eval_jaxpr/mhgqk,mkhd->mqhgd/dot_general | solution.py:257
  460.0 5.6 fusion.186
  465.6 10.0 %fusion.187 = f32[2,128,5,4,64]{1,4,3,2,0:T(8,128)} fusion(bf16[2,512,5,64,1]{1,3,4,2,0:T(8,128)(2,1)S(1)} %bitcast.313, f32[2,5,512,128,4]{3,2,4,1,0:T(8,128)} %fusion.186, f32[2,5,4,128]{3,2,1,0:T(4,128)S(1)} %get-tuple-element.876, f32[2,5,4,128]{3,2,1,0:T(4,128)S(1)} %get-tuple-element.873, pred[2,128,512]{1,2,0:T(8,128)(4,1)S(1)} %compare_and_fusion.8, ...), kind=kOutput, calls=%fused_computation.58.clone.1 | convolution fusion | flops 687472640 | bytes 15245313 | tf_op jit(solution)/shard_map/while/body/eval_jaxpr/mhgqk,mkhd->mqhgd/dot_general | solution.py:257
  479.2 2.3 reshape.271
  483.4 3.8 convolution_convert_fusion.1
  488.7 5.9 convolution_convert_fusion.3
  496.1 6.0 convolution_convert_fusion.5
  503.7 6.1 convolution_convert_fusion.4
  509.9 7.6 reduce-scatter.21.cloned.1.call-done
  517.6 61.6 %reduce-scatter.17.cloned.1.call-done = bf16[320,1920]{1,0:T(8,128)(2,1)} async-done(((bf16[1280,1920]{1,0:T(8,128)(2,1)}), bf16[320,1920]{1,0:T(8,128)(2,1)}) %reduce-scatter.17.cloned.1.call-update) | async-done | bytes 1228816 | tf_op jit(solution)/shard_map/reduce_scatter | solution.py:333
  579.3 12.1 %reduce-scatter.29.cloned.1.call-done = bf16[448,1280]{1,0:T(8,128)(2,1)} async-done(((bf16[896,1280]{1,0:T(8,128)(2,1)}), bf16[448,1280]{1,0:T(8,128)(2,1)}) %reduce-scatter.29.cloned.1.call-update) | async-done | bytes 1146896 | tf_op jit(solution)/shard_map/reduce_scatter | solution.py:222
  591.4 14.2 %reduce-scatter.25.cloned.1.call-done = bf16[640,896]{1,0:T(8,128)(2,1)} async-done(((bf16[1280,896]{1,0:T(8,128)(2,1)}), bf16[640,896]{1,0:T(8,128)(2,1)}) %reduce-scatter.25.cloned.1.call-update) | async-done | bytes 1146896 | tf_op jit(solution)/shard_map/reduce_scatter | solution.py:222
  605.5 14.0 %reduce-scatter.27.cloned.1.call-done = bf16[640,896]{1,0:T(8,128)(2,1)} async-done(((bf16[1280,896]{1,0:T(8,128)(2,1)}), bf16[640,896]{1,0:T(8,128)(2,1)}) %reduce-scatter.27.cloned.1.call-update) | async-done | bytes 1146896 | tf_op jit(solution)/shard_map/reduce_scatter | solution.py:222
  619.6 11.6 %reduce-scatter.23.cloned.1.call-done = bf16[160,1280]{1,0:T(8,128)(2,1)} async-done(((bf16[320,1280]{1,0:T(8,128)(2,1)}), bf16[160,1280]{1,0:T(8,128)(2,1)}) %reduce-scatter.23.cloned.1.call-update) | async-done | bytes 409616 | tf_op jit(solution)/shard_map/reduce_scatter | solution.py:222
  631.2 11.9 %reduce-scatter.19.cloned.1.call-done = bf16[160,1920]{1,0:T(8,128)(2,1)} async-done(((bf16[320,1920]{1,0:T(8,128)(2,1)}), bf16[160,1920]{1,0:T(8,128)(2,1)}) %reduce-scatter.19.cloned.1.call-update) | async-done | bytes 614416 | tf_op jit(solution)/shard_map/reduce_scatter | solution.py:222
  643.2 167.9 %all-reduce.6.cloned.1.call-done = (bf16[160,1920]{1,0:T(8,128)(2,1)}, bf16[160,1280]{1,0:T(8,128)(2,1)}, bf16[640,896]{1,0:T(8,128)(2,1)}, bf16[640,896]{1,0:T(8,128)(2,1)}, bf16[448,1280]{1,0:T(8,128)(2,1)}) async-done(((bf16[160,1920]{1,0:T(8,128)(2,1)}, bf16[160,1280]{1,0:T(8,128)(2,1)}, bf16[640,896]{1,0:T(8,128)(2,1)}, bf16[640,896]{1,0:T(8,128)(2,1)}, bf16[448,1280]{1,0:T(8,128)(2,1)}), ...) | async-done | bytes 4464656 | tf_op jit(solution)/shard_map/psum | solution.py:223
  813.2 5.3 fusion.74
  818.5 39.3 %psum.42 = bf16[1280,2]{0,1:T(2,128)(2,1)S(1)} all-reduce(bf16[1280,2]{0,1:T(2,128)(2,1)S(1)} %pad_maximum_fusion.7), channel_id=1, replica_groups=mesh['shard'=4,'line'=4,'core'=2] {'shard','line','core'}, use_global_device_ids=true, to_apply=%region_18.19 | all-reduce | flops 2560 | bytes 10240 | tf_op jit(solution)/shard_map/psum | solution.py:339
  858.5 2.6 fusion.71
  861.1 2.4 all_gather.48
  866.8 2.4 slice_convert_fusion
  869.2 4.1 convert_element_type.203
  873.4 4.2 convert_element_type.201
  877.6 4.1 convert_element_type.199
  (247 shorter events, 68.3 us)
Async XLA Ops:
  7.2 259.0 %copy-start = (bf16[896,1280]{1,0:T(8,128)(2,1)S(1)}, bf16[896,1280]{1,0:T(8,128)(2,1)}, u32[]{:S(2)}) copy-start(bf16[896,1280]{1,0:T(8,128)(2,1)} %param.31) | copy-start | bytes 6881284
  7.2 3.7 copy-start.38
  7.2 5.0 copy-start.31
  7.2 5.2 copy-start.32
  7.2 17.0 %copy-start.9 = (bf16[2,128,1280]{2,1,0:T(8,128)(2,1)S(1)}, bf16[2,128,1280]{2,1,0:T(8,128)(2,1)}, u32[]{:S(2)}) copy-start(bf16[2,128,1280]{2,1,0:T(8,128)(2,1)} %param.19) | copy-start | bytes 1966084
  7.2 17.2 %copy-start.23 = (s32[2]{0:T(128)S(1)}, s32[2]{0:T(128)}, u32[]{:S(2)}) copy-start(s32[2]{0:T(128)} %param.22) | copy-start | bytes 28
  7.3 17.2 %copy-start.20 = (s32[2,1024]{1,0:T(2,128)S(1)}, s32[2,1024]{1,0:T(2,128)}, u32[]{:S(2)}) copy-start(s32[2,1024]{1,0:T(2,128)} %param.21) | copy-start | bytes 24580
  7.3 65.0 %all-gather.11.cloned.1.call-start = ((), (), s32[]{:S(2)}) async-start(), calls=%async_computation.10 | async-start | bytes 6144000 | tf_op jit(solution)/shard_map/all_gather | solution.py:131
  10.9 94.7 %all-gather.13.cloned.1.call-start = ((), (), s32[]{:S(2)}) async-start(), calls=%async_computation.11 | async-start | bytes 1474560 | tf_op jit(solution)/shard_map/all_gather | solution.py:185
  24.2 52.2 %copy-start.24 = (f32[1280]{0:T(1024)}, f32[1280]{0:T(1024)S(1)}, u32[]{:S(2)}) copy-start(f32[1280]{0:T(1024)S(1)} %convert_element_type.163) | copy-start | bytes 15364
  24.5 52.0 %copy-start.27 = (f32[2,128]{1,0:T(2,128)}, f32[2,128]{1,0:T(2,128)S(1)}, u32[]{:S(2)}) copy-start(f32[2,128]{1,0:T(2,128)S(1)} %fusion.65) | copy-start | bytes 3076
  24.6 51.9 %copy-start.29 = (f32[256]{0:T(256)}, f32[256]{0:T(256)S(1)}, u32[]{:S(2)}) copy-start(f32[256]{0:T(256)S(1)} %rsqrt_bitcast_fusion) | copy-start | bytes 3076
  25.4 61.5 %copy-start.17 = (f32[256,32]{0,1:T(8,128)}, f32[256,32]{0,1:T(8,128)S(1)}, u32[]{:S(2)}) copy-start(f32[256,32]{0,1:T(8,128)S(1)} %get-tuple-element.489) | copy-start | bytes 98308
  78.7 54.7 %all-gather.15.cloned.1.call-start = ((), (), s32[]{:S(2)}) async-start(), calls=%async_computation.12 | async-start | bytes 1474560 | tf_op jit(solution)/shard_map/all_gather | solution.py:186
  80.7 98.4 %all-gather.17.cloned.1.call-start = ((), (), s32[]{:S(2)}) async-start(), calls=%async_computation.13 | async-start | bytes 4096000 | tf_op jit(solution)/shard_map/all_gather | solution.py:135
  81.3 143.0 %all-gather.19.cloned.1.call-start = ((), (), s32[]{:S(2)}) async-start(), calls=%async_computation.14 | async-start | bytes 3276800 | tf_op jit(solution)/shard_map/all_gather | solution.py:201
  138.1 2.8 copy-start.15
  149.4 2.8 copy-start.15
  184.7 81.5 %all-gather.21.cloned.1.call-start = ((), (), s32[]{:S(2)}) async-start(), calls=%async_computation.16 | async-start | bytes 3276800 | tf_op jit(solution)/shard_map/all_gather | solution.py:138
  186.8 135.7 %reduce-scatter.13.cloned.1.call-start = ((), (), s32[]{:S(2)}) async-start(), calls=%async_computation.17 | async-start | bytes 3276800 | tf_op jit(solution)/shard_map/reduce_scatter | solution.py:207
  224.3 7.3 copy-start.34
  224.3 7.3 copy-start.35
  266.1 9.5 %copy-start.36 = (bf16[1280,896]{1,0:T(8,128)(2,1)S(1)}, bf16[1280,896]{1,0:T(8,128)(2,1)}, u32[]{:S(2)}) copy-start(bf16[1280,896]{1,0:T(8,128)(2,1)} %param.29) | copy-start | bytes 6881284
  275.6 2.9 copy-start.39
  275.6 2.9 copy-start.42
  275.6 3.0 copy-start.37
  282.8 82.9 %reduce-scatter.11.cloned.1.call-start = ((), (), s32[]{:S(2)}) async-start(), calls=%async_computation.15 | async-start | bytes 3276800 | tf_op jit(solution)/shard_map/reduce_scatter | solution.py:213
  288.7 33.8 %copy-start.8 = (f32[256,1280]{1,0:T(8,128)S(1)}, f32[256,1280]{1,0:T(8,128)}, u32[]{:S(2)}) copy-start(f32[256,1280]{1,0:T(8,128)} %copy-done.7) | copy-start | bytes 3932164
  288.7 193.1 %reduce-scatter.15.cloned.1.call-start = ((), (), s32[]{:S(2)}) async-start(), calls=%async_computation.18 | async-start | bytes 2949120 | tf_op jit(solution)/shard_map/reduce_scatter | solution.py:302
  322.5 43.2 %copy-start.12 = (bf16[256,1280]{1,0:T(8,128)(2,1)S(1)}, bf16[256,1280]{1,0:T(8,128)(2,1)}, u32[]{:S(2)}) copy-start(bf16[256,1280]{1,0:T(8,128)(2,1)} %reduce-scatter.13.cloned.1.call-done) | copy-start | bytes 1966084
  365.7 3.1 copy-start.33
  370.9 5.0 copy-start.2
  379.7 5.6 copy-start.4
  379.7 5.6 copy-start.19
  401.3 2.6 copy-start.3
  407.6 5.6 copy-start.4
  407.6 5.6 copy-start.19
  429.2 2.6 copy-start.3
  431.9 85.6 %reduce-scatter.21.cloned.1.call-start = ((), (), s32[]{:S(2)}) async-start(), calls=%async_computation.22 | async-start | bytes 4096000 | tf_op jit(solution)/shard_map/reduce_scatter | solution.py:333
  437.0 142.2 %reduce-scatter.17.cloned.1.call-start = ((), (), s32[]{:S(2)}) async-start(), calls=%async_computation.19 | async-start | bytes 6144000 | tf_op jit(solution)/shard_map/reduce_scatter | solution.py:333
  477.1 4.5 copy-start.18
  477.1 4.5 copy-start.22
  481.8 1.7 copy-start.11
  487.2 1.5 copy-start.41
  487.3 104.1 %reduce-scatter.29.cloned.1.call-start = ((), (), s32[]{:S(2)}) async-start(), calls=%async_computation.28 | async-start | bytes 3440640 | tf_op jit(solution)/shard_map/reduce_scatter | solution.py:222
  494.6 1.5 copy-start.40
  494.7 110.9 %reduce-scatter.25.cloned.1.call-start = ((), (), s32[]{:S(2)}) async-start(), calls=%async_computation.24 | async-start | bytes 3440640 | tf_op jit(solution)/shard_map/reduce_scatter | solution.py:222
  502.2 1.5 copy-start.43
  502.2 117.3 %reduce-scatter.27.cloned.1.call-start = ((), (), s32[]{:S(2)}) async-start(), calls=%async_computation.26 | async-start | bytes 3440640 | tf_op jit(solution)/shard_map/reduce_scatter | solution.py:222
  509.8 121.4 %reduce-scatter.23.cloned.1.call-start = ((), (), s32[]{:S(2)}) async-start(), calls=%async_computation.23 | async-start | bytes 1228800 | tf_op jit(solution)/shard_map/reduce_scatter | solution.py:222
  517.5 125.5 %reduce-scatter.19.cloned.1.call-start = ((), (), s32[]{:S(2)}) async-start(), calls=%async_computation.20 | async-start | bytes 1843200 | tf_op jit(solution)/shard_map/reduce_scatter | solution.py:222
  579.2 231.8 %all-reduce.6.cloned.1.call-start = ((), (), s32[]{:S(2)}) async-start(), calls=%async_computation.30 | async-start | bytes 8929280 | tf_op jit(solution)/shard_map/psum | solution.py:223
  643.1 169.4 %copy-start.28 = (f32[2,128]{1,0:T(2,128)S(1)}, f32[2,128]{1,0:T(2,128)}, u32[]{:S(2)}) copy-start(f32[2,128]{1,0:T(2,128)} %copy-done.27) | copy-start | bytes 3076
  643.1 169.4 %copy-start.26 = (bf16[1280]{0:T(1024)(128)(2,1)S(1)}, bf16[1280]{0:T(1024)(128)(2,1)}, u32[]{:S(2)}) copy-start(bf16[1280]{0:T(1024)(128)(2,1)} %get-tuple-element.369) | copy-start | bytes 7684
  643.1 170.0 %copy-start.10 = (bf16[2,128,1280]{2,1,0:T(8,128)(2,1)S(1)}, bf16[2,128,1280]{2,1,0:T(8,128)(2,1)}, u32[]{:S(2)}) copy-start(bf16[2,128,1280]{2,1,0:T(8,128)(2,1)} %param.19) | copy-start | bytes 1966084
  643.1 170.0 %copy-start.25 = (f32[1280]{0:T(1024)S(1)}, f32[1280]{0:T(1024)}, u32[]{:S(2)}) copy-start(f32[1280]{0:T(1024)} %copy-done.24) | copy-start | bytes 15364
  643.1 170.0 %copy-start.30 = (f32[256]{0:T(256)S(1)}, f32[256]{0:T(256)}, u32[]{:S(2)}) copy-start(f32[256]{0:T(256)} %copy-done.29) | copy-start | bytes 3076
  643.1 221.6 %all-gather.23.cloned.1.call-start = ((), (), s32[]{:S(2)}) async-start(), calls=%async_computation.21 | async-start | bytes 1843200 | tf_op jit(solution)/shard_map/all_gather | solution.py:224
  811.1 58.2 %all-gather.29.cloned.1.call-start = ((), (), s32[]{:S(2)}) async-start(), calls=%async_computation.29 | async-start | bytes 3440640 | tf_op jit(solution)/shard_map/all_gather | solution.py:224
  811.8 61.6 %all-gather.27.cloned.1.call-start = ((), (), s32[]{:S(2)}) async-start(), calls=%async_computation.27 | async-start | bytes 3440640 | tf_op jit(solution)/shard_map/all_gather | solution.py:224
  812.4 65.2 %all-gather.25.cloned.1.call-start = ((), (), s32[]{:S(2)}) async-start(), calls=%async_computation.25 | async-start | bytes 3440640 | tf_op jit(solution)/shard_map/all_gather | solution.py:224
  813.2 45.3 %copy-start.6 = (f32[256,1280]{1,0:T(8,128)S(1)}, f32[256,1280]{1,0:T(8,128)}, u32[]{:S(2)}) copy-start(f32[256,1280]{1,0:T(8,128)} %copy-done.5) | copy-start | bytes 3932164
  818.4 42.6 %copy-start.21 = (bf16[160,1280]{1,0:T(8,128)(2,1)S(1)}, bf16[160,1280]{1,0:T(8,128)(2,1)}, u32[]{:S(2)}) copy-start(bf16[160,1280]{1,0:T(8,128)(2,1)} %get-tuple-element.444) | copy-start | bytes 1228804
  873.4 8.3 copy-start.1
  (6 other events, 6.6 us)
Sparse Core Ops, SparseCore 0:
  11.0 61.2 all-gather.10
  78.8 26.6 all-gather.12
  107.7 25.6 all-gather.14
  135.1 43.9 all-gather.16
  184.8 39.4 all-gather.18
  226.6 39.5 all-gather.20
  282.9 39.5 reduce-scatter.12
  326.1 39.5 reduce-scatter.10
  432.0 37.8 reduce-scatter.14
  473.3 44.1 reduce-scatter.20
  520.6 58.5 reduce-scatter.16
  581.3 10.0 reduce-scatter.28
  594.2 11.2 reduce-scatter.24
  608.2 11.3 reduce-scatter.26
  621.7 9.4 reduce-scatter.22
  633.3 9.7 reduce-scatter.18
  645.6 165.3 all-reduce.5
  812.4 8.2 all-gather.22
  822.3 12.0 all-gather.28
  835.7 12.0 all-gather.26
  849.3 12.0 all-gather.24

commit v2 on v1

v2 whole, which is shorter than its diff:
```python
import math

import jax
import jax.numpy as jnp
from jax import lax
from jax.experimental import pallas as pl
from jax.experimental.pallas import tpu as pltpu
from jax.sharding import Mesh
from jax.sharding import PartitionSpec as P

HQ = 20
HK = 5
HD = 64
GROUP = HQ // HK
EPSILON = 1e-05
NEGATIVE = -1e30
ROPE_BASE = 10000.0
BF = jnp.bfloat16
F32 = jnp.float32
BY_MESH = pl.DeviceIdType.MESH
VMEM_LIMIT = 67043328


def nn(a, b):
    return lax.dot_general(a, b, (((1,), (0,)), ((), ())), preferred_element_type=F32)


def nt(a, b):
    return lax.dot_general(a, b, (((1,), (1,)), ((), ())), preferred_element_type=F32)


def tn(a, b):
    return lax.dot_general(a, b, (((0,), (0,)), ((), ())), preferred_element_type=F32)


def lanes_of(rows):
    return lax.broadcasted_iota(jnp.int32, (rows, 128), 1)


def swap_halves(block, lane):
    left = pltpu.roll(block, 96, 1)
    right = pltpu.roll(block, 32, 1)
    return jnp.where(lane % 64 < 32, left, right)


def add_rows(target, parts, rows, step):
    def body(index, carry):
        span = pl.ds(pl.multiple_of(index * step, step), step)
        total = parts[0][span, :].astype(F32)
        for part in parts[1:]:
            total = total + part[span, :].astype(F32)
        target[span, :] = total.astype(target.dtype)
        return carry

    lax.fori_loop(0, rows // step, body, 0)


def backward_kernel(
    sizes,
    gm_ref,
    attn_ref,
    attn_t_ref,
    qp_ref,
    n1_t_ref,
    x_ref,
    gain_ref,
    cos_ref,
    sin_ref,
    gg_ref,
    wo_hbm,
    wq_hbm,
    wkv_hbm,
    pt_hbm,
    kv_hbm,
    dw_hbm,
    out_dw,
    out_wo,
    out_wq,
    out_wkv,
    out_gain,
    out_dx,
    w_buf,
    wkv_buf,
    pt_buf,
    kv_buf,
    dproj,
    dop,
    delta,
    dkv,
    dkv_x,
    dkv_z,
    dq,
    dkv_own,
    own,
    got_x,
    got_r,
    got_t,
    g_buf,
    g_kv,
    o_x,
    o_z,
    o_r,
    o_t,
    q_x,
    q_z,
    q_r,
    q_t,
    k_x,
    k_z,
    k_r,
    k_t,
    gn_own,
    gn_x,
    gn_z,
    gn_r,
    gn_t,
    load_sem,
    pt_sem,
    kv_sem,
    core_sem,
    up_send,
    r_recv,
    t_recv,
    down_send,
    sib_send,
    sib_recv,
    local_sem,
    dkv_core,
    dkv_send,
    dkv_recv,
    g_core,
    g_send,
    g_recv,
    a_up,
    a_r,
    a_t,
    a_down,
    a_sib_send,
    a_sib_recv,
    a_local,
):
    shards, line, keys, rows, width, feed = sizes
    s_id, l_id, c_id = lax.axis_index("shard"), lax.axis_index("line"), lax.axis_index("core")
    sibling = (s_id, l_id, 1 - c_id)
    in_low = l_id < line // 2
    toward = jnp.where(in_low, 1, -1)
    inner = (s_id, l_id + toward, c_id)
    has_outer = (l_id > 0) & (l_id < line - 1)
    is_mid = (l_id == line // 2 - 1) | (l_id == line // 2)
    outer = (s_id, jnp.where(has_outer, l_id - toward, l_id + toward), c_id)
    peers = [(lax.rem(s_id + k, shards), l_id, c_id) for k in range(1, shards)]
    mates = [(s_id, lax.rem(l_id + k, line), c_id) for k in range(1, line)]

    def remote(src, dst, send, recv, to):
        return pltpu.make_async_remote_copy(
            src, dst, send, recv, device_id=to, device_id_type=BY_MESH
        )

    barrier = pltpu.get_barrier_semaphore()
    for other in [sibling] + peers + mates:
        pl.semaphore_signal(barrier, inc=1, device_id=other, device_id_type=BY_MESH)
    pl.semaphore_wait(barrier, 1 + len(peers) + len(mates))

    half = width // 2
    chunk = half // 4
    chunks = 12
    slab = 16
    part = width // shards
    own_rows = part // 2
    blocks = keys // 1024
    hlf = pl.ds(pl.multiple_of(c_id * half, 16), half)
    oth = pl.ds(pl.multiple_of((1 - c_id) * half, 16), half)

    core_copy = [
        remote(dw_hbm.at[k, oth], got_x.at[k], core_sem.at[k], core_sem.at[3 + k], sibling)
        for k in range(3)
    ]
    own_load = [
        pltpu.make_async_copy(dw_hbm.at[k, hlf], own.at[k], load_sem.at[k]) for k in range(3)
    ]
    load_wo = pltpu.make_async_copy(wo_hbm, w_buf, load_sem.at[3])
    load_wkv = pltpu.make_async_copy(wkv_hbm, wkv_buf, load_sem.at[4])
    load_wq = pltpu.make_async_copy(wq_hbm, w_buf, load_sem.at[5])
    load_wo.start()
    for k in range(3):
        own_load[k].start()
        core_copy[k].start()
    load_wkv.start()

    total_steps = 2 * HK * blocks

    def pt_copy(step, slot):
        pair, block = step // blocks, step % blocks
        span = pl.ds(pl.multiple_of(block * 1024, 1024), 1024)
        return pltpu.make_async_copy(pt_hbm.at[pair, span], pt_buf.at[slot], pt_sem.at[slot])

    def kv_copy(step, slot):
        pair, block = step // blocks, step % blocks
        span = pl.ds(pl.multiple_of(block * 1024, 1024), 1024)
        return pltpu.make_async_copy(kv_hbm.at[pair, span], kv_buf.at[slot], kv_sem.at[slot])

    pt_copy(0, 0).start()
    kv_copy(0, 0).start()

    def spot(index):
        array, piece = index // 4, index % 4
        return array, pl.ds(pl.multiple_of(piece * chunk, 16), chunk)

    def up(index):
        array, span = spot(index)
        mine, extra, came = own.at[array, span], got_x.at[array, span], got_r.at[array, span]

        @pl.when(index % 4 == 0)
        def _():
            pltpu.make_async_copy(
                dw_hbm.at[array, hlf], own.at[array], load_sem.at[array]
            ).wait()
            remote(
                dw_hbm.at[array, oth],
                got_x.at[array],
                core_sem.at[array],
                core_sem.at[3 + array],
                sibling,
            ).wait()

        @pl.when(has_outer)
        def _():
            remote(mine, came, up_send.at[index], r_recv.at[index], inner).wait_recv()
            add_rows(mine, [mine, extra, came], chunk, slab)

        @pl.when(jnp.logical_not(has_outer))
        def _():
            add_rows(mine, [mine, extra], chunk, slab)

        @pl.when(is_mid)
        def _():
            remote(
                mine, got_t.at[array, span], up_send.at[index], t_recv.at[index], inner
            ).start()

        @pl.when(jnp.logical_not(is_mid))
        def _():
            remote(mine, came, up_send.at[index], r_recv.at[index], inner).start()

    def out_span(index, core):
        array, piece = index // 4, index % 4
        return out_dw.at[array, pl.ds(pl.multiple_of(core * half + piece * chunk, 16), chunk)]

    def down(index):
        array, span = spot(index)
        mine, total = own.at[array, span], got_t.at[array, span]
        remote(mine, total, up_send.at[index], t_recv.at[index], inner).wait_recv()

        @pl.when(is_mid)
        def _():
            add_rows(total, [mine, total], chunk, slab)

        @pl.when(has_outer)
        def _():
            remote(total, total, down_send.at[index], t_recv.at[index], outer).start()

        remote(
            total, out_span(index, c_id), sib_send.at[index], sib_recv.at[index], sibling
        ).start()
        pltpu.make_async_copy(total, out_span(index, c_id), local_sem.at[index]).start()

    def settle(index):
        array, span = spot(index)
        mine, total = own.at[array, span], got_t.at[array, span]
        remote(mine, total, up_send.at[index], t_recv.at[index], inner).wait_send()

        @pl.when(has_outer)
        def _():
            remote(total, total, down_send.at[index], t_recv.at[index], outer).wait_send()

        last = remote(
            total, out_span(index, 1 - c_id), sib_send.at[index], sib_recv.at[index], sibling
        )
        last.wait()
        pltpu.make_async_copy(total, out_span(index, c_id), local_sem.at[index]).wait()

    def ring(step):
        @pl.when((step >= 0) & (step < chunks))
        def _():
            up(step)

        @pl.when((step >= 3) & (step < chunks + 3) & is_mid)
        def _():
            down(step - 3)

        @pl.when((step >= 6) & (step < chunks + 6) & jnp.logical_not(is_mid))
        def _():
            down(step - 6)

    def core_part(grad, cols, box, slot):
        far = pl.ds(pl.multiple_of((1 - c_id) * own_rows, 16), own_rows)
        return remote(
            grad.at[:, far, :], box, g_core.at[slot], g_core.at[3 + slot], sibling
        )

    def scatter_part(grad, box, zone, slot):
        core_part(grad, None, box, slot).wait()
        near = pl.ds(pl.multiple_of(c_id * own_rows, 16), own_rows)

        def body(s, carry):
            add_rows(box.at[s], [grad.at[s, near], box.at[s]], own_rows, slab)
            return carry

        lax.fori_loop(0, shards, body, 0)
        for k in range(1, shards):
            scatter_copy(box, zone, slot, k).start()

    def scatter_copy(box, zone, slot, k):
        return remote(
            box.at[lax.rem(s_id + k, shards)],
            zone.at[k - 1],
            g_send.at[slot, k - 1],
            g_recv.at[slot, k - 1],
            peers[k - 1],
        )

    def gather_part(box, zone, slot):
        for k in range(1, shards):
            scatter_copy(box, zone, slot, k).wait()
        add_rows(
            box.at[s_id],
            [box.at[s_id]] + [zone.at[k] for k in range(shards - 1)],
            own_rows,
            slab,
        )

    def line_up(mine, came, total, slot, count):
        @pl.when(has_outer)
        def _():
            remote(mine, came, a_up.at[slot], a_r.at[slot], inner).wait_recv()
            add_rows(mine, [mine, came], count, slab if mine.dtype == BF else 8)

        @pl.when(is_mid)
        def _():
            remote(mine, total, a_up.at[slot], a_t.at[slot], inner).start()

        @pl.when(jnp.logical_not(is_mid))
        def _():
            remote(mine, came, a_up.at[slot], a_r.at[slot], inner).start()

    def line_down(mine, total, slot, count, near, far):
        remote(mine, total, a_up.at[slot], a_t.at[slot], inner).wait()

        @pl.when(is_mid)
        def _():
            add_rows(total, [mine, total], count, slab if mine.dtype == BF else 8)

        @pl.when(has_outer)
        def _():
            remote(total, total, a_down.at[slot], a_t.at[slot], outer).start()

        if far is not None:
            remote(total, near, a_sib_send.at[slot], a_sib_recv.at[slot], sibling).start()
        pltpu.make_async_copy(total, near, a_local.at[slot]).start()

    def line_settle(total, slot, near, far):
        @pl.when(has_outer)
        def _():
            remote(total, total, a_down.at[slot], a_t.at[slot], outer).wait_send()

        if far is not None:
            remote(total, far, a_sib_send.at[slot], a_sib_recv.at[slot], sibling).wait()
        pltpu.make_async_copy(total, near, a_local.at[slot]).wait()

    lane = lanes_of(128)
    dproj[...] = gm_ref[...].astype(BF)
    load_wo.wait()

    def spread(head, carry):
        block = nt(
            dproj[...], w_buf[pl.ds(pl.multiple_of(head * 256, 256), 256), :]
        ).astype(BF)
        for seq in range(2):
            for two in range(2):
                piece = block[seq * 128 : seq * 128 + 128, two * 128 : two * 128 + 128].astype(
                    F32
                )
                place = seq * HK + head
                first = jnp.where(lane >= 64, pltpu.roll(piece, 64, 1), 0.0)
                dop[place, pl.ds(two * 256, 128), :] = first.astype(BF)
                dop[place, pl.ds(two * 256 + 128, 128), :] = jnp.where(
                    lane >= 64, piece, 0.0
                ).astype(BF)
                value = attn_ref[
                    pl.ds(seq * 128, 128),
                    pl.ds(pl.multiple_of(head * 256 + two * 128, 128), 128),
                ].astype(F32)
                product = jnp.transpose(piece * value)
                delta[place, :, pl.ds(two * 256, 128)] = jnp.sum(
                    product[:64], 0, keepdims=True
                )
                delta[place, :, pl.ds(two * 256 + 128, 128)] = jnp.sum(
                    product[64:], 0, keepdims=True
                )
        return carry

    lax.fori_loop(0, HK, spread, 0)
    load_wq.start()
    ring(0)

    def weight_grad(left, right, grad, count):
        def body(s, carry):
            grad[s] = nn(
                left[pl.ds(pl.multiple_of(s * part, 16), part), :], right[...]
            ).astype(BF)
            return carry

        lax.fori_loop(0, count, body, 0)

    weight_grad(attn_t_ref, dproj, g_buf, shards)
    core_part(g_buf, None, o_x, 0).start()
    ring(1)

    cosine, sine = cos_ref, sin_ref

    def attend(step, carry):
        slot = lax.rem(step, 2)
        pair, block = step // blocks, step % blocks

        @pl.when(step + 1 < total_steps)
        def _():
            pt_copy(step + 1, 1 - slot).start()
            kv_copy(step + 1, 1 - slot).start()

        pt_copy(step, slot).wait()
        kv_copy(step, slot).wait()
        keyval = kv_buf[slot]
        soft = pt_buf[slot]
        grad_soft = nt(keyval, dop[pair])
        score = (soft.astype(F32) * (grad_soft - delta[pair])).astype(BF)
        both = (nn(score, qp_ref[pair]) + nn(soft, dop[pair])).astype(BF)
        for sub in range(8):
            dkv[pair, block * 4 + sub // 2, sub % 2] = both[sub * 128 : sub * 128 + 128]
        query = tn(keyval, score)[:64] * (1.0 / math.sqrt(HD))
        seq, head = pair // HK, pair % HK
        for two in range(2):
            piece = jnp.transpose(
                jnp.concatenate(
                    [
                        query[:, two * 256 : two * 256 + 128],
                        query[:, two * 256 + 128 : two * 256 + 256],
                    ],
                    0,
                )
            )
            where = (
                pl.ds(pl.multiple_of(seq * 128, 128), 128),
                pl.ds(pl.multiple_of(head * 256 + two * 128, 128), 128),
            )
            if blocks == 1:
                cos = cosine[where[0], :]
                sin = sine[where[0], :]
                dq[where] = (piece * cos - swap_halves(piece, lane) * sin).astype(BF)
            else:
                dq[where] = jnp.where(block == 0, piece, dq[where].astype(F32) + piece).astype(
                    dq.dtype
                )

        @pl.when(lax.rem(step, 2 * blocks) == 2 * blocks - 1)
        def _():
            ring(2 + step // (2 * blocks))

        return carry

    def dkv_core_copy(seq):
        return remote(
            dkv.at[pl.ds(seq * HK, HK), :, 1 - c_id],
            dkv_x.at[pl.ds(seq * HK, HK)],
            dkv_core.at[seq],
            dkv_core.at[2 + seq],
            sibling,
        )

    def dkv_copy(seq, k):
        return remote(
            dkv_x.at[pl.ds(seq * HK, HK), lax.rem(l_id + k, line)],
            dkv_z.at[seq, k - 1],
            dkv_send.at[seq, k - 1],
            dkv_recv.at[seq, k - 1],
            mates[k - 1],
        )

    def dkv_scatter(seq):
        dkv_core_copy(seq).wait()

        def body(index, carry):
            head, place = seq * HK + index // line, index % line
            dkv_x[head, place] = (
                dkv_x[head, place].astype(F32) + dkv[head, place, c_id].astype(F32)
            ).astype(BF)
            return carry

        lax.fori_loop(0, HK * line, body, 0)
        for k in range(1, line):
            dkv_copy(seq, k).start()

    def dkv_gather(seq):
        for k in range(1, line):
            dkv_copy(seq, k).wait()
        cos = jnp.where(lane < 64, cosine[pl.ds(seq * 128, 128), :], 1.0)
        sin = jnp.where(lane < 64, sine[pl.ds(seq * 128, 128), :], 0.0)
        for head in range(HK):
            total = dkv_x[seq * HK + head, l_id].astype(F32)
            for k in range(line - 1):
                total = total + dkv_z[seq, k, head].astype(F32)
            dkv_own[pl.ds(seq * 128, 128), pl.ds(head * 128, 128)] = (
                total * cos - swap_halves(total, lane) * sin
            ).astype(BF)

    lax.fori_loop(0, HK * blocks, attend, 0)
    dkv_core_copy(0).start()
    scatter_part(g_buf, o_x, o_z, 0)
    lax.fori_loop(HK * blocks, total_steps, attend, 0)
    dkv_core_copy(1).start()
    dkv_scatter(0)
    if blocks > 1:
        for two in range(width // 128):
            for seq in range(2):
                where = (pl.ds(seq * 128, 128), pl.ds(two * 128, 128))
                piece = dq[where].astype(F32)
                cos = cosine[where[0], :]
                sin = sine[where[0], :]
                dq[where] = (piece * cos - swap_halves(piece, lane) * sin).astype(dq.dtype)
    dkv_scatter(1)
    weight_grad(n1_t_ref, dq, g_buf, shards)
    core_part(g_buf, None, q_x, 1).start()
    ring(7)
    scatter_part(g_buf, q_x, q_z, 1)
    gather_part(o_x, o_z, 0)
    line_up(o_x.at[s_id], o_r, o_t, 0, own_rows)
    load_wq.wait()
    load_wkv.wait()
    back = nt(dq[...], w_buf[...])
    dkv_gather(0)
    dkv_gather(1)
    weight_grad(n1_t_ref, dkv_own, g_kv, shards)
    core_part(g_kv, None, k_x, 2).start()
    ring(8)
    back = back + nt(dkv_own[...], wkv_buf[...])
    scatter_part(g_kv, k_x, k_z, 2)
    hidden = x_ref[...].astype(F32)
    scale = lax.rsqrt(jnp.mean(hidden * hidden, -1, keepdims=True) + EPSILON)
    scaled = back * gain_ref[...]
    gn_own[0:1, :] = jnp.sum(back * hidden * scale, 0, keepdims=True)
    gn_own[1:2, :] = gg_ref[...]
    gn_own[2:8, :] = jnp.zeros((6, width), F32)
    gain_core = remote(gn_own, gn_x, g_core.at[6], g_core.at[7], sibling)
    gain_core.start()
    out_dx[...] = (
        gm_ref[...]
        + scale * scaled
        - hidden * (scale * scale * scale) * jnp.mean(scaled * hidden, -1, keepdims=True)
    ).astype(BF)
    ring(9)
    gather_part(q_x, q_z, 1)
    line_up(q_x.at[s_id], q_r, q_t, 1, own_rows)
    gain_core.wait()
    gn_own[...] = gn_own[...] + gn_x[...]

    def gain_copy(k):
        return remote(
            gn_own, gn_z.at[k - 1], g_send.at[3, k - 1], g_recv.at[3, k - 1], peers[k - 1]
        )

    for k in range(1, shards):
        gain_copy(k).start()
    ring(10)
    gather_part(k_x, k_z, 2)
    line_up(k_x.at[s_id], k_r, k_t, 2, own_rows)
    for k in range(1, shards):
        gain_copy(k).wait()
    total = gn_own[...]
    for k in range(shards - 1):
        total = total + gn_z[k]
    gn_x[...] = total
    line_up(gn_x, gn_r, gn_t, 3, 8)
    ring(11)

    def tail(step, carry):
        ring(step)
        return carry

    lax.fori_loop(12, chunks + 3, tail, 0)
    near = pl.ds(pl.multiple_of(c_id * own_rows, 16), own_rows)
    far = pl.ds(pl.multiple_of((1 - c_id) * own_rows, 16), own_rows)
    jobs = [
        (o_x.at[s_id], o_t, 0, own_rows, out_wo.at[near], out_wo.at[far]),
        (q_x.at[s_id], q_t, 1, own_rows, out_wq.at[near], out_wq.at[far]),
        (k_x.at[s_id], k_t, 2, own_rows, out_wkv.at[near], out_wkv.at[far]),
        (gn_x, gn_t, 3, 8, out_gain, None),
    ]
    for mine, tot, slot, count, to, other in jobs:
        line_down(mine, tot, slot, count, to, other)
    lax.fori_loop(chunks + 3, chunks + 6, tail, 0)
    for mine, tot, slot, count, to, other in jobs:
        line_settle(tot, slot, to, other)

    def last(index, carry):
        settle(index)
        return carry

    lax.fori_loop(0, chunks, last, 0)


def backward_call(
    shards, line, gm, attn, attn_t, qp, n1_t, x, gain, cos, sin, gg, wo, wq, wkv, pt, kv, dw
):
    rows, width = gm.shape
    keys = kv.shape[1]
    feed = dw.shape[2]
    part = width // shards
    own_rows = part // 2
    kv_width = 2 * HK * HD
    sizes = (shards, line, keys, rows, width, feed)
    dma = pltpu.SemaphoreType.DMA
    v = pltpu.VMEM
    vm = pl.BlockSpec(memory_space=pltpu.VMEM)
    hbm = pl.BlockSpec(memory_space=pltpu.HBM)
    blocks = keys // 1024
    half = width // 2

    def boxes(cols):
        return [
            v((shards, own_rows, cols), BF),
            v((shards - 1, own_rows, cols), BF),
            v((own_rows, cols), BF),
            v((own_rows, cols), BF),
        ]

    scratch = [
        v((width, width), BF),
        v((width, kv_width), BF),
        v((2, 1024, 512), BF),
        v((2, 1024, 128), BF),
        v((rows, width), BF),
        v((2 * HK, 512, 128), BF),
        v((2 * HK, 1, 512), F32),
        v((2 * HK, line, 2, 128, 128), BF),
        v((2 * HK, line, 128, 128), BF),
        v((2, line - 1, HK, 128, 128), BF),
        v((rows, width), BF if blocks == 1 else F32),
        v((rows, kv_width), BF),
        v((3, half, feed), BF),
        v((3, half, feed), BF),
        v((3, half, feed), BF),
        v((3, half, feed), BF),
        v((shards, part, width), BF),
        v((shards, part, kv_width), BF),
        *boxes(width),
        *boxes(width),
        *boxes(kv_width),
        v((8, width), F32),
        v((8, width), F32),
        v((shards - 1, 8, width), F32),
        v((8, width), F32),
        v((8, width), F32),
        dma((6,)),
        dma((2,)),
        dma((2,)),
        dma((6,)),
        *[dma((12,)) for _ in range(7)],
        dma((4,)),
        dma((2, line - 1)),
        dma((2, line - 1)),
        dma((8,)),
        dma((4, shards - 1)),
        dma((4, shards - 1)),
        *[dma((4,)) for _ in range(7)],
    ]
    return pl.pallas_call(
        lambda *refs: backward_kernel(sizes, *refs),
        out_shape=(
            jax.ShapeDtypeStruct((3, width, feed), BF),
            jax.ShapeDtypeStruct((part, width), BF),
            jax.ShapeDtypeStruct((part, width), BF),
            jax.ShapeDtypeStruct((part, kv_width), BF),
            jax.ShapeDtypeStruct((8, width), F32),
            jax.ShapeDtypeStruct((rows, width), BF),
        ),
        in_specs=[vm] * 10 + [hbm] * 6,
        out_specs=(hbm, hbm, hbm, hbm, hbm, vm),
        scratch_shapes=scratch,
        compiler_params=pltpu.CompilerParams(
            collective_id=3, has_side_effects=True, vmem_limit_bytes=VMEM_LIMIT
        ),
        name="backward",
    )(gm, attn, attn_t, qp, n1_t, x, gain, cos, sin, gg, wo, wq, wkv, pt, kv, dw)


def attend_kernel(qp_ref, kv_ref, bias_ref, pt_ref, out_ref):
    blocks = kv_ref.shape[1] // 1024

    def scores(block):
        span = pl.ds(pl.multiple_of(block * 1024, 1024), 1024)
        bias = bias_ref[0, span, :]
        return nt(kv_ref[0, span, :], qp_ref[0]) + jnp.concatenate([bias] * GROUP, 1)

    if blocks == 1:
        value = scores(0)
        top = jnp.max(value, 0, keepdims=True)
        weight = jnp.exp(value - top)
        soft = (weight * (1.0 / jnp.sum(weight, 0, keepdims=True))).astype(BF)
        pt_ref[0] = soft
        mixed = tn(kv_ref[0], soft)[HD:]
    else:

        def first(block, carry):
            top, total = carry
            value = scores(block)
            new = jnp.maximum(top, jnp.max(value, 0, keepdims=True))
            total = total * jnp.exp(top - new) + jnp.sum(jnp.exp(value - new), 0, keepdims=True)
            return new, total

        top, total = lax.fori_loop(
            0,
            blocks,
            first,
            (jnp.full((1, 512), NEGATIVE, F32), jnp.zeros((1, 512), F32)),
        )
        inverse = 1.0 / total

        def second(block, mixed):
            soft = (jnp.exp(scores(block) - top) * inverse).astype(BF)
            span = pl.ds(pl.multiple_of(block * 1024, 1024), 1024)
            pt_ref[0, span, :] = soft
            return mixed + tn(kv_ref[0, span, :], soft)[HD:]

        mixed = lax.fori_loop(0, blocks, second, jnp.zeros((HD, 512), F32))
    for two in range(2):
        pair = jnp.concatenate(
            [mixed[:, two * 256 : two * 256 + 128], mixed[:, two * 256 + 128 : two * 256 + 256]], 0
        )
        out_ref[:, two * 128 : two * 128 + 128] = jnp.transpose(pair).astype(BF)


def attend_call(qp, kv, bias):
    keys = kv.shape[1]
    rows = 256
    return pl.pallas_call(
        attend_kernel,
        grid=(2, HK),
        out_shape=(
            jax.ShapeDtypeStruct((2 * HK, keys, 512), BF),
            jax.ShapeDtypeStruct((rows, HQ * HD), BF),
        ),
        in_specs=[
            pl.BlockSpec((1, 512, 128), lambda m, h: (m * HK + h, 0, 0)),
            pl.BlockSpec((1, keys, 128), lambda m, h: (m * HK + h, 0, 0)),
            pl.BlockSpec((1, keys, 128), lambda m, h: (m, 0, 0)),
        ],
        out_specs=(
            pl.BlockSpec((1, keys, 512), lambda m, h: (m * HK + h, 0, 0)),
            pl.BlockSpec((128, 256), lambda m, h: (m, h)),
        ),
        compiler_params=pltpu.CompilerParams(vmem_limit_bytes=VMEM_LIMIT),
        name="attend",
    )(qp, kv, bias)


def rope_parts(places):
    half_dim = HD // 2
    frequency = ROPE_BASE ** (-jnp.arange(half_dim, dtype=F32) * 2.0 / HD)
    angles = places.astype(F32)[..., None] * frequency
    return (jnp.cos(angles), jnp.sin(angles))


def rotate_wide(values, cosine, sine, keys_only):
    rows, cols = values.shape
    tiles = values.reshape(rows, cols // 128, 128)
    lane = jnp.arange(128)
    left = jnp.roll(tiles, -32, 2)
    right = jnp.roll(tiles, 32, 2)
    swapped = jnp.where(lane % 64 < 32, left, right)
    if keys_only:
        cosine = jnp.where(lane < 64, cosine, 1.0)
        sine = jnp.where(lane < 64, sine, 0.0)
    return (tiles * cosine[:, None, :] + swapped * sine[:, None, :]).reshape(rows, cols)


def row_norm(hidden, gain_vec):
    inv_scale = lax.rsqrt(jnp.mean(hidden * hidden, -1, keepdims=True) + EPSILON)
    return (hidden * inv_scale * gain_vec, inv_scale)


def norm_back(grad_norm, hidden, inv_scale, gain_vec):
    scaled = grad_norm * gain_vec
    grad_gain = jnp.sum(grad_norm * hidden * inv_scale, 0)
    grad_hidden = inv_scale * scaled - hidden * inv_scale**3 * jnp.mean(
        scaled * hidden, -1, keepdims=True
    )
    return (grad_hidden, grad_gain)


def gate_back(grad_inner, gate_proj, up_proj):
    sigmoid_gate = jax.nn.sigmoid(gate_proj)
    grad_gate = (
        grad_inner * up_proj * sigmoid_gate * (1.0 + gate_proj * (1.0 - sigmoid_gate))
    ).astype(BF)
    grad_up = (grad_inner * gate_proj * sigmoid_gate).astype(BF)
    return (grad_gate, grad_up)


def per_device(
    tokens,
    cotangent,
    positions,
    lengths,
    attn_gain,
    w_query,
    w_key,
    w_value,
    w_out,
    mlp_gain,
    w_gate,
    w_up,
    w_down,
):
    seqs, stretch, width = tokens.shape
    shards, line = lax.axis_size("shard"), lax.axis_size("line")
    rows = seqs * stretch
    where_ctx = ("line", "core")
    rank = lax.axis_index("line") * 2 + lax.axis_index("core")
    places = lax.dynamic_slice_in_dim(positions, rank * stretch, stretch, 1)
    valid = (places < lengths[:, None]).astype(F32).reshape(rows, 1)
    cosine, sine = rope_parts(places.reshape(rows))
    cos_wide = jnp.concatenate([cosine] * 4, 1)
    sin_wide = jnp.concatenate([-sine, sine, -sine, sine], 1)
    allowed = (positions[:, :, None] <= places[:, None, :]) & (
        positions < lengths[:, None]
    )[:, :, None]
    bias = jnp.where(allowed, 0.0, NEGATIVE).astype(F32)
    gains = lax.all_gather(jnp.stack([attn_gain, mlp_gain]), "shard", axis=1, tiled=True)
    gain_one, gain_two = gains[0].astype(F32), gains[1].astype(F32)
    w_kv = jnp.stack(
        [w_key.reshape(-1, HK, HD), w_value.reshape(-1, HK, HD)], 2
    ).reshape(-1, 2 * HK * HD)
    qkv_local = jnp.concatenate([w_query, w_kv], axis=1)
    qkv_all = lax.all_gather(qkv_local, "shard", axis=0, tiled=True)
    out_all = lax.all_gather(w_out, "shard", axis=0, tiled=True)
    grad_out = cotangent.reshape(rows, width).astype(F32) * valid
    grad_low = grad_out.astype(BF)
    grad_low_all = lax.all_gather(grad_low, "shard", axis=0, tiled=True)
    hidden = tokens.reshape(rows, width).astype(F32)
    normed_one, inv_one = row_norm(hidden, gain_one)
    norm_one = normed_one.astype(BF)
    wq_all, wkv_all = qkv_all[:, :width], qkv_all[:, width:]
    queries = rotate_wide(nn(norm_one, wq_all), cos_wide, sin_wide, False).astype(BF)
    keyval = rotate_wide(nn(norm_one, wkv_all), cos_wide, sin_wide, True).astype(BF)
    packed_q = jnp.transpose(
        queries.reshape(seqs, stretch, HK, GROUP, HD), (0, 2, 3, 1, 4)
    ).reshape(seqs * HK, GROUP * stretch, HD) * BF(1.0 / math.sqrt(HD))
    packed_q = jnp.pad(packed_q, ((0, 0), (0, 0), (0, 128 - HD)))
    packed_kv = jnp.transpose(keyval.reshape(seqs, stretch, HK, 128), (0, 2, 1, 3))
    packed_kv = lax.all_gather(packed_kv, where_ctx, axis=2, tiled=True)
    packed_kv = packed_kv.reshape(seqs * HK, -1, 128)
    soft, attn = attend_call(packed_q, packed_kv, bias)
    middle = hidden + nn(attn, out_all)
    normed_two, inv_two = row_norm(middle, gain_two)
    norm_two = normed_two.astype(BF)
    norm_two_all = lax.all_gather(norm_two, "shard", axis=0, tiled=True)
    gate_proj = nn(norm_two_all, w_gate)
    up_proj = nn(norm_two_all, w_up)
    inner_act = (jax.nn.silu(gate_proj) * up_proj).astype(BF)
    grad_inner = nt(grad_low_all, w_down)
    grad_gate, grad_up = gate_back(grad_inner, gate_proj, up_proj)
    grad_norm_two = lax.psum_scatter(
        (nt(grad_gate, w_gate) + nt(grad_up, w_up)).astype(BF),
        "shard",
        scatter_dimension=0,
        tiled=True,
    ).astype(F32)
    mlp_out = lax.psum_scatter(
        nn(inner_act, w_down).astype(BF), "shard", scatter_dimension=0, tiled=True
    ).astype(F32)
    result = (middle + mlp_out).astype(BF).reshape(seqs, stretch, width)
    feed_grads = jnp.stack(
        [
            tn(norm_two_all, grad_gate).astype(BF),
            tn(norm_two_all, grad_up).astype(BF),
            tn(grad_low_all, inner_act).astype(BF),
        ]
    )
    grad_mid_norm, grad_gain_two = norm_back(grad_norm_two, middle, inv_two, gain_two)
    grad_middle = grad_out + grad_mid_norm
    sum_feed, sum_out, sum_query, sum_kv, sum_gain, grad_input = backward_call(
        shards,
        line,
        grad_middle,
        attn,
        attn.T,
        packed_q,
        norm_one.T,
        tokens.reshape(rows, width),
        gain_one[None],
        cos_wide,
        sin_wide,
        grad_gain_two[None],
        out_all,
        wq_all,
        wkv_all,
        soft,
        packed_kv,
        feed_grads,
    )
    sum_kv = sum_kv.reshape(-1, HK, 2, HD)
    span = attn_gain.shape[0]
    sum_gain = lax.dynamic_slice_in_dim(sum_gain, lax.axis_index("shard") * span, span, 1)
    return (
        result,
        grad_input.reshape(seqs, stretch, width),
        sum_gain[0],
        sum_query.astype(F32),
        sum_kv[:, :, 0].reshape(-1, HK * HD).astype(F32),
        sum_kv[:, :, 1].reshape(-1, HK * HD).astype(F32),
        sum_out.astype(F32),
        sum_gain[1],
        sum_feed[0].astype(F32),
        sum_feed[1].astype(F32),
        sum_feed[2].T.astype(F32),
    )


def solution(mesh):
    shards, ctx = mesh.devices.shape
    inner = Mesh(mesh.devices.reshape(shards, ctx // 2, 2), ("shard", "line", "core"))
    where = ("line", "core")
    return jax.shard_map(
        per_device,
        mesh=inner,
        in_specs=(
            P("shard", where, None),
            P("shard", where, None),
            P("shard", None),
            P("shard"),
            P("shard"),
            P("shard", None),
            P("shard", None),
            P("shard", None),
            P("shard", None),
            P("shard"),
            P(None, "shard"),
            P(None, "shard"),
            P("shard", None),
        ),
        out_specs=(
            P("shard", where, None),
            P("shard", where, None),
            P("shard"),
            P("shard", None),
            P("shard", None),
            P("shard", None),
            P("shard", None),
            P("shard"),
            P(None, "shard"),
            P(None, "shard"),
            P("shard", None),
        ),
        check_vma=False,
    )
```

time: 894 us -> 571 us (0.64)
  waiting for transfers between devices: 551 us -> 214 us
  Pallas kernels: 0 us -> 197 us
  matrix products: 154 us -> 55.9 us
  blocking collectives: 53.2 us -> 9.57 us
  local copies, waits for them, and re-layouts: 58.4 us -> 37.5 us
  other arithmetic: 50 us -> 31.3 us
    pallas_call x0 -> x2, Pallas kernels: none -> 197 us  [the longest x1 183 us: backward_call(): pl.pallas_call(lambda *refs: backward_kernel(sizes, *refs), out_shape=(ja...]
    psum x1 -> x0, waiting for transfers between devices: 168 us -> none  [over_ctx(): share = lax.psum(share, 'line')]
    reduce_scatter x10 -> x2, waiting for transfers between devices: 208 us -> 53.3 us  [the longest x1 41 us: per_device(): lax.psum_scatter(nn(inner_act, w_down).astype(BF), 'shard', scatter_dimen...]
    dot_general x29 -> x12, matrix products: 154 us -> 55.9 us  [the longest x6 26.9 us: nn(): lax.dot_general(a, b, (((1,), (0,)), ((), ())), preferred_element_type=F32)]
    psum x1 -> x0, blocking collectives: 39.3 us -> none  [per_device(): gains = lax.psum(gains, ('shard', 'line', 'core')).astype(jnp.float32)]
    all_gather x6 -> x1, waiting for transfers between devices: 41.1 us -> 15.3 us  [per_device(): packed_kv = lax.all_gather(packed_kv, where_ctx, axis=2, tiled=True)]
    dynamic_slice x12 -> x0, local copies, waits for them, and re-layouts: 14.7 us -> none  [the longest x2 4.16 us: query_step(): value_piece = lax.dynamic_slice_in_dim(value_full, offset, sub_rows, 1)]
    convert_element_type x15 -> x10, other arithmetic: 29.2 us -> 16.2 us  [the longest x1 8.36 us: per_device(): sum_feed[2].T.astype(F32)]
  transfers between devices with their start and end apart: 21 -> 7, of which waited for: 16 -> 7; matrix products, arithmetic and copies ran while one was open for 17% -> 11% of each run, Pallas kernels for 0% -> 3%
where the time goes in v2:
time: 571 us; the launch traced here: 561 us
  waiting for transfers between devices  214 us (37%)
  Pallas kernels  197 us (35%)
  matrix products  55.9 us (10%)
  local copies, waits for them, and re-layouts  37.5 us (7%)
  other arithmetic  31.3 us (5%)
  between operations  15.1 us (3%)
  blocking collectives  9.57 us (2%)
    pallas_call x1, Pallas kernels, backward_call(): pl.pallas_call(lambda *refs: backward_kernel(sizes, *refs), out_shape=(ja...  183 us
    all_gather x1, waiting for transfers between devices, per_device(): qkv_all = lax.all_gather(qkv_local, 'shard', axis=0, tiled=True)  45.6 us
    reduce_scatter x1, waiting for transfers between devices, per_device(): lax.psum_scatter(nn(inner_act, w_down).astype(BF), 'shard', scatter_dimen...  41 us
    all_gather x1, waiting for transfers between devices, per_device(): norm_two_all = lax.all_gather(norm_two, 'shard', axis=0, tiled=True)  38.3 us
    all_gather x1, waiting for transfers between devices, per_device(): out_all = lax.all_gather(w_out, 'shard', axis=0, tiled=True)  31.2 us
    all_gather x1, waiting for transfers between devices, per_device(): grad_low_all = lax.all_gather(grad_low, 'shard', axis=0, tiled=True)  29.2 us
    dot_general x6, matrix products, nn(): lax.dot_general(a, b, (((1,), (0,)), ((), ())), preferred_element_type=F32)  26.9 us
    dot_general x3, matrix products, nt(): lax.dot_general(a, b, (((1,), (1,)), ((), ())), preferred_element_type=F32)  17.1 us
  transfers between devices with their start and end apart: 7, of which 7 were waited for; matrix products, arithmetic and copies ran while one was open for 11% of the time, Pallas kernels for 3%

profile of v2, /device:TPU:0, one launch (start us, length us, event | category | flops | bytes accessed | tf_op | source)
XLA Modules:
  0.0 561.2 jit_solution(17564170219897066918)
XLA Ops:
  7.2 1.2 copy.77
  8.4 1.1 copy.76
  10.0 1.1 pad_maximum_fusion.1
  11.3 9.6 %all-gather = bf16[4,320,2]{1,2,0:T(2,128)(2,1)S(1)} all-gather(bf16[1,320,2]{1,2,0:T(2,128)(2,1)S(1)} %maximum_bitcast_fusion), channel_id=1, replica_groups=mesh['shard'=4,'line'=4,'core'=2] {'shard'}, dimensions={0}, use_global_device_ids=true | all-gather | bytes 6400 | tf_op jit(solution)/shard_map/all_gather | solution.py:837
  21.0 0.6 fusion.26
  21.7 0.5 multiply_cosine_fusion
  22.2 0.3 broadcast_select_fusion.1
  22.5 0.8 copy.87
  23.3 0.8 copy.86
  24.0 0.5 fusion.27
  24.5 0.6 fusion.25
  25.4 0.6 fusion.28
  25.9 1.1 fusion.12
  27.0 45.6 %all-gather.7.cloned.1.call-done = bf16[1280,1920]{1,0:T(8,128)(2,1)} async-done(((bf16[320,1920]{1,0:T(8,128)(2,1)}), bf16[1280,1920]{1,0:T(8,128)(2,1)}) %all-gather.7.cloned.1.call-update) | async-done | bytes 4915216 | tf_op jit(solution)/shard_map/all_gather | solution.py:843
  72.6 2.8 fusion.30
  75.5 1.2 copy.85
  76.7 1.8 fusion.38
  79.0 1.5 copy.88
  80.5 0.7 all-gather.11.cloned.1.call-update
  81.3 0.8 copy.83
  82.2 2.0 and_select_fusion.bias_ref
  84.2 4.1 fusion.31
  88.2 3.4 copy.80
  91.6 3.2 fusion.37
  95.1 0.7 copy-done.11
  95.8 0.4 fusion.23
  96.4 1.3 copy.84
  97.7 1.4 pad.4.qp_ref.refs_3_
  99.1 15.3 %all-gather.9.cloned.1.call-done = bf16[2,5,1024,128]{3,2,1,0:T(8,128)(2,1)} async-done(((bf16[2,5,128,128]{3,2,1,0:T(8,128)(2,1)}), bf16[2,5,1024,128]{3,2,1,0:T(8,128)(2,1)}) %all-gather.9.cloned.1.call-update) | async-done | bytes 2621456 | tf_op jit(solution)/shard_map/all_gather | solution.py:859
  114.3 14.7 %attend.1 = (bf16[10,1024,512]{2,1,0:T(8,128)(2,1)}, bf16[256,1280]{1,0:T(8,128)(2,1)}) custom-call(bf16[10,512,128]{2,1,0:T(8,128)(2,1)} %pad.4.qp_ref.refs_3_, bf16[10,1024,128]{2,1,0:T(8,128)(2,1)} %bitcast.93, f32[2,1024,128]{2,1,0:T(8,128)} %and_select_fusion.bias_ref), custom_call_target="tpu_custom_call" | custom-call | tf_op jit(solution)/shard_map/attend/pallas_call | solution.py:744
  129.0 31.2 %all-gather.11.cloned.1.call-done.refs_10_ = bf16[1280,1280]{1,0:T(8,128)(2,1)} async-done(((bf16[320,1280]{1,0:T(8,128)(2,1)}), bf16[1280,1280]{1,0:T(8,128)(2,1)}) %all-gather.11.cloned.1.call-update) | async-done | bytes 3276816 | tf_op jit(solution)/shard_map/all_gather | solution.py:844
  160.3 3.4 multiply_reduce_fusion
  163.7 1.0 multiply_convert_fusion.3
  164.8 1.0 fusion.18
  166.1 38.3 %all-gather.13.cloned.1.call-done = bf16[1024,1280]{1,0:T(8,128)(2,1)} async-done(((bf16[256,1280]{1,0:T(8,128)(2,1)}), bf16[1024,1280]{1,0:T(8,128)(2,1)}) %all-gather.13.cloned.1.call-update) | async-done | bytes 2621456 | tf_op jit(solution)/shard_map/all_gather | solution.py:865
  204.4 7.3 %fusion.39 = f32[1024,896]{1,0:T(8,128)} fusion(bf16[1024,1280]{1,0:T(8,128)(2,1)} %all-gather.13.cloned.1.call-done, bf16[1280,896]{1,0:T(8,128)(2,1)} %param.23), kind=kOutput, calls=%fused_computation.93 | convolution fusion | flops 2348810240 | bytes 8585216 | tf_op jit(solution)/shard_map/dot_general | solution.py:25
  211.7 4.7 fusion.40
  216.4 29.2 %all-gather.15.cloned.1.call-done = bf16[1024,1280]{1,0:T(8,128)(2,1)} async-done(((bf16[256,1280]{1,0:T(8,128)(2,1)}), bf16[1024,1280]{1,0:T(8,128)(2,1)}) %all-gather.15.cloned.1.call-update) | async-done | bytes 2621456 | tf_op jit(solution)/shard_map/all_gather | solution.py:847
  245.6 10.0 %multiply_convert_fusion = (bf16[1024,896]{1,0:T(8,128)(2,1)S(1)}, bf16[1024,896]{1,0:T(8,128)(2,1)S(1)}, bf16[1024,896]{1,0:T(8,128)(2,1)}) fusion(f32[1024,896]{1,0:T(8,128)} %fusion.39, f32[1024,896]{1,0:T(8,128)} %fusion.40, bf16[1024,1280]{1,0:T(8,128)(2,1)} %all-gather.15.cloned.1.call-done, bf16[896,1280]{1,0:T(8,128)(2,1)} %param.25), kind=kOutput, calls=%fused_computation.4 | convolution fusion | flops 2363490304 | bytes 17760256 | tf_op jit(solution)/shard_map/dot_general | solution.py:29
  255.7 2.9 fusion.41
  258.7 4.2 add_convert_fusion
  263.1 6.6 %convolution_convert_fusion = bf16[1024,1280]{1,0:T(8,128)(2,1)} fusion(bf16[1024,896]{1,0:T(8,128)(2,1)} %get-tuple-element.83, bf16[896,1280]{1,0:T(8,128)(2,1)} %param.25), kind=kOutput, calls=%fused_computation.3 | convolution fusion | flops 2350120960 | bytes 6750208 | tf_op jit(solution)/shard_map/dot_general | solution.py:25
  269.7 1.1 copy-done.1
  271.0 1.1 copy.90.refs_4_
  272.2 0.6 slice_convert_fusion.1.refs_6_
  272.8 2.2 copy.89
  274.9 5.5 fusion.2
  280.5 3.2 fusion.1
  283.7 3.2 fusion
  286.8 3.5 pad_maximum_fusion.refs_15_
  290.3 12.3 %reduce-scatter.5.cloned.1.call-done = bf16[256,1280]{1,0:T(8,128)(2,1)} async-done(((bf16[1024,1280]{1,0:T(8,128)(2,1)}), bf16[256,1280]{1,0:T(8,128)(2,1)}) %reduce-scatter.5.cloned.1.call-update) | async-done | bytes 655376 | tf_op jit(solution)/shard_map/reduce_scatter | solution.py:871
  302.6 1.5 fusion.14
  304.1 0.6 broadcast_in_dim.58.refs_9_
  304.7 41.0 %reduce-scatter.3.cloned.1.call-done = bf16[256,1280]{1,0:T(8,128)(2,1)} async-done(((bf16[1024,1280]{1,0:T(8,128)(2,1)}), bf16[256,1280]{1,0:T(8,128)(2,1)}) %reduce-scatter.3.cloned.1.call-update) | async-done | bytes 655376 | tf_op jit(solution)/shard_map/reduce_scatter | solution.py:877
  345.8 2.8 fusion.6
  348.6 182.7 %backward.1 = (bf16[3,1280,896]{2,1,0:T(8,128)(2,1)}, bf16[320,1280]{1,0:T(8,128)(2,1)}, bf16[320,1280]{1,0:T(8,128)(2,1)}, bf16[320,640]{1,0:T(8,128)(2,1)}, f3...) custom-call(f32[256,1280]{1,0:T(8,128)} %get-tuple-element.91.refs_0_, bf16[256,1280]{1,0:T(8,128)(2,1)} %get-tuple-element.19.refs_1_, ...), custom_call_target="tpu_custom_call" | custom-call | tf_op jit(solution)/shard_map/backward/pallas_call | solution.py:675
  531.3 2.5 convert_element_type.158
  534.2 1.0 copy.92
  535.2 1.0 copy.93
  536.2 1.3 convert_element_type.163
  537.5 8.4 %convert_bitcast_fusion = (f32[896,1280]{0,1:T(8,128)}, f32[1280,896]{1,0:T(8,128)}, f32[1280,896]{1,0:T(8,128)}) fusion(bf16[3,1280,896]{2,1,0:T(8,128)(2,1)} %get-tuple-element.26), kind=kLoop, calls=%fused_computation.2 | loop fusion | flops 3440640 | bytes 20643840 | tf_op jit(solution)/shard_map/convert_element_type | solution.py:924
  545.9 5.7 %copy.94 = f32[896,1280]{1,0:T(8,128)} copy(f32[896,1280]{0,1:T(8,128)} %get-tuple-element.84) | data formatting | bytes 9175040
  551.6 1.5 dynamic-slice_reduce_fusion
  553.1 0.8 copy.96
  (108 shorter events, 3.4 us)
Async XLA Ops:
  7.2 2.8 copy-start.6
  7.2 65.4 %all-gather.7.cloned.1.call-start = ((), (), s32[]{:S(2)}) async-start(), calls=%async_computation.2 | async-start | bytes 6144000 | tf_op jit(solution)/shard_map/all_gather | solution.py:843
  9.7 1.5 copy-start.24
  9.7 1.5 copy-start.25
  9.8 11.2 %copy-start.18 = (s32[2,1024]{1,0:T(2,128)S(1)}, s32[2,1024]{1,0:T(2,128)}, u32[]{:S(2)}) copy-start(s32[2,1024]{1,0:T(2,128)} %param.15) | copy-start | bytes 24580
  9.8 11.2 %copy-start.21 = (s32[2]{0:T(128)S(1)}, s32[2]{0:T(128)}, u32[]{:S(2)}) copy-start(s32[2]{0:T(128)} %param.16) | copy-start | bytes 28
  10.0 15.1 %copy-start = (bf16[2,128,1280]{2,1,0:T(8,128)(2,1)S(1)}, bf16[2,128,1280]{2,1,0:T(8,128)(2,1)}, u32[]{:S(2)}) copy-start(bf16[2,128,1280]{2,1,0:T(8,128)(2,1)} %param.13) | copy-start | bytes 1966084
  11.2 103.1 %all-gather.9.cloned.1.call-start = ((), (), s32[]{:S(2)}) async-start(), calls=%async_computation.3 | async-start | bytes 2949120 | tf_op jit(solution)/shard_map/all_gather | solution.py:859
  21.0 54.5 %copy-start.14 = (bf16[1280,2]{0,1:T(2,128)(2,1)}, bf16[1280,2]{0,1:T(2,128)(2,1)S(1)}, u32[]{:S(2)}) copy-start(bf16[1280,2]{0,1:T(2,128)(2,1)S(1)} %reshape.284) | copy-start | bytes 15364
  22.5 58.8 %copy-start.5 = (f32[256,128]{1,0:T(8,128)}, f32[256,128]{1,0:T(8,128)S(1)}, u32[]{:S(2)}) copy-start(f32[256,128]{1,0:T(8,128)S(1)} %get-tuple-element.113.refs_8_) | copy-start | bytes 393220
  22.5 59.5 %copy-start.4 = (f32[256,128]{1,0:T(8,128)}, f32[256,128]{1,0:T(8,128)S(1)}, u32[]{:S(2)}) copy-start(f32[256,128]{1,0:T(8,128)S(1)} %get-tuple-element.104.refs_7_) | copy-start | bytes 393220
  25.1 50.3 %copy-start.16 = (f32[1280]{0:T(1024)}, f32[1280]{0:T(1024)S(1)}, u32[]{:S(2)}) copy-start(f32[1280]{0:T(1024)S(1)} %get-tuple-element.76) | copy-start | bytes 15364
  76.7 1.9 copy-start.9
  76.7 1.9 copy-start.10
  76.7 1.9 copy-start.22
  80.5 79.8 %all-gather.11.cloned.1.call-start = ((), (), s32[]{:S(2)}) async-start(), calls=%async_computation.4 | async-start | bytes 4096000 | tf_op jit(solution)/shard_map/all_gather | solution.py:844
  81.2 123.2 %all-gather.13.cloned.1.call-start = ((), (), s32[]{:S(2)}) async-start(), calls=%async_computation.5 | async-start | bytes 3276800 | tf_op jit(solution)/shard_map/all_gather | solution.py:865
  94.8 0.9 copy-start.11
  94.9 0.9 copy-start.23
  160.3 3.4 copy-start.13
  163.7 1.1 copy-start.3
  163.7 1.1 copy-start.19
  164.7 80.9 %all-gather.15.cloned.1.call-start = ((), (), s32[]{:S(2)}) async-start(), calls=%async_computation.7 | async-start | bytes 3276800 | tf_op jit(solution)/shard_map/all_gather | solution.py:847
  165.9 136.7 %reduce-scatter.5.cloned.1.call-start = ((), (), s32[]{:S(2)}) async-start(), calls=%async_computation.8 | async-start | bytes 3276800 | tf_op jit(solution)/shard_map/reduce_scatter | solution.py:871
  204.4 7.3 %copy-start.26 = (bf16[1024,1280]{1,0:T(8,128)(2,1)S(1)}, bf16[1024,1280]{1,0:T(8,128)(2,1)}, u32[]{:S(2)}) copy-start(bf16[1024,1280]{1,0:T(8,128)(2,1)} %all-gather.13.cloned.1.call-done) | copy-start | bytes 7864324
  204.4 7.3 %copy-start.29 = (bf16[1280,896]{1,0:T(8,128)(2,1)S(1)}, bf16[1280,896]{1,0:T(8,128)(2,1)}, u32[]{:S(2)}) copy-start(bf16[1280,896]{1,0:T(8,128)(2,1)} %param.24) | copy-start | bytes 6881284
  245.6 10.0 %copy-start.28 = (bf16[1280,896]{1,0:T(8,128)(2,1)S(1)}, bf16[1280,896]{1,0:T(8,128)(2,1)}, u32[]{:S(2)}) copy-start(bf16[1280,896]{1,0:T(8,128)(2,1)} %param.23) | copy-start | bytes 6881284
  255.7 2.9 copy-start.31
  255.7 2.9 copy-start.33
  255.7 3.0 copy-start.30
  262.9 82.9 %reduce-scatter.3.cloned.1.call-start = ((), (), s32[]{:S(2)}) async-start(), calls=%async_computation.6 | async-start | bytes 3276800 | tf_op jit(solution)/shard_map/reduce_scatter | solution.py:877
  269.7 1.1 copy-start.1
  269.7 1.1 copy-start.17
  269.7 1.1 copy-start.20
  269.7 2.4 copy-start.15
  274.9 5.5 copy-start.27
  274.9 5.5 copy-start.34
  280.5 3.2 copy-start.32
  302.6 43.2 %copy-start.2 = (bf16[256,1280]{1,0:T(8,128)(2,1)S(1)}, bf16[256,1280]{1,0:T(8,128)(2,1)}, u32[]{:S(2)}) copy-start(bf16[256,1280]{1,0:T(8,128)(2,1)} %reduce-scatter.5.cloned.1.call-done) | copy-start | bytes 1966084
  531.3 2.5 copy-start.12
  534.0 2.2 copy-start.7
  545.9 7.2 %copy-start.8 = (bf16[256,1280]{1,0:T(8,128)(2,1)S(1)}, bf16[256,1280]{1,0:T(8,128)(2,1)}, u32[]{:S(2)}) copy-start(bf16[256,1280]{1,0:T(8,128)(2,1)} %get-tuple-element.21) | copy-start | bytes 1966084
Sparse Core Ops, SparseCore 0:
  11.3 61.2 all-gather.6
  80.6 33.6 all-gather.8
  116.2 44.0 all-gather.10
  164.9 39.4 all-gather.12
  206.1 39.4 all-gather.14
  263.0 39.5 reduce-scatter.4
  306.1 39.5 reduce-scatter.2

commit v3 on v2

--- a/solution.py
+++ b/solution.py
@@ -41,6 +41,243 @@
     left = pltpu.roll(block, 96, 1)
     right = pltpu.roll(block, 32, 1)
     return jnp.where(lane % 64 < 32, left, right)
+
+
+def peer_of(s_id, shards, k, back):
+    if shards == 4:
+        if isinstance(k, int):
+            return [s_id, s_id + 1 - 2 * (s_id % 2), (s_id + 2) % 4, 3 - s_id][k]
+        return jnp.where(
+            k == 0,
+            s_id,
+            jnp.where(
+                k == 1, s_id + 1 - 2 * (s_id % 2), jnp.where(k == 2, (s_id + 2) % 4, 3 - s_id)
+            ),
+        )
+    return (s_id + (shards - k if back else k)) % shards
+
+
+def feed_kernel(
+    sizes,
+    n2_ref,
+    mid_ref,
+    g_ref,
+    gain_ref,
+    g_hbm,
+    wg_hbm,
+    wu_hbm,
+    wd_hbm,
+    out_gm,
+    out_gg,
+    out_parts,
+    out_dw,
+    n2_all,
+    g_all,
+    wg,
+    wu,
+    wd,
+    inner,
+    dgate,
+    dup,
+    back,
+    zone,
+    part_stage,
+    dw_stage,
+    load_sem,
+    n2_send,
+    n2_recv,
+    back_send,
+    back_recv,
+    part_sem,
+    dw_sem,
+):
+    shards, rows, width, feed = sizes
+    s_id, l_id, c_id = lax.axis_index("shard"), lax.axis_index("line"), lax.axis_index("core")
+
+    def remote(src, dst, send, recv, shard):
+        return pltpu.make_async_remote_copy(
+            src,
+            dst,
+            send,
+            recv,
+            device_id=(shard, l_id, c_id),
+            device_id_type=BY_MESH,
+        )
+
+    barrier = pltpu.get_barrier_semaphore()
+    for k in range(1, shards):
+        pl.semaphore_signal(
+            barrier,
+            inc=1,
+            device_id=(peer_of(s_id, shards, k, False), l_id, c_id),
+            device_id_type=BY_MESH,
+        )
+    pl.semaphore_wait(barrier, shards - 1)
+
+    def n2_copy(k):
+        return remote(
+            n2_ref,
+            n2_all.at[s_id],
+            n2_send.at[k],
+            n2_recv.at[k],
+            peer_of(s_id, shards, k, False),
+        )
+
+    for k in range(1, shards):
+        n2_copy(k).start()
+    loads = [
+        pltpu.make_async_copy(src, dst, load_sem.at[i])
+        for i, (src, dst) in enumerate(
+            ((wg_hbm, wg), (wu_hbm, wu), (g_hbm, g_all), (wd_hbm, wd))
+        )
+    ]
+    for load in loads:
+        load.start()
+    n2_all[s_id] = n2_ref[...]
+    for load in loads:
+        load.wait()
+
+    def back_copy(k):
+        return remote(
+            back.at[peer_of(s_id, shards, k, True)],
+            zone.at[k - 1],
+            back_send.at[k],
+            back_recv.at[k],
+            peer_of(s_id, shards, k, True),
+        )
+
+    def block(step, carry):
+        k = step
+        source = peer_of(s_id, shards, k, True)
+
+        @pl.when(k > 0)
+        def _():
+            remote(n2_ref, n2_all.at[source], n2_send.at[k], n2_recv.at[k], source).wait_recv()
+
+        normed, grad = n2_all[source], g_all[source]
+        gate, upper = nn(normed, wg[...]), nn(normed, wu[...])
+        grad_inner = nt(grad, wd[...])
+        sig = 1.0 / (1.0 + jnp.exp(-gate))
+        act = gate * sig
+        inner[source] = (act * upper).astype(BF)
+        dgate[source] = (grad_inner * upper * sig * (1.0 + gate * (1.0 - sig))).astype(BF)
+        dup[source] = (grad_inner * act).astype(BF)
+        back[source] = (nt(dgate[source], wg[...]) + nt(dup[source], wu[...])).astype(BF)
+
+        @pl.when(k > 0)
+        def _():
+            back_copy(k).start()
+
+        return carry
+
+    lax.fori_loop(0, shards, block, 0)
+
+    def part_copy(k, slot):
+        return pltpu.make_async_copy(part_stage.at[slot], out_parts.at[k], part_sem.at[slot])
+
+    def project(k, carry):
+        slot = k % 2
+
+        @pl.when(k >= 2)
+        def _():
+            part_copy(k - 2, slot).wait()
+
+        part_stage[slot] = nn(inner[k], wd[...]).astype(BF)
+        part_copy(k, slot).start()
+        return carry
+
+    def dw_copy(tile, slot):
+        span = pl.ds(pl.multiple_of(tile * 256, 256), 256)
+        return pltpu.make_async_copy(dw_stage.at[slot], out_dw.at[:, span, :], dw_sem.at[slot])
+
+    def weight(tile, carry):
+        slot = tile % 2
+
+        @pl.when(tile >= 2)
+        def _():
+            dw_copy(tile - 2, slot).wait()
+
+        span = pl.ds(pl.multiple_of(tile * 256, 256), 256)
+        left = jnp.zeros((256, feed), F32)
+        right = jnp.zeros((256, feed), F32)
+        low = jnp.zeros((256, feed), F32)
+        for k in range(shards):
+            n2_t = jnp.transpose(n2_all[k, :, span])
+            left = left + nn(n2_t, dgate[k])
+            right = right + nn(n2_t, dup[k])
+            low = low + nn(jnp.transpose(g_all[k, :, span]), inner[k])
+        dw_stage[slot, 0] = left.astype(BF)
+        dw_stage[slot, 1] = right.astype(BF)
+        dw_stage[slot, 2] = low.astype(BF)
+        dw_copy(tile, slot).start()
+        return carry
+
+    tiles = width // 256
+    lax.fori_loop(0, tiles, weight, 0)
+    lax.fori_loop(0, shards, project, 0)
+    total = back[s_id].astype(F32)
+    for k in range(1, shards):
+        back_copy(k).wait()
+        total = total + zone[k - 1].astype(F32)
+    hidden = mid_ref[...]
+    scale = lax.rsqrt(jnp.mean(hidden * hidden, -1, keepdims=True) + EPSILON)
+    scaled = total * gain_ref[...]
+    out_gg[...] = jnp.sum(total * hidden * scale, 0, keepdims=True)
+    out_gm[...] = (
+        g_ref[...].astype(F32)
+        + scale * scaled
+        - hidden * (scale * scale * scale) * jnp.mean(scaled * hidden, -1, keepdims=True)
+    )
+    for k in range(1, shards):
+        n2_copy(k).wait_send()
+    for last in (2, 1):
+        part_copy(shards - last, (shards - last) % 2).wait()
+        dw_copy(tiles - last, (tiles - last) % 2).wait()
+
+
+def feed_call(shards, n2, middle, grad, gain, grad_all, w_gate, w_up, w_down):
+    rows, width = n2.shape
+    feed = w_gate.shape[1]
+    dma = pltpu.SemaphoreType.DMA
+    v = pltpu.VMEM
+    vm = pl.BlockSpec(memory_space=pltpu.VMEM)
+    hbm = pl.BlockSpec(memory_space=pltpu.HBM)
+    return pl.pallas_call(
+        lambda *refs: feed_kernel((shards, rows, width, feed), *refs),
+        out_shape=(
+            jax.ShapeDtypeStruct((rows, width), F32),
+            jax.ShapeDtypeStruct((1, width), F32),
+            jax.ShapeDtypeStruct((shards, rows, width), BF),
+            jax.ShapeDtypeStruct((3, width, feed), BF),
+        ),
+        in_specs=[vm] * 4 + [hbm] * 4,
+        out_specs=(vm, vm, hbm, hbm),
+        scratch_shapes=[
+            v((shards, rows, width), BF),
+            v((shards, rows, width), BF),
+            v((width, feed), BF),
+            v((width, feed), BF),
+            v((feed, width), BF),
+            v((shards, rows, feed), BF),
+            v((shards, rows, feed), BF),
+            v((shards, rows, feed), BF),
+            v((shards, rows, width), BF),
+            v((shards - 1, rows, width), BF),
+            v((2, rows, width), BF),
+            v((2, 3, 256, feed), BF),
+            dma((4,)),
+            dma((shards,)),
+            dma((shards,)),
+            dma((shards,)),
+            dma((shards,)),
+            dma((2,)),
+            dma((2,)),
+        ],
+        compiler_params=pltpu.CompilerParams(
+            collective_id=2, has_side_effects=True, vmem_limit_bytes=VMEM_LIMIT
+        ),
+        name="feed",
+    )(n2, middle, grad, gain, grad_all, w_gate, w_up, w_down)
 
 
 def add_rows(target, parts, rows, step):
@@ -67,6 +304,8 @@
     cos_ref,
     sin_ref,
     gg_ref,
+    mid_ref,
+    parts_hbm,
     wo_hbm,
     wq_hbm,
     wkv_hbm,
@@ -79,6 +318,8 @@
     out_wkv,
     out_gain,
     out_dx,
+    out_result,
+    p_zone,
     w_buf,
     wkv_buf,
     pt_buf,
@@ -96,7 +337,6 @@
     got_r,
     got_t,
     g_buf,
-    g_kv,
     o_x,
     o_z,
     o_r,
@@ -138,6 +378,8 @@
     a_sib_send,
     a_sib_recv,
     a_local,
+    p_send,
+    p_recv,
 ):
     shards, line, keys, rows, width, feed = sizes
     s_id, l_id, c_id = lax.axis_index("shard"), lax.axis_index("line"), lax.axis_index("core")
@@ -148,7 +390,7 @@
     has_outer = (l_id > 0) & (l_id < line - 1)
     is_mid = (l_id == line // 2 - 1) | (l_id == line // 2)
     outer = (s_id, jnp.where(has_outer, l_id - toward, l_id + toward), c_id)
-    peers = [(lax.rem(s_id + k, shards), l_id, c_id) for k in range(1, shards)]
+    peers = [(peer_of(s_id, shards, k, False), l_id, c_id) for k in range(1, shards)]
     mates = [(s_id, lax.rem(l_id + k, line), c_id) for k in range(1, line)]
 
     def remote(src, dst, send, recv, to):
@@ -182,6 +424,16 @@
     load_wkv = pltpu.make_async_copy(wkv_hbm, wkv_buf, load_sem.at[4])
     load_wq = pltpu.make_async_copy(wq_hbm, w_buf, load_sem.at[5])
     load_wo.start()
+
+    def part_copy(k):
+        return remote(
+            parts_hbm.at[peer_of(s_id, shards, k, False)],
+            p_zone.at[k - 1],
+            p_send.at[k - 1],
+            p_recv.at[k - 1],
+            peers[k - 1],
+        )
+
     for k in range(3):
         own_load[k].start()
         core_copy[k].start()
@@ -312,7 +564,7 @@
 
     def scatter_copy(box, zone, slot, k):
         return remote(
-            box.at[lax.rem(s_id + k, shards)],
+            box.at[peer_of(s_id, shards, k, False)],
             zone.at[k - 1],
             g_send.at[slot, k - 1],
             g_recv.at[slot, k - 1],
@@ -512,6 +764,8 @@
                 total * cos - swap_halves(total, lane) * sin
             ).astype(BF)
 
+    for k in range(1, shards):
+        part_copy(k).start()
     lax.fori_loop(0, HK * blocks, attend, 0)
     dkv_core_copy(0).start()
     scatter_part(g_buf, o_x, o_z, 0)
@@ -538,6 +792,7 @@
     back = nt(dq[...], w_buf[...])
     dkv_gather(0)
     dkv_gather(1)
+    g_kv = g_buf.at[:, :, pl.ds(0, 2 * HK * HD)]
     weight_grad(n1_t_ref, dkv_own, g_kv, shards)
     core_part(g_kv, None, k_x, 2).start()
     ring(8)
@@ -557,6 +812,24 @@
         - hidden * (scale * scale * scale) * jnp.mean(scaled * hidden, -1, keepdims=True)
     ).astype(BF)
     ring(9)
+    for k in range(1, shards):
+        part_copy(k).wait()
+    result = mid_ref[...]
+    for first in range(0, shards, 4):
+        stage = [
+            pltpu.make_async_copy(
+                parts_hbm.at[s_id] if k == 0 else p_zone.at[k - 1],
+                w_buf.at[pl.ds((k - first) * rows, rows)],
+                load_sem.at[k - first],
+            )
+            for k in range(first, min(shards, first + 4))
+        ]
+        for copy in stage:
+            copy.start()
+        for k, copy in enumerate(stage):
+            copy.wait()
+            result = result + w_buf[k * rows : (k + 1) * rows, :].astype(F32)
+    out_result[...] = result.astype(BF)
     gather_part(q_x, q_z, 1)
     line_up(q_x.at[s_id], q_r, q_t, 1, own_rows)
     gain_core.wait()
@@ -608,7 +881,7 @@
 
 
 def backward_call(
-    shards, line, gm, attn, attn_t, qp, n1_t, x, gain, cos, sin, gg, wo, wq, wkv, pt, kv, dw
+    shards, line, gm, attn, attn_t, qp, n1_t, x, gain, cos, sin, gg, middle, parts, wo, wq, wkv, pt, kv, dw
 ):
     rows, width = gm.shape
     keys = kv.shape[1]
@@ -650,7 +923,6 @@
         v((3, half, feed), BF),
         v((3, half, feed), BF),
         v((shards, part, width), BF),
-        v((shards, part, kv_width), BF),
         *boxes(width),
         *boxes(width),
         *boxes(kv_width),
@@ -671,6 +943,8 @@
         dma((4, shards - 1)),
         dma((4, shards - 1)),
         *[dma((4,)) for _ in range(7)],
+        dma((shards - 1,)),
+        dma((shards - 1,)),
     ]
     return pl.pallas_call(
         lambda *refs: backward_kernel(sizes, *refs),
@@ -681,85 +955,466 @@
             jax.ShapeDtypeStruct((part, kv_width), BF),
             jax.ShapeDtypeStruct((8, width), F32),
             jax.ShapeDtypeStruct((rows, width), BF),
+            jax.ShapeDtypeStruct((rows, width), BF),
+            jax.ShapeDtypeStruct((shards - 1, rows, width), BF),
         ),
-        in_specs=[vm] * 10 + [hbm] * 6,
-        out_specs=(hbm, hbm, hbm, hbm, hbm, vm),
+        in_specs=[vm] * 11 + [hbm] * 7,
+        out_specs=(hbm, hbm, hbm, hbm, hbm, vm, vm, hbm),
         scratch_shapes=scratch,
         compiler_params=pltpu.CompilerParams(
             collective_id=3, has_side_effects=True, vmem_limit_bytes=VMEM_LIMIT
         ),
         name="backward",
-    )(gm, attn, attn_t, qp, n1_t, x, gain, cos, sin, gg, wo, wq, wkv, pt, kv, dw)
-
-
-def attend_kernel(qp_ref, kv_ref, bias_ref, pt_ref, out_ref):
-    blocks = kv_ref.shape[1] // 1024
-
-    def scores(block):
+    )(gm, attn, attn_t, qp, n1_t, x, gain, cos, sin, gg, middle, parts, wo, wq, wkv, pt, kv, dw)
+
+
+class Spread:
+    def __init__(self, env, block, source, sems, shared):
+        self.env, self.block, self.source, self.shared = env, block, source, shared
+        self.send, self.recv, self.sib_send, self.sib_recv = sems
+        self.relay = env.shards == 4
+
+    def copy(self, k):
+        env = self.env
+        return env.remote(
+            self.source,
+            self.block(env.s_id, env.c_id, 0, 2),
+            self.send.at[k],
+            self.recv.at[k],
+            env.peer(k),
+        )
+
+    def passing(self, k):
+        env = self.env
+        piece = self.block(env.origin(k), env.c_id, k - 1, 1)
+        return env.remote(
+            piece, piece, self.send.at[2 + k], self.recv.at[2 + k], env.peer(3 - k)
+        )
+
+    def direct(self):
+        return range(1, 3 if self.relay else self.env.shards)
+
+    def start(self):
+        for k in self.direct():
+            self.copy(k).start()
+
+    def sib_copy(self, k):
+        piece = self.block(self.env.origin(k), self.env.c_id, 0, 2)
+        return self.env.remote(
+            piece, piece, self.sib_send.at[k], self.sib_recv.at[k], self.env.sibling
+        )
+
+    def forward(self):
+        for k in self.direct():
+            self.copy(k).wait_recv()
+            if self.relay:
+                self.passing(k).start()
+            if self.shared:
+                self.sib_copy(k).start()
+
+    def collect(self):
+        if self.relay:
+            for k in (1, 2):
+                self.passing(k).wait_recv()
+            if self.shared:
+                self.sib_copy(3).start()
+
+    def finish(self):
+        if self.shared:
+            for k in range(1, self.env.shards):
+                self.sib_copy(k).wait_recv()
+
+    def settle(self):
+        for k in self.direct():
+            self.copy(k).wait_send()
+            if self.relay:
+                self.passing(k).wait_send()
+        if self.shared:
+            for k in range(1, self.env.shards):
+                self.sib_copy(k).wait_send()
+
+
+class Env:
+    def __init__(self, shards, line):
+        self.shards, self.line = shards, line
+        self.s_id = lax.axis_index("shard")
+        self.l_id = lax.axis_index("line")
+        self.c_id = lax.axis_index("core")
+        self.sibling = (self.s_id, self.l_id, 1 - self.c_id)
+
+    def remote(self, src, dst, send, recv, to):
+        return pltpu.make_async_remote_copy(
+            src, dst, send, recv, device_id=to, device_id_type=BY_MESH
+        )
+
+    def peer(self, k):
+        return (peer_of(self.s_id, self.shards, k, False), self.l_id, self.c_id)
+
+    def origin(self, k):
+        return peer_of(self.s_id, self.shards, k, True)
+
+    def mate(self, k):
+        return (self.s_id, lax.rem(self.l_id + k, self.line), self.c_id)
+
+    def barrier(self, others):
+        barrier = pltpu.get_barrier_semaphore()
+        for other in others:
+            pl.semaphore_signal(barrier, inc=1, device_id=other, device_id_type=BY_MESH)
+        pl.semaphore_wait(barrier, len(others))
+
+
+def front_kernel(
+    sizes,
+    x_ref,
+    gains_ref,
+    wq_ref,
+    wkv_ref,
+    wo_ref,
+    g_ref,
+    bias_ref,
+    cos_ref,
+    sin_ref,
+    out_attn,
+    out_attn_t,
+    out_n1_t,
+    out_qp,
+    out_mid,
+    out_n2,
+    out_gains,
+    out_wq,
+    out_wkv,
+    out_wo,
+    out_kv,
+    out_pt,
+    out_g,
+    wq_all,
+    wkv_all,
+    wo_all,
+    kv_all,
+    norm,
+    gain_zone,
+    pt_stage,
+    gain_send,
+    gain_recv,
+    wq_s,
+    wq_r,
+    wq_ss,
+    wq_sr,
+    wkv_s,
+    wkv_r,
+    wkv_ss,
+    wkv_sr,
+    wo_s,
+    wo_r,
+    wo_ss,
+    wo_sr,
+    g_s,
+    g_r,
+    kv_send,
+    kv_recv,
+    kv_sib_send,
+    kv_sib_recv,
+    pt_sem,
+    out_sem,
+):
+    shards, line, keys, rows, width = sizes
+    env = Env(shards, line)
+    s_id, l_id, c_id = env.s_id, env.l_id, env.c_id
+    part = width // shards
+    hp = part // 2
+    quarter = hp // 2
+    blocks = keys // 1024
+    env.barrier(
+        [env.sibling]
+        + [env.peer(k) for k in range(1, shards)]
+        + [env.mate(k) for k in range(1, line)]
+    )
+
+    def rows_of(ref):
+        def block(s, core, first, count):
+            start = s * part + core * hp + first * quarter
+            return ref.at[pl.ds(pl.multiple_of(start, 16), count * quarter)]
+
+        return block
+
+    def g_rows(s, core, first, count):
+        start = s * rows + first * (rows // 2)
+        return out_g.at[pl.ds(pl.multiple_of(start, 16), count * (rows // 2))]
+
+    mine = pl.ds(pl.multiple_of(c_id * hp, 16), hp)
+    own = pl.ds(pl.multiple_of(s_id * part, 16), part)
+    kv_gather = Spread(
+        env, rows_of(wkv_all), wkv_ref.at[mine], (wkv_s, wkv_r, wkv_ss, wkv_sr), True
+    )
+    q_gather = Spread(env, rows_of(wq_all), wq_ref.at[mine], (wq_s, wq_r, wq_ss, wq_sr), True)
+    o_gather = Spread(env, rows_of(wo_all), wo_ref.at[mine], (wo_s, wo_r, wo_ss, wo_sr), True)
+    grad_gather = Spread(env, g_rows, g_ref, (g_s, g_r, None, None), False)
+
+    def gain_copy(k):
+        return env.remote(
+            gains_ref, gain_zone.at[s_id], gain_send.at[k], gain_recv.at[k], env.peer(k)
+        )
+
+    for k in range(1, shards):
+        gain_copy(k).start()
+    kv_gather.start()
+    q_gather.start()
+    locals_ = [
+        pltpu.make_async_copy(wkv_ref, wkv_all.at[own], out_sem.at[0]),
+        pltpu.make_async_copy(wq_ref, wq_all.at[own], out_sem.at[1]),
+        pltpu.make_async_copy(wo_ref, wo_all.at[own], out_sem.at[2]),
+        pltpu.make_async_copy(
+            g_ref, out_g.at[pl.ds(pl.multiple_of(s_id * rows, 16), rows)], out_sem.at[3]
+        ),
+    ]
+    for copy in locals_:
+        copy.start()
+    gain_zone[s_id] = gains_ref[...]
+    hidden = x_ref[...].astype(F32)
+    scale = lax.rsqrt(jnp.mean(hidden * hidden, -1, keepdims=True) + EPSILON)
+    for k in range(1, shards):
+        gain_copy(k).wait()
+    out_gains[...] = jnp.concatenate([gain_zone[s] for s in range(shards)], 1)
+    norm[...] = (hidden * scale * out_gains[0:1, :]).astype(BF)
+    for tile in range(width // 128):
+        piece = norm[:, tile * 128 : tile * 128 + 128].astype(F32)
+        out_n1_t[tile * 128 : tile * 128 + 128, :] = jnp.transpose(piece).astype(BF)
+    kv_gather.forward()
+    q_gather.forward()
+    o_gather.start()
+    kv_gather.collect()
+    q_gather.collect()
+    grad_gather.start()
+    for copy in locals_:
+        copy.wait()
+    kv_gather.finish()
+
+    lane = lanes_of(128)
+    place = l_id * 2 + c_id
+
+    def make_kv(head, carry):
+        block = nn(norm[...], wkv_all[:, pl.ds(pl.multiple_of(head * 128, 128), 128)])
+        for seq in range(2):
+            piece = block[seq * 128 : seq * 128 + 128]
+            cos = jnp.where(lane < 64, cos_ref[pl.ds(seq * 128, 128), :], 1.0)
+            sin = jnp.where(lane < 64, sin_ref[pl.ds(seq * 128, 128), :], 0.0)
+            kv_all[seq * HK + head, place] = (piece * cos + swap_halves(piece, lane) * sin).astype(
+                BF
+            )
+        return carry
+
+    lax.fori_loop(0, HK, make_kv, 0)
+
+    def kv_slice(seq, l, c):
+        return kv_all.at[pl.ds(seq * HK, HK), l * 2 + c]
+
+    def kv_copy(seq, k):
+        piece = kv_slice(seq, l_id, c_id)
+        return env.remote(
+            piece, piece, kv_send.at[seq, k - 1], kv_recv.at[seq, k - 1], env.mate(k)
+        )
+
+    def kv_sib(seq, k):
+        piece = kv_slice(seq, lax.rem(l_id + line - k, line), c_id)
+        return env.remote(
+            piece, piece, kv_sib_send.at[seq, k], kv_sib_recv.at[seq, k], env.sibling
+        )
+
+    for seq in range(2):
+        for k in range(1, line):
+            kv_copy(seq, k).start()
+        kv_sib(seq, 0).start()
+
+    q_gather.finish()
+
+    def make_q(head, carry):
+        block = nn(norm[...], wq_all[:, pl.ds(pl.multiple_of(head * 256, 256), 256)])
+        for seq in range(2):
+            cos = cos_ref[pl.ds(seq * 128, 128), :]
+            sin = sin_ref[pl.ds(seq * 128, 128), :]
+            for two in range(2):
+                piece = block[seq * 128 : seq * 128 + 128, two * 128 : two * 128 + 128]
+                piece = piece * cos + swap_halves(piece, lane) * sin
+                piece = piece.astype(BF).astype(F32) * (1.0 / math.sqrt(HD))
+                pair = seq * HK + head
+                out_qp[pair, pl.ds(two * 256, 128), :] = jnp.where(lane < 64, piece, 0.0).astype(
+                    BF
+                )
+                out_qp[pair, pl.ds(two * 256 + 128, 128), :] = jnp.where(
+                    lane < 64, pltpu.roll(piece, 64, 1), 0.0
+                ).astype(BF)
+        return carry
+
+    lax.fori_loop(0, HK, make_q, 0)
+    o_gather.forward()
+
+    def pt_copy(pair, block, slot):
         span = pl.ds(pl.multiple_of(block * 1024, 1024), 1024)
-        bias = bias_ref[0, span, :]
-        return nt(kv_ref[0, span, :], qp_ref[0]) + jnp.concatenate([bias] * GROUP, 1)
-
+        return pltpu.make_async_copy(pt_stage.at[slot], out_pt.at[pair, span], pt_sem.at[slot])
+
+    def keys_of(pair, block):
+        if blocks == 1:
+            return kv_all[pair].reshape(1024, 128)
+        return kv_all[pair, pl.ds(block * 8, 8)].reshape(1024, 128)
+
+    def scores(pair, block):
+        span = pl.ds(pl.multiple_of(block * 1024, 1024), 1024)
+        bias = bias_ref[pair // HK, span, :]
+        return nt(keys_of(pair, block), out_qp[pair]) + jnp.concatenate([bias] * GROUP, 1)
+
+    def attend(pair, carry):
+        if blocks == 1:
+            slot = lax.rem(pair, 2)
+
+            @pl.when(pair >= 2)
+            def _():
+                pt_copy(pair - 2, 0, slot).wait()
+
+            value = scores(pair, 0)
+            top = jnp.max(value, 0, keepdims=True)
+            weight = jnp.exp(value - top)
+            inverse = 1.0 / jnp.sum(weight, 0, keepdims=True)
+            soft = (weight * inverse).astype(BF)
+            pt_stage[slot] = soft
+            pt_copy(pair, 0, slot).start()
+            mixed = tn(keys_of(pair, 0), soft)[HD:]
+        else:
+
+            def first(block, state):
+                top, total = state
+                value = scores(pair, block)
+                new = jnp.maximum(top, jnp.max(value, 0, keepdims=True))
+                total = total * jnp.exp(top - new) + jnp.sum(
+                    jnp.exp(value - new), 0, keepdims=True
+                )
+                return new, total
+
+            top, total = lax.fori_loop(
+                0,
+                blocks,
+                first,
+                (jnp.full((1, 512), NEGATIVE, F32), jnp.zeros((1, 512), F32)),
+            )
+            inverse = 1.0 / total
+
+            def second(block, mixed):
+                pt_stage[0] = (jnp.exp(scores(pair, block) - top) * inverse).astype(BF)
+                copy = pt_copy(pair, block, 0)
+                copy.start()
+                mixed = mixed + tn(keys_of(pair, block), pt_stage[0])[HD:]
+                copy.wait()
+                return mixed
+
+            mixed = lax.fori_loop(0, blocks, second, jnp.zeros((HD, 512), F32))
+        seq, head = pair // HK, pair % HK
+        for two in range(2):
+            both = jnp.concatenate(
+                [
+                    mixed[:, two * 256 : two * 256 + 128],
+                    mixed[:, two * 256 + 128 : two * 256 + 256],
+                ],
+                0,
+            )
+            tokens_ = pl.ds(pl.multiple_of(seq * 128, 128), 128)
+            cols = pl.ds(pl.multiple_of(head * 256 + two * 128, 128), 128)
+            out_attn_t[cols, tokens_] = both.astype(BF)
+            out_attn[tokens_, cols] = jnp.transpose(both).astype(BF)
+        return carry
+
+    for seq in range(2):
+        for k in range(1, line):
+            kv_copy(seq, k).wait()
+            kv_sib(seq, k).start()
+        if seq == 0:
+            o_gather.collect()
+        for k in range(line):
+            kv_sib(seq, k).wait()
+        lax.fori_loop(seq * HK, seq * HK + HK, attend, 0)
+    outs = [
+        pltpu.make_async_copy(wkv_all, out_wkv, out_sem.at[0]),
+        pltpu.make_async_copy(wq_all, out_wq, out_sem.at[1]),
+        pltpu.make_async_copy(kv_all, out_kv, out_sem.at[2]),
+    ]
+    for copy in outs:
+        copy.start()
+    o_gather.finish()
+    outs.append(pltpu.make_async_copy(wo_all, out_wo, out_sem.at[3]))
+    outs[3].start()
+    grad_gather.forward()
+
+    def project(tile, carry):
+        cols = pl.ds(pl.multiple_of(tile * 256, 256), 256)
+        out_mid[:, cols] = x_ref[:, cols].astype(F32) + nn(out_attn[...], wo_all[:, cols])
+        return carry
+
+    lax.fori_loop(0, width // 256, project, 0)
+    middle = out_mid[...]
+    scale_two = lax.rsqrt(jnp.mean(middle * middle, -1, keepdims=True) + EPSILON)
+    out_n2[...] = (middle * scale_two * out_gains[1:2, :]).astype(BF)
     if blocks == 1:
-        value = scores(0)
-        top = jnp.max(value, 0, keepdims=True)
-        weight = jnp.exp(value - top)
-        soft = (weight * (1.0 / jnp.sum(weight, 0, keepdims=True))).astype(BF)
-        pt_ref[0] = soft
-        mixed = tn(kv_ref[0], soft)[HD:]
-    else:
-
-        def first(block, carry):
-            top, total = carry
-            value = scores(block)
-            new = jnp.maximum(top, jnp.max(value, 0, keepdims=True))
-            total = total * jnp.exp(top - new) + jnp.sum(jnp.exp(value - new), 0, keepdims=True)
-            return new, total
-
-        top, total = lax.fori_loop(
-            0,
-            blocks,
-            first,
-            (jnp.full((1, 512), NEGATIVE, F32), jnp.zeros((1, 512), F32)),
-        )
-        inverse = 1.0 / total
-
-        def second(block, mixed):
-            soft = (jnp.exp(scores(block) - top) * inverse).astype(BF)
-            span = pl.ds(pl.multiple_of(block * 1024, 1024), 1024)
-            pt_ref[0, span, :] = soft
-            return mixed + tn(kv_ref[0, span, :], soft)[HD:]
-
-        mixed = lax.fori_loop(0, blocks, second, jnp.zeros((HD, 512), F32))
-    for two in range(2):
-        pair = jnp.concatenate(
-            [mixed[:, two * 256 : two * 256 + 128], mixed[:, two * 256 + 128 : two * 256 + 256]], 0
-        )
-        out_ref[:, two * 128 : two * 128 + 128] = jnp.transpose(pair).astype(BF)
-
-
-def attend_call(qp, kv, bias):
-    keys = kv.shape[1]
-    rows = 256
+        pt_copy(2 * HK - 2, 0, 0).wait()
+        pt_copy(2 * HK - 1, 0, 1).wait()
+    grad_gather.collect()
+    for gather in (kv_gather, q_gather, o_gather, grad_gather):
+        gather.settle()
+    for copy in outs:
+        copy.wait()
+
+
+def front_call(shards, line, keys, x, gains, wq, wkv, wo, grad, bias, cos, sin):
+    rows, width = x.shape
+    kv_width = wkv.shape[1]
+    dma = pltpu.SemaphoreType.DMA
+    v = pltpu.VMEM
+    vm = pl.BlockSpec(memory_space=pltpu.VMEM)
+    hbm = pl.BlockSpec(memory_space=pltpu.HBM)
+    part = width // shards
+    shape = jax.ShapeDtypeStruct
+    hops = max(5, shards)
     return pl.pallas_call(
-        attend_kernel,
-        grid=(2, HK),
+        lambda *refs: front_kernel((shards, line, keys, rows, width), *refs),
         out_shape=(
-            jax.ShapeDtypeStruct((2 * HK, keys, 512), BF),
-            jax.ShapeDtypeStruct((rows, HQ * HD), BF),
+            shape((rows, width), BF),
+            shape((width, rows), BF),
+            shape((width, rows), BF),
+            shape((2 * HK, 512, 128), BF),
+            shape((rows, width), F32),
+            shape((rows, width), BF),
+            shape((8, width), F32),
+            shape((width, width), BF),
+            shape((width, kv_width), BF),
+            shape((width, width), BF),
+            shape((2 * HK, 2 * line, 128, 128), BF),
+            shape((2 * HK, keys, 512), BF),
+            shape((shards * rows, width), BF),
         ),
-        in_specs=[
-            pl.BlockSpec((1, 512, 128), lambda m, h: (m * HK + h, 0, 0)),
-            pl.BlockSpec((1, keys, 128), lambda m, h: (m * HK + h, 0, 0)),
-            pl.BlockSpec((1, keys, 128), lambda m, h: (m, 0, 0)),
+        in_specs=[vm] * 9,
+        out_specs=(*[vm] * 7, *[hbm] * 6),
+        scratch_shapes=[
+            v((width, width), BF),
+            v((width, kv_width), BF),
+            v((width, width), BF),
+            v((2 * HK, 2 * line, 128, 128), BF),
+            v((rows, width), BF),
+            v((shards, 8, part), F32),
+            v((2, 1024, 512), BF),
+            dma((shards,)),
+            dma((shards,)),
+            *[dma((hops,)) for _ in range(12)],
+            dma((hops,)),
+            dma((hops,)),
+            dma((2, line)),
+            dma((2, line)),
+            dma((2, line)),
+            dma((2, line)),
+            dma((2,)),
+            dma((4,)),
         ],
-        out_specs=(
-            pl.BlockSpec((1, keys, 512), lambda m, h: (m * HK + h, 0, 0)),
-            pl.BlockSpec((128, 256), lambda m, h: (m, h)),
+        compiler_params=pltpu.CompilerParams(
+            collective_id=1, has_side_effects=True, vmem_limit_bytes=VMEM_LIMIT
         ),
-        compiler_params=pltpu.CompilerParams(vmem_limit_bytes=VMEM_LIMIT),
-        name="attend",
-    )(qp, kv, bias)
+        name="front",
+    )(x, gains, wq, wkv, wo, grad, bias, cos, sin)
 
 
 def rope_parts(places):
@@ -767,42 +1422,6 @@
     frequency = ROPE_BASE ** (-jnp.arange(half_dim, dtype=F32) * 2.0 / HD)
     angles = places.astype(F32)[..., None] * frequency
     return (jnp.cos(angles), jnp.sin(angles))
-
-
-def rotate_wide(values, cosine, sine, keys_only):
-    rows, cols = values.shape
-    tiles = values.reshape(rows, cols // 128, 128)
-    lane = jnp.arange(128)
-    left = jnp.roll(tiles, -32, 2)
-    right = jnp.roll(tiles, 32, 2)
-    swapped = jnp.where(lane % 64 < 32, left, right)
-    if keys_only:
-        cosine = jnp.where(lane < 64, cosine, 1.0)
-        sine = jnp.where(lane < 64, sine, 0.0)
-    return (tiles * cosine[:, None, :] + swapped * sine[:, None, :]).reshape(rows, cols)
-
-
-def row_norm(hidden, gain_vec):
-    inv_scale = lax.rsqrt(jnp.mean(hidden * hidden, -1, keepdims=True) + EPSILON)
-    return (hidden * inv_scale * gain_vec, inv_scale)
-
-
-def norm_back(grad_norm, hidden, inv_scale, gain_vec):
-    scaled = grad_norm * gain_vec
-    grad_gain = jnp.sum(grad_norm * hidden * inv_scale, 0)
-    grad_hidden = inv_scale * scaled - hidden * inv_scale**3 * jnp.mean(
-        scaled * hidden, -1, keepdims=True
-    )
-    return (grad_hidden, grad_gain)
-
-
-def gate_back(grad_inner, gate_proj, up_proj):
-    sigmoid_gate = jax.nn.sigmoid(gate_proj)
-    grad_gate = (
-        grad_inner * up_proj * sigmoid_gate * (1.0 + gate_proj * (1.0 - sigmoid_gate))
-    ).astype(BF)
-    grad_up = (grad_inner * gate_proj * sigmoid_gate).astype(BF)
-    return (grad_gate, grad_up)
 
 
 def per_device(
@@ -823,7 +1442,6 @@
     seqs, stretch, width = tokens.shape
     shards, line = lax.axis_size("shard"), lax.axis_size("line")
     rows = seqs * stretch
-    where_ctx = ("line", "core")
     rank = lax.axis_index("line") * 2 + lax.axis_index("core")
     places = lax.dynamic_slice_in_dim(positions, rank * stretch, stretch, 1)
     valid = (places < lengths[:, None]).astype(F32).reshape(rows, 1)
@@ -834,72 +1452,72 @@
         positions < lengths[:, None]
     )[:, :, None]
     bias = jnp.where(allowed, 0.0, NEGATIVE).astype(F32)
-    gains = lax.all_gather(jnp.stack([attn_gain, mlp_gain]), "shard", axis=1, tiled=True)
-    gain_one, gain_two = gains[0].astype(F32), gains[1].astype(F32)
     w_kv = jnp.stack(
         [w_key.reshape(-1, HK, HD), w_value.reshape(-1, HK, HD)], 2
     ).reshape(-1, 2 * HK * HD)
-    qkv_local = jnp.concatenate([w_query, w_kv], axis=1)
-    qkv_all = lax.all_gather(qkv_local, "shard", axis=0, tiled=True)
-    out_all = lax.all_gather(w_out, "shard", axis=0, tiled=True)
     grad_out = cotangent.reshape(rows, width).astype(F32) * valid
     grad_low = grad_out.astype(BF)
-    grad_low_all = lax.all_gather(grad_low, "shard", axis=0, tiled=True)
-    hidden = tokens.reshape(rows, width).astype(F32)
-    normed_one, inv_one = row_norm(hidden, gain_one)
-    norm_one = normed_one.astype(BF)
-    wq_all, wkv_all = qkv_all[:, :width], qkv_all[:, width:]
-    queries = rotate_wide(nn(norm_one, wq_all), cos_wide, sin_wide, False).astype(BF)
-    keyval = rotate_wide(nn(norm_one, wkv_all), cos_wide, sin_wide, True).astype(BF)
-    packed_q = jnp.transpose(
-        queries.reshape(seqs, stretch, HK, GROUP, HD), (0, 2, 3, 1, 4)
-    ).reshape(seqs * HK, GROUP * stretch, HD) * BF(1.0 / math.sqrt(HD))
-    packed_q = jnp.pad(packed_q, ((0, 0), (0, 0), (0, 128 - HD)))
-    packed_kv = jnp.transpose(keyval.reshape(seqs, stretch, HK, 128), (0, 2, 1, 3))
-    packed_kv = lax.all_gather(packed_kv, where_ctx, axis=2, tiled=True)
+    span = attn_gain.shape[0]
+    gains = jnp.concatenate(
+        [attn_gain[None].astype(F32), mlp_gain[None].astype(F32), jnp.zeros((6, span), F32)], 0
+    )
+    x = tokens.reshape(rows, width)
+    (
+        attn,
+        attn_t,
+        norm_t,
+        packed_q,
+        middle,
+        norm_two,
+        gains,
+        wq_all,
+        wkv_all,
+        out_all,
+        packed_kv,
+        soft,
+        grad_low_all,
+    ) = front_call(
+        shards,
+        line,
+        positions.shape[1],
+        x,
+        gains,
+        w_query,
+        w_kv,
+        w_out,
+        grad_low,
+        bias,
+        cos_wide,
+        sin_wide,
+    )
     packed_kv = packed_kv.reshape(seqs * HK, -1, 128)
-    soft, attn = attend_call(packed_q, packed_kv, bias)
-    middle = hidden + nn(attn, out_all)
-    normed_two, inv_two = row_norm(middle, gain_two)
-    norm_two = normed_two.astype(BF)
-    norm_two_all = lax.all_gather(norm_two, "shard", axis=0, tiled=True)
-    gate_proj = nn(norm_two_all, w_gate)
-    up_proj = nn(norm_two_all, w_up)
-    inner_act = (jax.nn.silu(gate_proj) * up_proj).astype(BF)
-    grad_inner = nt(grad_low_all, w_down)
-    grad_gate, grad_up = gate_back(grad_inner, gate_proj, up_proj)
-    grad_norm_two = lax.psum_scatter(
-        (nt(grad_gate, w_gate) + nt(grad_up, w_up)).astype(BF),
-        "shard",
-        scatter_dimension=0,
-        tiled=True,
-    ).astype(F32)
-    mlp_out = lax.psum_scatter(
-        nn(inner_act, w_down).astype(BF), "shard", scatter_dimension=0, tiled=True
-    ).astype(F32)
-    result = (middle + mlp_out).astype(BF).reshape(seqs, stretch, width)
-    feed_grads = jnp.stack(
-        [
-            tn(norm_two_all, grad_gate).astype(BF),
-            tn(norm_two_all, grad_up).astype(BF),
-            tn(grad_low_all, inner_act).astype(BF),
-        ]
+    gain_one, gain_two = gains[0:1], gains[1:2]
+    grad_middle, grad_gain_two, parts, feed_grads = feed_call(
+        shards,
+        norm_two,
+        middle,
+        grad_low,
+        gain_two,
+        grad_low_all.reshape(shards, rows, width),
+        w_gate,
+        w_up,
+        w_down,
     )
-    grad_mid_norm, grad_gain_two = norm_back(grad_norm_two, middle, inv_two, gain_two)
-    grad_middle = grad_out + grad_mid_norm
-    sum_feed, sum_out, sum_query, sum_kv, sum_gain, grad_input = backward_call(
+    sum_feed, sum_out, sum_query, sum_kv, sum_gain, grad_input, result, _ = backward_call(
         shards,
         line,
         grad_middle,
         attn,
-        attn.T,
+        attn_t,
         packed_q,
-        norm_one.T,
-        tokens.reshape(rows, width),
-        gain_one[None],
+        norm_t,
+        x,
+        gain_one,
         cos_wide,
         sin_wide,
-        grad_gain_two[None],
+        grad_gain_two,
+        middle,
+        parts,
         out_all,
         wq_all,
         wkv_all,
@@ -908,10 +1526,9 @@
         feed_grads,
     )
     sum_kv = sum_kv.reshape(-1, HK, 2, HD)
-    span = attn_gain.shape[0]
     sum_gain = lax.dynamic_slice_in_dim(sum_gain, lax.axis_index("shard") * span, span, 1)
     return (
-        result,
+        result.reshape(seqs, stretch, width),
         grad_input.reshape(seqs, stretch, width),
         sum_gain[0],
         sum_query.astype(F32),

time: 571 us -> 367 us (0.64); the launches traced: 561 us -> 365 us
  waiting for transfers between devices: 214 us -> 0 us
  Pallas kernels: 197 us -> 330 us
  matrix products: 55.9 us -> 0 us
  local copies, waits for them, and re-layouts: 37.5 us -> 14.1 us
  between operations: 15.1 us -> 0.79 us
  other arithmetic: 31.3 us -> 20.4 us
  blocking collectives: 9.57 us -> 0 us
    all_gather x5 -> x0, waiting for transfers between devices: 160 us -> none  [the longest x1 45.6 us: per_device(): qkv_all = lax.all_gather(qkv_local, 'shard', axis=0, tiled=True)]
    pallas_call x1 -> x2, Pallas kernels: 14.7 us -> 148 us  [the longest x1 84.5 us: front_call(): pl.pallas_call(lambda *refs: front_kernel((shards, line, keys, rows, widt...]
    dot_general x12 -> x0, matrix products: 55.9 us -> none  [the longest x6 26.9 us: nn(): lax.dot_general(a, b, (((1,), (0,)), ((), ())), preferred_element_type=F32)]
    reduce_scatter x2 -> x0, waiting for transfers between devices: 53.3 us -> none  [the longest x1 41 us: per_device(): lax.psum_scatter(nn(inner_act, w_down).astype(BF), 'shard', scatter_dimen...]
    all_gather x1 -> x0, blocking collectives: 9.57 us -> none  [per_device(): lax.all_gather(jnp.stack([attn_gain, mlp_gain]), 'shard', axis=1, tiled=T...]
    slice x6 -> x1, local copies, waits for them, and re-layouts: 7.29 us -> 1.46 us  [per_device(): gain_one, gain_two = (gains[0:1], gains[1:2])]
    unnamed x77 -> x25, local copies, waits for them, and re-layouts: 12.9 us -> 9.81 us
  transfers between devices with their start and end apart: 7 -> 0, of which waited for: 7 -> 0; matrix products, arithmetic and copies ran while one was open for 11% -> 0% of each run, Pallas kernels for 3% -> 0%
where the time goes in v3:
time: 367 us; the launch traced here: 365 us
  Pallas kernels  330 us (90%)
  other arithmetic  20.4 us (6%)
  local copies, waits for them, and re-layouts  14.1 us (4%)
    pallas_call x1, Pallas kernels, backward_call(): pl.pallas_call(lambda *refs: backward_kernel(sizes, *refs), out_shape=(ja...  182 us
    pallas_call x1, Pallas kernels, front_call(): pl.pallas_call(lambda *refs: front_kernel((shards, line, keys, rows, widt...  84.5 us
    pallas_call x1, Pallas kernels, feed_call(): pl.pallas_call(lambda *refs: feed_kernel((shards, rows, width, feed), *re...  63.2 us
    unnamed x25, local copies, waits for them, and re-layouts  9.81 us
    convert_element_type x1, other arithmetic, per_device(): sum_feed[2].T.astype(F32)  8.37 us

profile of v3, /device:TPU:0, one launch (start us, length us, event | category | flops | bytes accessed | tf_op | source)
XLA Modules:
  0.0 365.0 jit_solution(5279231139307003553)
XLA Ops:
  0.6 0.0 copy-start.5
  0.7 0.0 copy-start.6
  0.7 0.7 convert_bitcast_fusion.1
  1.4 0.5 fusion.1
  2.0 1.0 pad_maximum_fusion.1
  2.9 0.7 fusion.2
  3.7 2.1 fusion.refs_5_.refs_2_
  5.8 0.0 copy-start.7
  5.8 0.0 copy-start.8
  5.8 0.8 broadcast_compare_fusion
  6.6 2.7 and_select_fusion.refs_6_
  9.3 0.0 copy-done.5
  9.3 0.2 copy.35
  9.4 0.0 copy-done.6
  9.5 0.2 copy.36
  9.7 0.1 pad_maximum_fusion
  9.8 0.1 copy.37
  9.8 1.0 copy.39.refs_3_
  10.8 0.0 copy-done.7
  10.8 0.0 copy-done.8
  10.8 0.1 pad.12.clone
  10.9 0.7 maximum_maximum_fusion.refs_1_
  11.6 84.5 %front.1 = (bf16[256,1280]{1,0:T(8,128)(2,1)}, bf16[1280,256]{1,0:T(8,128)(2,1)}, bf16[1280,256]{1,0:T(8,128)(2,1)}, bf16[10,512,128]{2,1,0:T(8,128)(2,1)}, f32[...) custom-call(bf16[256,1280]{1,0:T(8,128)(2,1)} %bitcast.35, ...), custom_call_target="tpu_custom_call" | custom-call | tf_op jit(solution)/shard_map/front/pallas_call | solution.py:1374
  96.1 1.5 fusion.4
  97.6 63.2 %feed.1 = (f32[256,1280]{1,0:T(8,128)}, f32[1,1280]{1,0:T(1,128)}, bf16[4,256,1280]{2,1,0:T(8,128)(2,1)}, bf16[3,1280,896]{2,1,0:T(8,128)(2,1)}) custom-call(bf16[256,1280]{1,0:T(8,128)(2,1)} %get-tuple-element.35.refs_0_, f32[256,1280]{1,0:T(8,128)} %get-tuple-element.36.refs_1_.refs_10_, bf16[256,1280]{1,0:T(8,128)(2,1)} %fusion.refs_5_.refs_2_, ...), custom_call_target="tpu_custom_call" | custom-call | tf_op jit(solution)/shard_map/feed/pallas_call | solution.py:245
  160.8 182.0 %backward.1 = (bf16[3,1280,896]{2,1,0:T(8,128)(2,1)}, bf16[320,1280]{1,0:T(8,128)(2,1)}, bf16[320,1280]{1,0:T(8,128)(2,1)}, bf16[320,640]{1,0:T(8,128)(2,1)}, f3...) custom-call(f32[256,1280]{1,0:T(8,128)} %get-tuple-element.39.refs_0_, ...), custom_call_target="tpu_custom_call" | custom-call | tf_op jit(solution)/shard_map/backward/pallas_call | solution.py:949
  342.7 8.4 %convert_bitcast_fusion = (f32[896,1280]{0,1:T(8,128)}, f32[1280,896]{1,0:T(8,128)}, f32[1280,896]{1,0:T(8,128)}) fusion(bf16[3,1280,896]{2,1,0:T(8,128)(2,1)} %get-tuple-element.58), kind=kLoop, calls=%fused_computation | loop fusion | flops 3440640 | bytes 20643840 | tf_op jit(solution)/shard_map/convert_element_type | solution.py:1541
  351.1 0.0 copy-start.4
  351.1 5.7 %copy.43 = f32[896,1280]{1,0:T(8,128)} copy(f32[896,1280]{0,1:T(8,128)} %get-tuple-element.96) | data formatting | bytes 9175040
  356.8 0.0 copy-done.4
  356.8 0.0 copy-start.1
  356.8 0.3 copy.40
  357.1 0.1 fusion.3
  357.2 0.1 bitcast_convert_fusion.3
  357.2 0.0 copy-start
  357.2 1.0 copy.41
  358.2 0.1 bitcast_convert_fusion.2
  358.3 1.0 copy.42
  359.3 0.0 copy-start.3
  359.3 0.0 copy-done.1
  359.3 0.0 copy-start.2
  359.3 1.3 convert_element_type.80
  360.6 0.0 copy-done
  360.6 1.3 convert_element_type.85
  361.9 1.5 dynamic-slice_reduce_fusion
  363.3 0.0 copy-done.3
  363.3 0.8 copy.46
  364.2 0.0 copy-done.2
  364.2 0.8 copy.47
  (4 shorter events, 0.0 us)
Async XLA Ops:
  0.6 8.6 %copy-start.5 = (bf16[320,320]{1,0:T(8,128)(2,1)S(1)}, bf16[320,320]{1,0:T(8,128)(2,1)}, u32[]{:S(2)}) copy-start(bf16[320,320]{1,0:T(8,128)(2,1)} %param.19) | copy-start | bytes 614404
  0.7 8.8 %copy-start.6 = (bf16[320,320]{1,0:T(8,128)(2,1)S(1)}, bf16[320,320]{1,0:T(8,128)(2,1)}, u32[]{:S(2)}) copy-start(bf16[320,320]{1,0:T(8,128)(2,1)} %param.20) | copy-start | bytes 614404
  5.8 5.0 %copy-start.7 = (bf16[320]{0:T(512)(128)(2,1)S(1)}, bf16[320]{0:T(512)(128)(2,1)}, u32[]{:S(2)}) copy-start(bf16[320]{0:T(512)(128)(2,1)} %param.17) | copy-start | bytes 1924
  5.8 5.0 %copy-start.8 = (bf16[320]{0:T(512)(128)(2,1)S(1)}, bf16[320]{0:T(512)(128)(2,1)}, u32[]{:S(2)}) copy-start(bf16[320]{0:T(512)(128)(2,1)} %param.22) | copy-start | bytes 1924
  351.1 5.7 %copy-start.4 = (bf16[320,640]{1,0:T(8,128)(2,1)S(1)}, bf16[320,640]{1,0:T(8,128)(2,1)}, u32[]{:S(2)}) copy-start(bf16[320,640]{1,0:T(8,128)(2,1)} %get-tuple-element.56) | copy-start | bytes 1228804
  356.8 2.5 copy-start.1
  357.2 3.3 copy-start
  359.3 4.0 %copy-start.3 = (bf16[256,1280]{1,0:T(8,128)(2,1)S(1)}, bf16[256,1280]{1,0:T(8,128)(2,1)}, u32[]{:S(2)}) copy-start(bf16[256,1280]{1,0:T(8,128)(2,1)} %get-tuple-element.52) | copy-start | bytes 1966084
  359.3 4.9 %copy-start.2 = (bf16[256,1280]{1,0:T(8,128)(2,1)S(1)}, bf16[256,1280]{1,0:T(8,128)(2,1)}, u32[]{:S(2)}) copy-start(bf16[256,1280]{1,0:T(8,128)(2,1)} %get-tuple-element.53) | copy-start | bytes 1966084

commit v4 on v1

v4 whole, which is shorter than its diff:
```python
import math

import jax
import jax.numpy as jnp
from jax import lax
from jax.experimental import pallas as pl
from jax.experimental.pallas import tpu as pltpu
from jax.sharding import Mesh
from jax.sharding import PartitionSpec as P

HQ = 20
HK = 5
HD = 64
GROUP = HQ // HK
EPSILON = 1e-05
NEGATIVE = -1e30
ROPE_BASE = 10000.0
BF = jnp.bfloat16
F32 = jnp.float32
BY_MESH = pl.DeviceIdType.MESH
VMEM_LIMIT = 67043328


def nn(a, b):
    return lax.dot_general(a, b, (((1,), (0,)), ((), ())), preferred_element_type=F32)


def nt(a, b):
    return lax.dot_general(a, b, (((1,), (1,)), ((), ())), preferred_element_type=F32)


def tn(a, b):
    return lax.dot_general(a, b, (((0,), (0,)), ((), ())), preferred_element_type=F32)


def lanes_of(rows):
    return lax.broadcasted_iota(jnp.int32, (rows, 128), 1)


def swap_halves(block, lane):
    left = pltpu.roll(block, 96, 1)
    right = pltpu.roll(block, 32, 1)
    return jnp.where(lane % 64 < 32, left, right)


def peer_of(s_id, shards, k, back):
    if shards == 4:
        if isinstance(k, int):
            return [s_id, s_id + 1 - 2 * (s_id % 2), (s_id + 2) % 4, 3 - s_id][k]
        return jnp.where(
            k == 0,
            s_id,
            jnp.where(
                k == 1, s_id + 1 - 2 * (s_id % 2), jnp.where(k == 2, (s_id + 2) % 4, 3 - s_id)
            ),
        )
    return (s_id + (shards - k if back else k)) % shards


class Spread:
    def __init__(self, env, block, source, sems, shared):
        self.env, self.block, self.source, self.shared = env, block, source, shared
        self.send, self.recv, self.sib_send, self.sib_recv = sems
        self.relay = env.shards == 4

    def copy(self, k):
        env = self.env
        return env.remote(
            self.source,
            self.block(env.s_id, env.c_id, 0, 2),
            self.send.at[k],
            self.recv.at[k],
            env.peer(k),
        )

    def passing(self, k):
        env = self.env
        piece = self.block(env.origin(k), env.c_id, k - 1, 1)
        return env.remote(
            piece, piece, self.send.at[2 + k], self.recv.at[2 + k], env.peer(3 - k)
        )

    def direct(self):
        return range(1, 3 if self.relay else self.env.shards)

    def start(self):
        for k in self.direct():
            self.copy(k).start()

    def sib_copy(self, k):
        piece = self.block(self.env.origin(k), self.env.c_id, 0, 2)
        return self.env.remote(
            piece, piece, self.sib_send.at[k], self.sib_recv.at[k], self.env.sibling
        )

    def forward(self):
        for k in self.direct():
            self.copy(k).wait_recv()
            if self.relay:
                self.passing(k).start()
            if self.shared:
                self.sib_copy(k).start()

    def collect(self):
        if self.relay:
            for k in (1, 2):
                self.passing(k).wait_recv()
            if self.shared:
                self.sib_copy(3).start()

    def finish(self):
        if self.shared:
            for k in range(1, self.env.shards):
                self.sib_copy(k).wait_recv()

    def settle(self):
        for k in self.direct():
            self.copy(k).wait_send()
            if self.relay:
                self.passing(k).wait_send()
        if self.shared:
            for k in range(1, self.env.shards):
                self.sib_copy(k).wait_send()


class Env:
    def __init__(self, shards, line):
        self.shards, self.line = shards, line
        self.s_id = lax.axis_index("shard")
        self.l_id = lax.axis_index("line")
        self.c_id = lax.axis_index("core")
        self.sibling = (self.s_id, self.l_id, 1 - self.c_id)

    def remote(self, src, dst, send, recv, to):
        return pltpu.make_async_remote_copy(
            src, dst, send, recv, device_id=to, device_id_type=BY_MESH
        )

    def peer(self, k):
        return (peer_of(self.s_id, self.shards, k, False), self.l_id, self.c_id)

    def origin(self, k):
        return peer_of(self.s_id, self.shards, k, True)

    def mate(self, k):
        return (self.s_id, lax.rem(self.l_id + k, self.line), self.c_id)

    def barrier(self, others):
        barrier = pltpu.get_barrier_semaphore()
        for other in others:
            pl.semaphore_signal(barrier, inc=1, device_id=other, device_id_type=BY_MESH)
        pl.semaphore_wait(barrier, len(others))


def front_kernel(
    sizes,
    info_ref,
    keys_ref,
    freq_ref,
    gain_one_ref,
    gain_two_ref,
    x_hbm,
    g_hbm,
    wq_ref,
    wkv_ref,
    wo_ref,
    out_attn,
    out_attn_t,
    out_n1_t,
    out_qp,
    out_mid,
    out_n2,
    out_gains,
    cos_ref,
    sin_ref,
    out_wq,
    out_wkv,
    out_wo,
    out_kv,
    out_pt,
    out_g,
    wq_all,
    wkv_all,
    wo_all,
    kv_all,
    norm,
    x_ref,
    g_ref,
    bias_ref,
    gains_ref,
    gain_zone,
    pt_stage,
    gain_send,
    gain_recv,
    wq_s,
    wq_r,
    wq_ss,
    wq_sr,
    wkv_s,
    wkv_r,
    wkv_ss,
    wkv_sr,
    wo_s,
    wo_r,
    wo_ss,
    wo_sr,
    g_s,
    g_r,
    kv_send,
    kv_recv,
    kv_sib_send,
    kv_sib_recv,
    pt_sem,
    out_sem,
):
    shards, line, keys, rows, width = sizes
    env = Env(shards, line)
    s_id, l_id, c_id = env.s_id, env.l_id, env.c_id
    part = width // shards
    hp = part // 2
    quarter = hp // 2
    blocks = keys // 1024
    load_x = pltpu.make_async_copy(x_hbm, x_ref, out_sem.at[4])
    load_g = pltpu.make_async_copy(g_hbm, g_ref, out_sem.at[5])
    load_x.start()
    load_g.start()
    gains_ref[0:1, :] = gain_one_ref[...].astype(F32)
    gains_ref[1:2, :] = gain_two_ref[...].astype(F32)
    gains_ref[2:8, :] = jnp.zeros((6, part), F32)
    env.barrier(
        [env.sibling]
        + [env.peer(k) for k in range(1, shards)]
        + [env.mate(k) for k in range(1, line)]
    )

    def rows_of(ref):
        def block(s, core, first, count):
            start = s * part + core * hp + first * quarter
            return ref.at[pl.ds(pl.multiple_of(start, 16), count * quarter)]

        return block

    def g_rows(s, core, first, count):
        start = s * rows + first * (rows // 2)
        return out_g.at[pl.ds(pl.multiple_of(start, 16), count * (rows // 2))]

    mine = pl.ds(pl.multiple_of(c_id * hp, 16), hp)
    own = pl.ds(pl.multiple_of(s_id * part, 16), part)
    kv_gather = Spread(
        env, rows_of(wkv_all), wkv_ref.at[mine], (wkv_s, wkv_r, wkv_ss, wkv_sr), True
    )
    q_gather = Spread(env, rows_of(wq_all), wq_ref.at[mine], (wq_s, wq_r, wq_ss, wq_sr), True)
    o_gather = Spread(env, rows_of(wo_all), wo_ref.at[mine], (wo_s, wo_r, wo_ss, wo_sr), True)
    grad_gather = Spread(env, g_rows, g_ref, (g_s, g_r, None, None), False)

    def gain_copy(k):
        return env.remote(
            gains_ref, gain_zone.at[s_id], gain_send.at[k], gain_recv.at[k], env.peer(k)
        )

    for k in range(1, shards):
        gain_copy(k).start()
    kv_gather.start()
    locals_ = [
        pltpu.make_async_copy(wkv_ref, wkv_all.at[own], out_sem.at[0]),
        pltpu.make_async_copy(wq_ref, wq_all.at[own], out_sem.at[1]),
        pltpu.make_async_copy(wo_ref, wo_all.at[own], out_sem.at[2]),
    ]
    for copy in locals_:
        copy.start()
    gain_zone[s_id] = gains_ref[...]
    lane = lanes_of(128)
    info = jnp.transpose(info_ref[...])
    for seq in range(2):
        angle = info[:, seq : seq + 1] * freq_ref[...]
        cos_ref[seq * 128 : seq * 128 + 128, :] = jnp.cos(angle)
        sine = jnp.sin(angle)
        sin_ref[seq * 128 : seq * 128 + 128, :] = jnp.where(lane % 64 < 32, -sine, sine)
    load_x.wait()
    hidden = x_ref[...].astype(F32)
    scale = lax.rsqrt(jnp.mean(hidden * hidden, -1, keepdims=True) + EPSILON)
    for k in range(1, shards):
        gain_copy(k).wait()
    out_gains[...] = jnp.concatenate([gain_zone[s] for s in range(shards)], 1)
    norm[...] = (hidden * scale * out_gains[0:1, :]).astype(BF)
    kv_gather.forward()
    q_gather.start()
    for copy in locals_:
        copy.wait()
    kv_gather.collect()
    kv_gather.finish()

    place = l_id * 2 + c_id

    def make_kv(head, carry):
        block = nn(norm[...], wkv_all[:, pl.ds(pl.multiple_of(head * 128, 128), 128)])
        for seq in range(2):
            piece = block[seq * 128 : seq * 128 + 128]
            cos = jnp.where(lane < 64, cos_ref[pl.ds(seq * 128, 128), :], 1.0)
            sin = jnp.where(lane < 64, sin_ref[pl.ds(seq * 128, 128), :], 0.0)
            kv_all[seq * HK + head, place] = (piece * cos + swap_halves(piece, lane) * sin).astype(
                BF
            )
        return carry

    lax.fori_loop(0, HK, make_kv, 0)

    def kv_slice(seq, l, c):
        return kv_all.at[pl.ds(seq * HK, HK), l * 2 + c]

    def kv_move(seq, way, src):
        piece = kv_slice(seq, src, c_id)
        to = (s_id, lax.rem(l_id + (1 if way == 0 else line - 1), line), c_id)
        return env.remote(
            piece, piece, kv_send.at[seq, way * line + src], kv_recv.at[seq, src], to
        )

    def kv_sib(seq, src):
        piece = kv_slice(seq, src, c_id)
        return env.remote(
            piece, piece, kv_sib_send.at[seq, src], kv_sib_recv.at[seq, src], env.sibling
        )

    def kv_onward(seq, way, src):
        @pl.when((l_id < line - 1) if way == 0 else (l_id > 0))
        def _():
            kv_move(seq, way, src).start()

    def kv_start(seq):
        for way in range(2):
            kv_onward(seq, way, l_id)
        kv_sib(seq, l_id).start()

    def kv_step(seq, far):
        for way in range(2):
            src = l_id - far if way == 0 else l_id + far

            @pl.when((src >= 0) & (src < line))
            def _():
                kv_move(seq, way, src).wait_recv()
                kv_onward(seq, way, src)
                kv_sib(seq, src).start()

    def kv_finish(seq):
        for src in range(line):
            kv_sib(seq, src).wait()

    def kv_settle(seq):
        for src in range(line):

            @pl.when((l_id < line - 1) & (src <= l_id))
            def _():
                kv_move(seq, 0, src).wait_send()

            @pl.when((l_id > 0) & (src >= l_id))
            def _():
                kv_move(seq, 1, src).wait_send()

    kv_start(0)
    load_g.wait()
    for seq in range(2):
        rows_ = pl.ds(seq * 128, 128)
        g_ref[rows_, :] = (g_ref[rows_, :].astype(F32) * info[:, 2 + seq : 3 + seq]).astype(BF)
        key_at = jnp.transpose(keys_ref[seq])
        for tile in range(keys // 128):
            bias_ref[seq, tile * 128 : tile * 128 + 128, :] = jnp.where(
                key_at[:, tile : tile + 1] <= info_ref[seq : seq + 1, :], 0.0, NEGATIVE
            )
    keep_g = pltpu.make_async_copy(
        g_ref, out_g.at[pl.ds(pl.multiple_of(s_id * rows, 16), rows)], out_sem.at[4]
    )
    keep_g.start()
    for tile in range(width // 128):
        piece = norm[:, tile * 128 : tile * 128 + 128].astype(F32)
        out_n1_t[tile * 128 : tile * 128 + 128, :] = jnp.transpose(piece).astype(BF)
    q_gather.forward()
    o_gather.start()
    kv_step(0, 1)
    if line == 2:
        kv_start(1)
    else:
        kv_step(0, 2)
        kv_start(1)
    q_gather.collect()
    q_gather.finish()

    def make_q(head, carry):
        block = nn(norm[...], wq_all[:, pl.ds(pl.multiple_of(head * 256, 256), 256)])
        for seq in range(2):
            cos = cos_ref[pl.ds(seq * 128, 128), :]
            sin = sin_ref[pl.ds(seq * 128, 128), :]
            for two in range(2):
                piece = block[seq * 128 : seq * 128 + 128, two * 128 : two * 128 + 128]
                piece = piece * cos + swap_halves(piece, lane) * sin
                piece = piece.astype(BF).astype(F32) * (1.0 / math.sqrt(HD))
                pair = seq * HK + head
                out_qp[pair, pl.ds(two * 256, 128), :] = jnp.where(lane < 64, piece, 0.0).astype(
                    BF
                )
                out_qp[pair, pl.ds(two * 256 + 128, 128), :] = jnp.where(
                    lane < 64, pltpu.roll(piece, 64, 1), 0.0
                ).astype(BF)
        return carry

    lax.fori_loop(0, HK, make_q, 0)

    def pt_copy(pair, block, slot):
        span = pl.ds(pl.multiple_of(block * 1024, 1024), 1024)
        return pltpu.make_async_copy(pt_stage.at[slot], out_pt.at[pair, span], pt_sem.at[slot])

    def keys_of(pair, block):
        if blocks == 1:
            return kv_all[pair].reshape(1024, 128)
        return kv_all[pair, pl.ds(block * 8, 8)].reshape(1024, 128)

    def scores(pair, block):
        span = pl.ds(pl.multiple_of(block * 1024, 1024), 1024)
        bias = bias_ref[pair // HK, span, :]
        return nt(keys_of(pair, block), out_qp[pair]) + jnp.concatenate([bias] * GROUP, 1)

    def attend(pair, carry):
        if blocks == 1:
            slot = lax.rem(pair, 2)

            @pl.when(pair >= 2)
            def _():
                pt_copy(pair - 2, 0, slot).wait()

            value = scores(pair, 0)
            top = jnp.max(value, 0, keepdims=True)
            weight = jnp.exp(value - top)
            inverse = 1.0 / jnp.sum(weight, 0, keepdims=True)
            soft = (weight * inverse).astype(BF)
            pt_stage[slot] = soft
            pt_copy(pair, 0, slot).start()
            mixed = tn(keys_of(pair, 0), soft)[HD:]
        else:

            def first(block, state):
                top, total = state
                value = scores(pair, block)
                new = jnp.maximum(top, jnp.max(value, 0, keepdims=True))
                total = total * jnp.exp(top - new) + jnp.sum(
                    jnp.exp(value - new), 0, keepdims=True
                )
                return new, total

            top, total = lax.fori_loop(
                0,
                blocks,
                first,
                (jnp.full((1, 512), NEGATIVE, F32), jnp.zeros((1, 512), F32)),
            )
            inverse = 1.0 / total

            def second(block, mixed):
                pt_stage[0] = (jnp.exp(scores(pair, block) - top) * inverse).astype(BF)
                copy = pt_copy(pair, block, 0)
                copy.start()
                mixed = mixed + tn(keys_of(pair, block), pt_stage[0])[HD:]
                copy.wait()
                return mixed

            mixed = lax.fori_loop(0, blocks, second, jnp.zeros((HD, 512), F32))
        seq, head = pair // HK, pair % HK
        for two in range(2):
            both = jnp.concatenate(
                [
                    mixed[:, two * 256 : two * 256 + 128],
                    mixed[:, two * 256 + 128 : two * 256 + 256],
                ],
                0,
            )
            tokens_ = pl.ds(pl.multiple_of(seq * 128, 128), 128)
            cols = pl.ds(pl.multiple_of(head * 256 + two * 128, 128), 128)
            out_attn_t[cols, tokens_] = both.astype(BF)
            out_attn[tokens_, cols] = jnp.transpose(both).astype(BF)
        return carry

    for far in range(3, line):
        kv_step(0, far)
    o_gather.forward()
    grad_gather.start()
    kv_step(1, 1)
    kv_finish(0)
    lax.fori_loop(0, 2, attend, 0)
    if line > 2:
        kv_step(1, 2)
    lax.fori_loop(2, HK, attend, 0)
    for far in range(3, line):
        kv_step(1, far)
    o_gather.collect()
    kv_finish(1)
    lax.fori_loop(HK, 2 * HK - 2, attend, 0)
    grad_gather.forward()
    lax.fori_loop(2 * HK - 2, 2 * HK, attend, 0)
    outs = [
        pltpu.make_async_copy(wkv_all, out_wkv, out_sem.at[0]),
        pltpu.make_async_copy(wq_all, out_wq, out_sem.at[1]),
        pltpu.make_async_copy(kv_all, out_kv, out_sem.at[2]),
    ]
    for copy in outs:
        copy.start()
    o_gather.finish()
    outs.append(pltpu.make_async_copy(wo_all, out_wo, out_sem.at[3]))
    outs[3].start()

    def project(tile, carry):
        cols = pl.ds(pl.multiple_of(tile * 256, 256), 256)
        out_mid[:, cols] = x_ref[:, cols].astype(F32) + nn(out_attn[...], wo_all[:, cols])
        return carry

    lax.fori_loop(0, width // 256, project, 0)
    middle = out_mid[...]
    scale_two = lax.rsqrt(jnp.mean(middle * middle, -1, keepdims=True) + EPSILON)
    out_n2[...] = (middle * scale_two * out_gains[1:2, :]).astype(BF)
    if blocks == 1:
        pt_copy(2 * HK - 2, 0, 0).wait()
        pt_copy(2 * HK - 1, 0, 1).wait()
    grad_gather.collect()
    for gather in (kv_gather, q_gather, o_gather, grad_gather):
        gather.settle()
    kv_settle(0)
    kv_settle(1)
    keep_g.wait()
    for copy in outs:
        copy.wait()


def front_call(shards, line, *arrays):
    info, keys_at, x, wkv = arrays[0], arrays[1], arrays[5], arrays[8]
    rows, width = x.shape
    keys = keys_at.shape[1] * 128
    kv_width = wkv.shape[1]
    dma = pltpu.SemaphoreType.DMA
    v = pltpu.VMEM
    vm = pl.BlockSpec(memory_space=pltpu.VMEM)
    hbm = pl.BlockSpec(memory_space=pltpu.HBM)
    part = width // shards
    shape = jax.ShapeDtypeStruct
    hops = max(5, shards)
    return pl.pallas_call(
        lambda *refs: front_kernel((shards, line, keys, rows, width), *refs),
        out_shape=(
            shape((rows, width), BF),
            shape((width, rows), BF),
            shape((width, rows), BF),
            shape((2 * HK, 512, 128), BF),
            shape((rows, width), F32),
            shape((rows, width), BF),
            shape((8, width), F32),
            shape((rows, 128), F32),
            shape((rows, 128), F32),
            shape((width, width), BF),
            shape((width, kv_width), BF),
            shape((width, width), BF),
            shape((2 * HK, 2 * line, 128, 128), BF),
            shape((2 * HK, keys, 512), BF),
            shape((shards * rows, width), BF),
        ),
        in_specs=[vm] * 5 + [hbm] * 5,
        out_specs=(*[vm] * 9, *[hbm] * 6),
        scratch_shapes=[
            v((width, width), BF),
            v((width, kv_width), BF),
            v((width, width), BF),
            v((2 * HK, 2 * line, 128, 128), BF),
            v((rows, width), BF),
            v((rows, width), BF),
            v((rows, width), BF),
            v((2, keys, 128), F32),
            v((8, part), F32),
            v((shards, 8, part), F32),
            v((2, 1024, 512), BF),
            dma((shards,)),
            dma((shards,)),
            *[dma((hops,)) for _ in range(12)],
            dma((hops,)),
            dma((hops,)),
            dma((2, 2 * line)),
            dma((2, line)),
            dma((2, line)),
            dma((2, line)),
            dma((2,)),
            dma((6,)),
        ],
        compiler_params=pltpu.CompilerParams(
            collective_id=1, has_side_effects=True, vmem_limit_bytes=VMEM_LIMIT
        ),
        name="front",
    )(*arrays)


def feed_kernel(
    sizes,
    n2_ref,
    g_hbm,
    wg_hbm,
    wu_hbm,
    wd_hbm,
    out_parts,
    out_back,
    out_n2_t,
    out_inner_t,
    out_dgate,
    out_dup,
    n2_all,
    g_all,
    wg,
    wu,
    wd,
    inner,
    dgate,
    dup,
    stage,
    part_stage,
    n2_t,
    inner_t,
    load_sem,
    n2_send,
    n2_recv,
    part_sem,
    back_sem,
    out_sem,
):
    shards, rows, width, feed = sizes
    env = Env(shards, 1)
    s_id = env.s_id
    env.barrier([env.peer(k) for k in range(1, shards)])

    def n2_rows(s, core, first, count):
        return n2_all.at[s, pl.ds(first * (rows // 2), count * (rows // 2))]

    gather = Spread(env, n2_rows, n2_ref, (n2_send, n2_recv, None, None), False)
    gather.start()
    loads = [
        pltpu.make_async_copy(src, dst, load_sem.at[i])
        for i, (src, dst) in enumerate(
            ((wg_hbm, wg), (wu_hbm, wu), (g_hbm, g_all), (wd_hbm, wd))
        )
    ]
    for load in loads:
        load.start()
    n2_all[s_id] = n2_ref[...]
    loads[0].wait()
    loads[1].wait()

    def back_copy(k, slot):
        return pltpu.make_async_copy(
            stage.at[slot], out_back.at[peer_of(s_id, shards, k, True)], back_sem.at[slot]
        )

    def part_copy(k, slot):
        return pltpu.make_async_copy(
            part_stage.at[slot], out_parts.at[peer_of(s_id, shards, k, True)], part_sem.at[slot]
        )

    def outs(k):
        source = peer_of(s_id, shards, k, True)
        cols = pl.ds(pl.multiple_of(source * rows, 128), rows)
        return [
            pltpu.make_async_copy(n2_t.at[k], out_n2_t.at[:, cols], out_sem.at[k, 0]),
            pltpu.make_async_copy(inner_t.at[k], out_inner_t.at[:, cols], out_sem.at[k, 1]),
            pltpu.make_async_copy(dgate.at[source], out_dgate.at[source], out_sem.at[k, 2]),
            pltpu.make_async_copy(dup.at[source], out_dup.at[source], out_sem.at[k, 3]),
        ]

    def project(k):
        slot = lax.rem(k, 2)

        @pl.when(k >= 2)
        def _():
            part_copy(k - 2, slot).wait()

        part_stage[slot] = nn(inner[peer_of(s_id, shards, k, True)], wd[...]).astype(BF)
        part_copy(k, slot).start()

    def block(k, carry):
        source = peer_of(s_id, shards, k, True)
        slot = lax.rem(k, 2)
        if gather.relay:

            @pl.when(k == 1)
            def _():
                gather.forward()

            @pl.when(k == 3)
            def _():
                gather.passing(1).wait_recv()
                gather.passing(2).wait_recv()

        else:

            @pl.when(k > 0)
            def _():
                gather.copy(k).wait_recv()

        normed = n2_all[source]
        gate, upper = nn(normed, wg[...]), nn(normed, wu[...])

        @pl.when(k == 0)
        def _():
            loads[2].wait()
            loads[3].wait()

        grad = g_all[source]
        grad_inner = nt(grad, wd[...])
        sig = 1.0 / (1.0 + jnp.exp(-gate))
        act = gate * sig
        inner[source] = (act * upper).astype(BF)
        dgate[source] = (grad_inner * upper * sig * (1.0 + gate * (1.0 - sig))).astype(BF)
        dup[source] = (grad_inner * act).astype(BF)

        @pl.when(k >= 2)
        def _():
            back_copy(k - 2, slot).wait()

        stage[slot] = (nt(dgate[source], wg[...]) + nt(dup[source], wu[...])).astype(BF)
        back_copy(k, slot).start()
        n2_t[k] = jnp.transpose(normed)
        inner_t[k] = jnp.transpose(inner[source])
        for copy in outs(k):
            copy.start()

        @pl.when(k > 0)
        def _():
            project(k - 1)

        return carry

    lax.fori_loop(0, shards, block, 0)
    project(shards - 1)
    for k in range(shards):
        for copy in outs(k):
            copy.wait()
    gather.settle()
    for last in (2, 1):
        part_copy(shards - last, (shards - last) % 2).wait()
        back_copy(shards - last, (shards - last) % 2).wait()


def feed_call(shards, n2, grad_all, w_gate, w_up, w_down):
    rows, width = n2.shape
    feed = w_gate.shape[1]
    dma = pltpu.SemaphoreType.DMA
    v = pltpu.VMEM
    vm = pl.BlockSpec(memory_space=pltpu.VMEM)
    hbm = pl.BlockSpec(memory_space=pltpu.HBM)
    shape = jax.ShapeDtypeStruct
    hops = max(5, shards)
    return pl.pallas_call(
        lambda *refs: feed_kernel((shards, rows, width, feed), *refs),
        out_shape=(
            shape((shards, rows, width), BF),
            shape((shards, rows, width), BF),
            shape((width, shards * rows), BF),
            shape((feed, shards * rows), BF),
            shape((shards, rows, feed), BF),
            shape((shards, rows, feed), BF),
        ),
        in_specs=[vm] + [hbm] * 4,
        out_specs=tuple([hbm] * 6),
        scratch_shapes=[
            v((shards, rows, width), BF),
            v((shards, rows, width), BF),
            v((width, feed), BF),
            v((width, feed), BF),
            v((feed, width), BF),
            v((shards, rows, feed), BF),
            v((shards, rows, feed), BF),
            v((shards, rows, feed), BF),
            v((2, rows, width), BF),
            v((2, rows, width), BF),
            v((shards, width, rows), BF),
            v((shards, feed, rows), BF),
            dma((4,)),
            dma((hops,)),
            dma((hops,)),
            dma((2,)),
            dma((2,)),
            dma((shards, 4)),
        ],
        compiler_params=pltpu.CompilerParams(
            collective_id=2, has_side_effects=True, vmem_limit_bytes=VMEM_LIMIT
        ),
        name="feed",
    )(n2, grad_all, w_gate, w_up, w_down)


def add_rows(target, parts, rows, step):
    def body(index, carry):
        span = pl.ds(pl.multiple_of(index * step, step), step)
        total = parts[0][span, :].astype(F32)
        for part in parts[1:]:
            total = total + part[span, :].astype(F32)
        target[span, :] = total.astype(target.dtype)
        return carry

    lax.fori_loop(0, rows // step, body, 0)


def backward_kernel(
    sizes,
    gains_ref,
    cos_ref,
    sin_ref,
    attn_hbm,
    attn_t_hbm,
    qp_hbm,
    n1_t_hbm,
    x_hbm,
    mid_hbm,
    parts_hbm,
    back_hbm,
    n2_t_hbm,
    g_hbm,
    inner_t_hbm,
    dgate_hbm,
    dup_hbm,
    wo_hbm,
    wq_hbm,
    wkv_hbm,
    pt_hbm,
    kv_hbm,
    out_gate,
    out_up,
    out_dn,
    out_wo,
    out_wq,
    out_wkv,
    out_gain,
    out_dx,
    out_result,
    p_zone,
    b_zone,
    w_buf,
    gm,
    mid_ref,
    dkv_x,
    dkv_z,
    own_gu,
    got_gu_x,
    got_gu_r,
    got_gu_t,
    own_dn,
    got_dn_x,
    got_dn_r,
    got_dn_t,
    o_x,
    o_z,
    o_r,
    o_t,
    q_x,
    q_z,
    q_r,
    q_t,
    k_x,
    k_z,
    k_r,
    k_t,
    gn_own,
    gn_x,
    gn_z,
    gn_r,
    gn_t,
    load_sem,
    pt_sem,
    kv_sem,
    core_sem,
    up_send,
    r_recv,
    t_recv,
    down_send,
    sib_send,
    sib_recv,
    local_sem,
    dkv_core,
    dkv_send,
    dkv_recv,
    g_core,
    g_send,
    g_recv,
    a_up,
    a_r,
    a_t,
    a_down,
    a_sib_send,
    a_sib_recv,
    a_local,
    p_send,
    p_recv,
    b_send,
    b_recv,
    late_sem,
):
    shards, line, keys, rows, width, feed = sizes
    env = Env(shards, line)
    s_id, l_id, c_id = env.s_id, env.l_id, env.c_id
    sibling, remote = env.sibling, env.remote
    toward = jnp.where(l_id < line // 2, 1, -1)
    inner_to = (s_id, l_id + toward, c_id)
    has_outer = (l_id > 0) & (l_id < line - 1)
    is_mid = (l_id == line // 2 - 1) | (l_id == line // 2)
    outer_to = (s_id, jnp.where(has_outer, l_id - toward, l_id + toward), c_id)
    peers = [env.peer(k) for k in range(1, shards)]
    mates = [env.mate(k) for k in range(1, line)]
    env.barrier([sibling] + peers + mates)

    half = width // 2
    chunks = 12
    slab = 16
    part = width // shards
    own_rows = part // 2
    blocks = keys // 1024
    tokens = shards * rows
    hops = line == 4
    near_half = pl.ds(pl.multiple_of(c_id * half, 128), half)
    far_half = pl.ds(pl.multiple_of((1 - c_id) * half, 128), half)

    def back_copy(k):
        return remote(
            back_hbm.at[peer_of(s_id, shards, k, False)],
            b_zone.at[k - 1],
            b_send.at[k - 1],
            b_recv.at[k - 1],
            peers[k - 1],
        )

    def part_copy(k):
        return remote(
            parts_hbm.at[peer_of(s_id, shards, k, False)],
            p_zone.at[k - 1],
            p_send.at[k - 1],
            p_recv.at[k - 1],
            peers[k - 1],
        )

    for k in range(1, shards):
        back_copy(k).start()

    def local(src, dst, sem):
        return pltpu.make_async_copy(src, dst, sem)

    def views(index, where):
        if where != "dn":
            rows_ = half // 4
            array, piece = (0 if where == "gate" else 1), index % 4
            array_of = out_gate if where == "gate" else out_up
            span = pl.ds(pl.multiple_of(piece * rows_, 16), rows_)
            bufs = [ref.at[array, span] for ref in (own_gu, got_gu_x, got_gu_r, got_gu_t)]

            def out(core):
                start = core * half + piece * rows_
                return array_of.at[pl.ds(pl.multiple_of(start, 16), rows_)]

            return rows_, bufs, out
        rows_ = feed // 4
        span = pl.ds(pl.multiple_of((index - 8) * rows_, 16), rows_)
        bufs = [ref.at[span] for ref in (own_dn, got_dn_x, got_dn_r, got_dn_t)]

        def out(core):
            return out_dn.at[span, pl.ds(pl.multiple_of(core * half, 128), half)]

        return rows_, bufs, out

    def split(action):
        def run(index):
            if isinstance(index, int):
                if 0 <= index < chunks:
                    action(index, ("gate", "up", "dn")[index // 4])
                return
            for number, where in enumerate(("gate", "up", "dn")):

                @pl.when(index // 4 == number)
                def _():
                    action(index, where)

        return run

    def up_end(index, where):
        count, (mine, extra, came, total), _ = views(index, where)
        add_rows(mine, [mine, extra], count, slab)
        send_up(index, mine, came, total)

    def up_inner(index, where):
        count, (mine, extra, came, total), _ = views(index, where)
        remote(mine, came, up_send.at[index], r_recv.at[index], inner_to).wait_recv()
        add_rows(mine, [mine, extra, came], count, slab)
        send_up(index, mine, came, total)

    def send_up(index, mine, came, total):
        @pl.when(is_mid)
        def _():
            remote(mine, total, up_send.at[index], t_recv.at[index], inner_to).start()

        @pl.when(jnp.logical_not(is_mid))
        def _():
            remote(mine, came, up_send.at[index], r_recv.at[index], inner_to).start()

    def down(index, where):
        count, (mine, _, _, total), out = views(index, where)
        remote(mine, total, up_send.at[index], t_recv.at[index], inner_to).wait_recv()

        @pl.when(is_mid)
        def _():
            add_rows(total, [mine, total], count, slab)

        @pl.when(has_outer)
        def _():
            remote(total, total, down_send.at[index], t_recv.at[index], outer_to).start()

        remote(total, out(c_id), sib_send.at[index], sib_recv.at[index], sibling).start()
        local(total, out(c_id), local_sem.at[index]).start()

    def settle(index, where):
        _, (mine, _, _, total), out = views(index, where)
        remote(mine, total, up_send.at[index], t_recv.at[index], inner_to).wait_send()

        @pl.when(has_outer)
        def _():
            remote(total, total, down_send.at[index], t_recv.at[index], outer_to).wait_send()

        remote(total, out(1 - c_id), sib_send.at[index], sib_recv.at[index], sibling).wait()
        local(total, out(c_id), local_sem.at[index]).wait()

    up_end, up_inner, down, settle = [split(f) for f in (up_end, up_inner, down, settle)]

    def ends_up(first, last):
        @pl.when(jnp.logical_not(has_outer))
        def _():
            for index in range(first, last):
                up_end(index)

    def ring(step, lag=2):
        @pl.when((step < chunks) & has_outer)
        def _():
            up_inner(step)

        @pl.when((step >= lag) & (step < chunks + lag) & is_mid)
        def _():
            down(step - lag)

    def ring_down(index):
        @pl.when(is_mid)
        def _():
            down(index)

    def ends_down(first, last):
        @pl.when(jnp.logical_not(is_mid))
        def _():
            for index in range(first, last):
                down(index)

    def core_send(array, src):
        dst = got_gu_x.at[array] if array < 2 else got_dn_x
        return remote(src, dst, core_sem.at[array], core_sem.at[3 + array], sibling)

    load_wo = local(wo_hbm, w_buf, late_sem.at[3])

    load_mid = local(mid_hbm, mid_ref, late_sem.at[0])

    def feed_grads(g_v, g_own, dgate_v, dup_v, wide_t, near_t, inner_t, far_gu, far_dn):
        loads = [
            local(src, dst, load_sem.at[i])
            for i, (src, dst) in enumerate(
                (
                    (n2_t_hbm.at[far_half], wide_t),
                    (dgate_hbm, dgate_v),
                    (dup_hbm, dup_v),
                    (inner_t_hbm, inner_t),
                    (g_hbm, g_v),
                )
            )
        ]
        load_near = local(n2_t_hbm.at[near_half], near_t, late_sem.at[1])
        load_own = local(g_hbm.at[s_id], g_own, late_sem.at[2])
        loads[0].start()
        loads[1].start()
        load_near.start()
        for load in loads[2:]:
            load.start()
        load_own.start()
        load_mid.start()
        load_wo.start()

        def flat(ref):
            return ref[...].reshape(tokens, ref.shape[2])

        loads[0].wait()
        loads[1].wait()
        far_gu[0] = nn(wide_t[...], flat(dgate_v)).astype(BF)
        core_send(0, far_gu.at[0]).start()
        load_near.wait()
        own_gu[0] = nn(near_t[...], flat(dgate_v)).astype(BF)
        core_send(0, far_gu.at[0]).wait()
        ends_up(0, 4)
        loads[2].wait()
        far_gu[1] = nn(wide_t[...], flat(dup_v)).astype(BF)
        core_send(1, far_gu.at[1]).start()
        own_gu[1] = nn(near_t[...], flat(dup_v)).astype(BF)
        core_send(1, far_gu.at[1]).wait()
        ends_up(4, 7)
        loads[3].wait()
        loads[4].wait()
        far_dn[...] = nn(inner_t[...], g_v[:, :, far_half].reshape(tokens, half)).astype(BF)
        core_send(2, far_dn).start()
        own_dn[...] = nn(inner_t[...], g_v[:, :, near_half].reshape(tokens, half)).astype(BF)
        ring(0)
        core_send(2, far_dn).wait()
        ring(1)
        own_back = local(back_hbm.at[s_id], g_v.at[0], load_sem.at[shards - 1])
        own_back.start()
        stage = []
        for k in range(1, shards):
            back_copy(k).wait()
            stage.append(local(b_zone.at[k - 1], g_v.at[k], load_sem.at[k - 1]))
            stage[-1].start()
        own_back.wait()
        total = g_v[0].astype(F32)
        for k in range(1, shards):
            stage[k - 1].wait()
            total = total + g_v[k].astype(F32)
        load_mid.wait()
        load_own.wait()
        hidden = mid_ref[...]
        scale = lax.rsqrt(jnp.mean(hidden * hidden, -1, keepdims=True) + EPSILON)
        scaled = total * gains_ref[1:2, :]
        gn_own[1:2, :] = jnp.sum(total * hidden * scale, 0, keepdims=True)
        gm[...] = (
            g_own[...].astype(F32)
            + scale * scaled
            - hidden * (scale * scale * scale) * jnp.mean(scaled * hidden, -1, keepdims=True)
        )

    v = pltpu.VMEM
    pl.run_scoped(
        feed_grads,
        v((shards, rows, width), BF),
        v((rows, width), BF),
        v((shards, rows, feed), BF),
        v((shards, rows, feed), BF),
        v((half, tokens), BF),
        v((half, tokens), BF),
        v((feed, tokens), BF),
        v((2, half, feed), BF),
        v((feed, half), BF),
    )

    def attention(
        wkv_buf,
        pt_buf,
        kv_buf,
        dproj,
        dop,
        delta,
        dkv,
        dq,
        dkv_own,
        g_buf,
        attn_ref,
        attn_t_ref,
        qp_ref,
        n1_t_ref,
        x_ref,
    ):
        load_wkv = local(wkv_hbm, wkv_buf, late_sem.at[0])
        load_wq = local(wq_hbm, w_buf, late_sem.at[3])
        early = [
            local(src, dst, late_sem.at[4 + i])
            for i, (src, dst) in enumerate(
                (
                    (attn_hbm, attn_ref),
                    (attn_t_hbm, attn_t_ref),
                    (qp_hbm, qp_ref),
                    (n1_t_hbm, n1_t_ref),
                    (x_hbm, x_ref),
                )
            )
        ]
        for load in early:
            load.start()
        load_wkv.start()
        total_steps = 2 * HK * blocks

        def pt_copy(step, slot):
            pair, block = step // blocks, step % blocks
            span = pl.ds(pl.multiple_of(block * 1024, 1024), 1024)
            return local(pt_hbm.at[pair, span], pt_buf.at[slot], pt_sem.at[slot])

        def kv_copy(step, slot):
            pair, block = step // blocks, step % blocks
            span = pl.ds(pl.multiple_of(block * 1024, 1024), 1024)
            return local(kv_hbm.at[pair, span], kv_buf.at[slot], kv_sem.at[slot])

        pt_copy(0, 0).start()
        kv_copy(0, 0).start()

        def core_part(grad, box, slot):
            far = pl.ds(pl.multiple_of((1 - c_id) * own_rows, 16), own_rows)
            return remote(grad.at[:, far, :], box, g_core.at[slot], g_core.at[3 + slot], sibling)

        def scatter_part(grad, box, zone, slot):
            core_part(grad, box, slot).wait()
            near = pl.ds(pl.multiple_of(c_id * own_rows, 16), own_rows)

            def body(s, carry):
                add_rows(box.at[s], [grad.at[s, near], box.at[s]], own_rows, slab)
                return carry

            lax.fori_loop(0, shards, body, 0)
            for k in range(1, shards):
                scatter_copy(box, zone, slot, k).start()

        def scatter_copy(box, zone, slot, k):
            return remote(
                box.at[peer_of(s_id, shards, k, False)],
                zone.at[k - 1],
                g_send.at[slot, k - 1],
                g_recv.at[slot, k - 1],
                peers[k - 1],
            )

        def gather_part(box, zone, slot):
            for k in range(1, shards):
                scatter_copy(box, zone, slot, k).wait()
            add_rows(
                box.at[s_id],
                [box.at[s_id]] + [zone.at[k] for k in range(shards - 1)],
                own_rows,
                slab,
            )

        def line_up(mine, came, total, slot, count):
            @pl.when(has_outer)
            def _():
                remote(mine, came, a_up.at[slot], a_r.at[slot], inner_to).wait_recv()
                add_rows(mine, [mine, came], count, slab if mine.dtype == BF else 8)

            @pl.when(is_mid)
            def _():
                remote(mine, total, a_up.at[slot], a_t.at[slot], inner_to).start()

            @pl.when(jnp.logical_not(is_mid))
            def _():
                remote(mine, came, a_up.at[slot], a_r.at[slot], inner_to).start()

        def line_down(mine, total, slot, count, near, far):
            remote(mine, total, a_up.at[slot], a_t.at[slot], inner_to).wait()

            @pl.when(is_mid)
            def _():
                add_rows(total, [mine, total], count, slab if mine.dtype == BF else 8)

            @pl.when(has_outer)
            def _():
                remote(total, total, a_down.at[slot], a_t.at[slot], outer_to).start()

            if far is not None:
                remote(total, near, a_sib_send.at[slot], a_sib_recv.at[slot], sibling).start()
            local(total, near, a_local.at[slot]).start()

        def line_settle(total, slot, near, far):
            @pl.when(has_outer)
            def _():
                remote(total, total, a_down.at[slot], a_t.at[slot], outer_to).wait_send()

            if far is not None:
                remote(total, far, a_sib_send.at[slot], a_sib_recv.at[slot], sibling).wait()
            local(total, near, a_local.at[slot]).wait()

        lane = lanes_of(128)
        dproj[...] = gm[...].astype(BF)
        load_wo.wait()
        early[0].wait()

        def spread(head, carry):
            block = nt(
                dproj[...], w_buf[pl.ds(pl.multiple_of(head * 256, 256), 256), :]
            ).astype(BF)
            for seq in range(2):
                for two in range(2):
                    piece = block[
                        seq * 128 : seq * 128 + 128, two * 128 : two * 128 + 128
                    ].astype(F32)
                    place = seq * HK + head
                    first = jnp.where(lane >= 64, pltpu.roll(piece, 64, 1), 0.0)
                    dop[place, pl.ds(two * 256, 128), :] = first.astype(BF)
                    dop[place, pl.ds(two * 256 + 128, 128), :] = jnp.where(
                        lane >= 64, piece, 0.0
                    ).astype(BF)
                    value = attn_ref[
                        pl.ds(seq * 128, 128),
                        pl.ds(pl.multiple_of(head * 256 + two * 128, 128), 128),
                    ].astype(F32)
                    product = jnp.transpose(piece * value)
                    delta[place, :, pl.ds(two * 256, 128)] = jnp.sum(
                        product[:64], 0, keepdims=True
                    )
                    delta[place, :, pl.ds(two * 256 + 128, 128)] = jnp.sum(
                        product[64:], 0, keepdims=True
                    )
            return carry

        lax.fori_loop(0, HK, spread, 0)
        load_wq.start()
        ring(2)

        def weight_grad(left, right, grad, count):
            def body(s, carry):
                grad[s] = nn(
                    left[pl.ds(pl.multiple_of(s * part, 16), part), :], right[...]
                ).astype(BF)
                return carry

            lax.fori_loop(0, count, body, 0)

        early[1].wait()
        weight_grad(attn_t_ref, dproj, g_buf, shards)
        for load in early[2:]:
            load.wait()
        core_part(g_buf, o_x, 0).start()
        cosine, sine = cos_ref, sin_ref

        def attend(step, carry):
            slot = lax.rem(step, 2)
            pair, block = step // blocks, step % blocks

            @pl.when(step + 1 < total_steps)
            def _():
                pt_copy(step + 1, 1 - slot).start()
                kv_copy(step + 1, 1 - slot).start()

            pt_copy(step, slot).wait()
            kv_copy(step, slot).wait()
            keyval = kv_buf[slot]
            soft = pt_buf[slot]
            grad_soft = nt(keyval, dop[pair])
            score = (soft.astype(F32) * (grad_soft - delta[pair])).astype(BF)
            both = (nn(score, qp_ref[pair]) + nn(soft, dop[pair])).astype(BF)
            for sub in range(8):
                dkv[pair, block * 4 + sub // 2, sub % 2] = both[sub * 128 : sub * 128 + 128]
            query = tn(keyval, score)[:64] * (1.0 / math.sqrt(HD))
            seq, head = pair // HK, pair % HK
            for two in range(2):
                piece = jnp.transpose(
                    jnp.concatenate(
                        [
                            query[:, two * 256 : two * 256 + 128],
                            query[:, two * 256 + 128 : two * 256 + 256],
                        ],
                        0,
                    )
                )
                where = (
                    pl.ds(pl.multiple_of(seq * 128, 128), 128),
                    pl.ds(pl.multiple_of(head * 256 + two * 128, 128), 128),
                )
                if blocks == 1:
                    cos = cosine[where[0], :]
                    sin = sine[where[0], :]
                    dq[where] = (piece * cos - swap_halves(piece, lane) * sin).astype(BF)
                else:
                    dq[where] = jnp.where(
                        block == 0, piece, dq[where].astype(F32) + piece
                    ).astype(dq.dtype)
            return carry

        def dkv_core_copy(seq):
            return remote(
                dkv.at[pl.ds(seq * HK, HK), :, 1 - c_id],
                dkv_x.at[pl.ds(seq * HK, HK)],
                dkv_core.at[seq],
                dkv_core.at[2 + seq],
                sibling,
            )

        def dkv_copy(seq, k):
            return remote(
                dkv_x.at[pl.ds(seq * HK, HK), lax.rem(l_id + k, line)],
                dkv_z.at[seq, k - 1],
                dkv_send.at[seq, k - 1],
                dkv_recv.at[seq, k - 1],
                mates[k - 1],
            )

        def dkv_scatter(seq):
            dkv_core_copy(seq).wait()

            def body(index, carry):
                head, place = seq * HK + index // line, index % line
                dkv_x[head, place] = (
                    dkv_x[head, place].astype(F32) + dkv[head, place, c_id].astype(F32)
                ).astype(BF)
                return carry

            lax.fori_loop(0, HK * line, body, 0)
            if not hops:
                for k in range(1, line):
                    dkv_copy(seq, k).start()
                return

            @pl.when(l_id == 0)
            def _():
                for dest in range(line - 1, 0, -1):
                    dkv_hop(seq, 0, dest).start()

            @pl.when(l_id == line - 1)
            def _():
                for dest in range(line - 1):
                    dkv_hop(seq, 1, dest).start()

        def dkv_hop(seq, way, dest):
            to = (s_id, lax.rem(l_id + (1 if way == 0 else line - 1), line), c_id)
            return remote(
                dkv_x.at[pl.ds(seq * HK, HK), dest],
                dkv_z.at[seq, way, dest],
                dkv_send.at[seq, way * line + dest],
                dkv_recv.at[seq, way * line + dest],
                to,
            )

        def dkv_hops(seq):
            if not hops:
                return
            low = l_id < line // 2
            for first in (True, False):
                for step in range(1, line):
                    for way, dest in ((0, line - step), (1, step - 1)):
                        ahead = (
                            (l_id > 0) & (l_id < dest)
                            if way == 0
                            else (l_id < line - 1) & (l_id > dest)
                        )
                        turn_now = low if first == (way == 0) else jnp.logical_not(low)

                        @pl.when(ahead & turn_now)
                        def _():
                            dkv_hop(seq, way, dest).wait_recv()
                            dkv_take(seq, way, dest)
                            dkv_hop(seq, way, dest).start()

        def dkv_take(seq, way, dest):
            def body(head, carry):
                dkv_x[seq * HK + head, dest] = (
                    dkv_x[seq * HK + head, dest].astype(F32)
                    + dkv_z[seq, way, dest, head].astype(F32)
                ).astype(BF)
                return carry

            lax.fori_loop(0, HK, body, 0)

        def dkv_arrive(seq):
            if not hops:
                for k in range(1, line):
                    dkv_copy(seq, k).wait()
                return
            for dest in range(line):

                @pl.when(l_id < dest)
                def _():
                    dkv_hop(seq, 0, dest).wait_send()

                @pl.when(l_id > dest)
                def _():
                    dkv_hop(seq, 1, dest).wait_send()

                @pl.when((l_id == dest) & (l_id > 0))
                def _():
                    dkv_hop(seq, 0, dest).wait_recv()

                @pl.when((l_id == dest) & (l_id < line - 1))
                def _():
                    dkv_hop(seq, 1, dest).wait_recv()

        def dkv_parts(seq, head, total):
            if not hops:
                for k in range(line - 1):
                    total = total + dkv_z[seq, k, head].astype(F32)
                return total
            left = jnp.where(l_id > 0, dkv_z[seq, 0, l_id, head].astype(F32), 0.0)
            right = jnp.where(l_id < line - 1, dkv_z[seq, 1, l_id, head].astype(F32), 0.0)
            return total + left + right

        def dkv_gather(seq):
            dkv_arrive(seq)
            cos = jnp.where(lane < 64, cosine[pl.ds(seq * 128, 128), :], 1.0)
            sin = jnp.where(lane < 64, sine[pl.ds(seq * 128, 128), :], 0.0)
            for head in range(HK):
                total = dkv_x[seq * HK + head, l_id].astype(F32)
                total = dkv_parts(seq, head, total)
                dkv_own[pl.ds(seq * 128, 128), pl.ds(head * 128, 128)] = (
                    total * cos - swap_halves(total, lane) * sin
                ).astype(BF)

        near = c_id * own_rows
        far = (1 - c_id) * own_rows
        pieces = 2 if own_rows % 32 == 0 else 1

        def jobs_of(box, came, total, out, slot):
            count = own_rows // pieces
            result = []
            for piece in range(pieces):
                span = pl.ds(piece * count, count)
                result.append(
                    (
                        box.at[s_id, span],
                        came.at[span],
                        total.at[span],
                        slot + piece,
                        count,
                        out.at[pl.ds(pl.multiple_of(near + piece * count, 16), count)],
                        out.at[pl.ds(pl.multiple_of(far + piece * count, 16), count)],
                    )
                )
            return result

        o_jobs = jobs_of(o_x, o_r, o_t, out_wo, 0)
        q_jobs = jobs_of(q_x, q_r, q_t, out_wq, 2)
        k_jobs = jobs_of(k_x, k_r, k_t, out_wkv, 4)
        gain_job = [(gn_x, gn_r, gn_t, 6, 8, out_gain, None)]
        jobs = o_jobs + q_jobs + gain_job + k_jobs

        def first_up(some):
            @pl.when(jnp.logical_not(has_outer))
            def _():
                for mine, came, total, slot, count, _, _ in some:
                    line_up(mine, came, total, slot, count)

        def job_up(job):
            mine, came, total, slot, count, _, _ = job

            @pl.when(has_outer)
            def _():
                line_up(mine, came, total, slot, count)

        def job_down(job):
            mine, _, total, slot, count, to, other = job
            line_down(mine, total, slot, count, to, other)

        lax.fori_loop(0, 2 * blocks, attend, 0)
        scatter_part(g_buf, o_x, o_z, 0)
        ring(3)
        lax.fori_loop(2 * blocks, HK * blocks, attend, 0)
        dkv_core_copy(0).start()
        ring(4)
        lax.fori_loop(HK * blocks, (HK + 2) * blocks, attend, 0)
        dkv_scatter(0)
        lax.fori_loop((HK + 2) * blocks, total_steps, attend, 0)
        dkv_core_copy(1).start()
        if blocks > 1:
            for two in range(width // 128):
                for seq in range(2):
                    where = (pl.ds(seq * 128, 128), pl.ds(two * 128, 128))
                    piece = dq[where].astype(F32)
                    cos = cosine[where[0], :]
                    sin = sine[where[0], :]
                    dq[where] = (piece * cos - swap_halves(piece, lane) * sin).astype(dq.dtype)
        ring(5)
        weight_grad(n1_t_ref, dq, g_buf, shards)
        core_part(g_buf, q_x, 1).start()
        dkv_scatter(1)
        ends_up(7, chunks)
        ring(6)
        ring_down(5)
        dkv_hops(0)
        scatter_part(g_buf, q_x, q_z, 1)
        gather_part(o_x, o_z, 0)
        first_up(o_jobs)
        dkv_hops(1)
        ring_down(6)
        load_wq.wait()
        load_wkv.wait()
        back = nt(dq[...], w_buf[...])
        ends_down(0, 3)
        dkv_gather(0)
        dkv_gather(1)
        g_kv = g_buf.at[:, :, pl.ds(0, 2 * HK * HD)]
        weight_grad(n1_t_ref, dkv_own, g_kv, shards)
        core_part(g_kv, k_x, 2).start()
        back = back + nt(dkv_own[...], wkv_buf[...])
        scatter_part(g_kv, k_x, k_z, 2)
        ring(7, 8)
        hidden = x_ref[...].astype(F32)
        scale = lax.rsqrt(jnp.mean(hidden * hidden, -1, keepdims=True) + EPSILON)
        scaled = back * gains_ref[0:1, :]
        gn_own[0:1, :] = jnp.sum(back * hidden * scale, 0, keepdims=True)
        gn_own[2:8, :] = jnp.zeros((6, width), F32)
        gain_core = remote(gn_own, gn_x, g_core.at[6], g_core.at[7], sibling)
        gain_core.start()
        out_dx[...] = (
            gm[...]
            + scale * scaled
            - hidden * (scale * scale * scale) * jnp.mean(scaled * hidden, -1, keepdims=True)
        ).astype(BF)
        gain_core.wait()
        gn_own[...] = gn_own[...] + gn_x[...]

        def gain_copy(k):
            return remote(
                gn_own, gn_z.at[k - 1], g_send.at[3, k - 1], g_recv.at[3, k - 1], peers[k - 1]
            )

        for k in range(1, shards):
            gain_copy(k).start()
        for k in range(1, shards):
            part_copy(k).start()

        def gather_gain():
            for k in range(1, shards):
                gain_copy(k).wait()
            total = gn_own[...]
            for k in range(shards - 1):
                total = total + gn_z[k]
            gn_x[...] = total

        @pl.when(jnp.logical_not(has_outer))
        def _():
            gather_part(q_x, q_z, 1)
            for mine, came, total, slot, count, _, _ in q_jobs:
                line_up(mine, came, total, slot, count)
            gather_gain()
            gather_part(k_x, k_z, 2)
            for mine, came, total, slot, count, _, _ in gain_job + k_jobs:
                line_up(mine, came, total, slot, count)

        @pl.when(has_outer)
        def _():
            ring(8, 1)
            ring(9, 1)
            gather_part(q_x, q_z, 1)
            ring(10, 1)
            gather_gain()
            gather_part(k_x, k_z, 2)
            ring(11, 1)

        ends_down(3, 8)
        todo = list(jobs)
        done = [todo.pop(0)]
        job_up(done[-1])
        ring(chunks, 1)
        ends_down(8, chunks)
        for job in todo:
            job_up(job)
            done.append(job)
            job_down(done.pop(0))
        for job in done:
            job_down(job)
        for k in range(1, shards):
            part_copy(k).wait()
        result = mid_ref[...]
        for first in range(0, shards, 4):
            stage = [
                local(
                    parts_hbm.at[s_id] if k == 0 else p_zone.at[k - 1],
                    w_buf.at[pl.ds((k - first) * rows, rows)],
                    load_sem.at[k - first],
                )
                for k in range(first, min(shards, first + 4))
            ]
            for copy in stage:
                copy.start()
            for k, copy in enumerate(stage):
                copy.wait()
                result = result + w_buf[k * rows : (k + 1) * rows, :].astype(F32)
        out_result[...] = result.astype(BF)
        for _, _, total, slot, _, to, other in jobs:
            line_settle(total, slot, to, other)

    pl.run_scoped(
        attention,
        v((width, 2 * HK * HD), BF),
        v((2, 1024, 512), BF),
        v((2, 1024, 128), BF),
        v((rows, width), BF),
        v((2 * HK, 512, 128), BF),
        v((2 * HK, 1, 512), F32),
        v((2 * HK, line, 2, 128, 128), BF),
        v((rows, width), BF if blocks == 1 else F32),
        v((rows, 2 * HK * HD), BF),
        v((shards, part, width), BF),
        v((rows, width), BF),
        v((width, rows), BF),
        v((2 * HK, 512, 128), BF),
        v((width, rows), BF),
        v((rows, width), BF),
    )

    def last(index, carry):
        settle(index)
        return carry

    lax.fori_loop(0, chunks, last, 0)


def backward_call(shards, line, *arrays):
    x, kv, gate = arrays[7], arrays[-1], arrays[14]
    rows, width = x.shape
    keys = kv.shape[1]
    feed = gate.shape[2]
    part = width // shards
    own_rows = part // 2
    kv_width = 2 * HK * HD
    sizes = (shards, line, keys, rows, width, feed)
    dma = pltpu.SemaphoreType.DMA
    v = pltpu.VMEM
    vm = pl.BlockSpec(memory_space=pltpu.VMEM)
    hbm = pl.BlockSpec(memory_space=pltpu.HBM)
    half = width // 2
    shape = jax.ShapeDtypeStruct

    def boxes(cols):
        return [
            v((shards, own_rows, cols), BF),
            v((shards - 1, own_rows, cols), BF),
            v((own_rows, cols), BF),
            v((own_rows, cols), BF),
        ]

    scratch = [
        v((width, width), BF),
        v((rows, width), F32),
        v((rows, width), F32),
        v((2 * HK, line, 128, 128), BF),
        v((2, 2, 4, HK, 128, 128) if line == 4 else (2, line - 1, HK, 128, 128), BF),
        *[v((2, half, feed), BF) for _ in range(4)],
        *[v((feed, half), BF) for _ in range(4)],
        *boxes(width),
        *boxes(width),
        *boxes(kv_width),
        v((8, width), F32),
        v((8, width), F32),
        v((shards - 1, 8, width), F32),
        v((8, width), F32),
        v((8, width), F32),
        dma((max(6, shards),)),
        dma((2,)),
        dma((2,)),
        dma((6,)),
        *[dma((12,)) for _ in range(7)],
        dma((4,)),
        dma((2, 2 * line)),
        dma((2, 2 * line)),
        dma((8,)),
        dma((4, shards - 1)),
        dma((4, shards - 1)),
        *[dma((7,)) for _ in range(7)],
        *[dma((shards - 1,)) for _ in range(4)],
        dma((9,)),
    ]
    return pl.pallas_call(
        lambda *refs: backward_kernel(sizes, *refs),
        out_shape=(
            shape((width, feed), BF),
            shape((width, feed), BF),
            shape((feed, width), BF),
            shape((part, width), BF),
            shape((part, width), BF),
            shape((part, kv_width), BF),
            shape((8, width), F32),
            shape((rows, width), BF),
            shape((rows, width), BF),
            shape((shards - 1, rows, width), BF),
            shape((shards - 1, rows, width), BF),
        ),
        in_specs=[vm] * 3 + [hbm] * 18,
        out_specs=(*[hbm] * 7, vm, vm, hbm, hbm),
        scratch_shapes=scratch,
        compiler_params=pltpu.CompilerParams(
            collective_id=3, has_side_effects=True, vmem_limit_bytes=VMEM_LIMIT
        ),
        name="backward",
    )(*arrays)


def per_device(
    tokens,
    cotangent,
    positions,
    lengths,
    attn_gain,
    w_query,
    w_key,
    w_value,
    w_out,
    mlp_gain,
    w_gate,
    w_up,
    w_down,
):
    seqs, stretch, width = tokens.shape
    shards, line = lax.axis_size("shard"), lax.axis_size("line")
    rows = seqs * stretch
    rank = lax.axis_index("line") * 2 + lax.axis_index("core")
    places = lax.dynamic_slice_in_dim(positions, rank * stretch, stretch, 1)
    valid = (places < lengths[:, None]).astype(F32)
    info = jnp.concatenate([places.astype(F32), valid, jnp.zeros((4, stretch), F32)], 0)
    keys_at = jnp.where(positions < lengths[:, None], positions, 1 << 24).astype(F32)
    frequency = ROPE_BASE ** (-jnp.arange(HD // 2, dtype=F32) * 2.0 / HD)
    frequency = jnp.concatenate([frequency] * 4)[None]
    w_kv = jnp.stack(
        [w_key.reshape(-1, HK, HD), w_value.reshape(-1, HK, HD)], 2
    ).reshape(-1, 2 * HK * HD)
    span = attn_gain.shape[0]
    x = tokens.reshape(rows, width)
    (
        attn,
        attn_t,
        norm_t,
        packed_q,
        middle,
        norm_two,
        gains,
        cos_wide,
        sin_wide,
        wq_all,
        wkv_all,
        out_all,
        packed_kv,
        soft,
        grad_low_all,
    ) = front_call(
        shards,
        line,
        info,
        keys_at.reshape(seqs, -1, 128),
        frequency,
        attn_gain[None],
        mlp_gain[None],
        x,
        cotangent.reshape(rows, width),
        w_query,
        w_kv,
        w_out,
    )
    packed_kv = packed_kv.reshape(seqs * HK, -1, 128)
    grad_low_all = grad_low_all.reshape(shards, rows, width)
    parts, back, norm_all_t, inner_t, grad_gate, grad_up = feed_call(
        shards, norm_two, grad_low_all, w_gate, w_up, w_down
    )
    sum_gate, sum_up, sum_down, sum_out, sum_query, sum_kv, sum_gain, grad_input, result, _, _ = (
        backward_call(
            shards,
            line,
            gains,
            cos_wide,
            sin_wide,
            attn,
            attn_t,
            packed_q,
            norm_t,
            x,
            middle,
            parts,
            back,
            norm_all_t,
            grad_low_all,
            inner_t,
            grad_gate,
            grad_up,
            out_all,
            wq_all,
            wkv_all,
            soft,
            packed_kv,
        )
    )
    sum_kv = sum_kv.reshape(-1, HK, 2, HD)
    sum_gain = lax.dynamic_slice_in_dim(sum_gain, lax.axis_index("shard") * span, span, 1)
    return (
        result.reshape(seqs, stretch, width),
        grad_input.reshape(seqs, stretch, width),
        sum_gain[0],
        sum_query.astype(F32),
        sum_kv[:, :, 0].reshape(-1, HK * HD).astype(F32),
        sum_kv[:, :, 1].reshape(-1, HK * HD).astype(F32),
        sum_out.astype(F32),
        sum_gain[1],
        sum_gate.astype(F32),
        sum_up.astype(F32),
        sum_down.astype(F32),
    )


def solution(mesh):
    shards, ctx = mesh.devices.shape
    inner = Mesh(mesh.devices.reshape(shards, ctx // 2, 2), ("shard", "line", "core"))
    where = ("line", "core")
    return jax.shard_map(
        per_device,
        mesh=inner,
        in_specs=(
            P("shard", where, None),
            P("shard", where, None),
            P("shard", None),
            P("shard"),
            P("shard"),
            P("shard", None),
            P("shard", None),
            P("shard", None),
            P("shard", None),
            P("shard"),
            P(None, "shard"),
            P(None, "shard"),
            P("shard", None),
        ),
        out_specs=(
            P("shard", where, None),
            P("shard", where, None),
            P("shard"),
            P("shard", None),
            P("shard", None),
            P("shard", None),
            P("shard", None),
            P("shard"),
            P(None, "shard"),
            P(None, "shard"),
            P("shard", None),
        ),
        check_vma=False,
    )
```

time: 894 us -> 291 us (0.33)
  waiting for transfers between devices: 551 us -> 0 us
  Pallas kernels: 0 us -> 264 us
  matrix products: 154 us -> 0 us
  blocking collectives: 53.2 us -> 0 us
  local copies, waits for them, and re-layouts: 58.4 us -> 12 us
  other arithmetic: 50 us -> 12.9 us
  between operations: 16.1 us -> 0.78 us
    pallas_call x0 -> x3, Pallas kernels: none -> 264 us  [the longest x1 160 us: backward_call(): pl.pallas_call(lambda *refs: backward_kernel(sizes, *refs), out_shape=(sh...]
    reduce_scatter x10 -> x0, waiting for transfers between devices: 208 us -> none  [the longest x2 69.2 us: over_all(): share = lax.psum_scatter(part, 'shard', scatter_dimension=0, tiled=True)]
    all_gather x10 -> x0, waiting for transfers between devices: 173 us -> none  [the longest x1 45.8 us: per_device(): qkv_all = lax.all_gather(qkv_local, 'shard', axis=0, tiled=True)]
    psum x1 -> x0, waiting for transfers between devices: 168 us -> none  [over_ctx(): share = lax.psum(share, 'line')]
    dot_general x29 -> x0, matrix products: 154 us -> none  [the longest x5 25.9 us: product_tn(): jnp.einsum('ra,rb->ab', left_side, right_side, preferred_element_type=jnp...]
    psum x1 -> x0, blocking collectives: 39.3 us -> none  [per_device(): gains = lax.psum(gains, ('shard', 'line', 'core')).astype(jnp.float32)]
    convert_element_type x15 -> x8, other arithmetic: 29.2 us -> 11.5 us  [the longest x1 2.48 us: per_device(): sum_down.astype(F32)]
    dynamic_slice x12 -> x0, local copies, waits for them, and re-layouts: 14.7 us -> none  [the longest x2 4.16 us: query_step(): value_piece = lax.dynamic_slice_in_dim(value_full, offset, sub_rows, 1)]
  transfers between devices with their start and end apart: 21 -> 0, of which waited for: 16 -> 0; matrix products, arithmetic and copies ran while one was open for 17% -> 0% of each run, Pallas kernels for 0% -> 0%
where the time goes in v4:
time: 291 us; the launch traced here: 290 us
  Pallas kernels  264 us (91%)
  other arithmetic  12.9 us (4%)
  local copies, waits for them, and re-layouts  12 us (4%)
    pallas_call x1, Pallas kernels, backward_call(): pl.pallas_call(lambda *refs: backward_kernel(sizes, *refs), out_shape=(sh...  160 us
    pallas_call x1, Pallas kernels, front_call(): pl.pallas_call(lambda *refs: front_kernel((shards, line, keys, rows, widt...  68 us
    pallas_call x1, Pallas kernels, feed_call(): pl.pallas_call(lambda *refs: feed_kernel((shards, rows, width, feed), *re...  36.7 us
    unnamed x29, local copies, waits for them, and re-layouts  6.97 us

profile of v4, /device:TPU:0, one launch (start us, length us, event | category | flops | bytes accessed | tf_op | source)
XLA Modules:
  0.0 290.0 jit_solution(16197423791508842532)
XLA Ops:
  0.6 0.0 copy-start.7
  0.7 0.0 copy-start.8
  0.7 0.0 copy-start.9
  0.7 0.0 copy-start.10
  0.7 0.8 compare_convert_fusion
  1.5 0.7 dynamic-slice_convert_fusion
  2.2 0.1 pad.8.clone
  2.2 0.7 maximum_maximum_fusion.refs_0_
  2.9 1.1 copy.26
  4.0 1.1 copy.27
  5.2 0.1 pad_maximum_fusion
  5.3 0.1 copy.28
  5.3 1.0 copy.29.refs_8_
  6.3 0.0 copy-done.7
  6.3 0.0 copy-done.8
  6.3 0.1 fusion.1
  6.4 0.6 copy.35
  7.0 0.0 copy-done.9
  7.0 0.6 broadcast_in_dim.21.refs_3_
  7.5 0.0 copy-done.10
  7.5 0.6 broadcast_in_dim.22.refs_4_
  8.1 0.6 maximum_bitcast_fusion.refs_2_
  8.7 68.0 %front.1 = (bf16[256,1280]{1,0:T(8,128)(2,1)}, bf16[1280,256]{1,0:T(8,128)(2,1)}, bf16[1280,256]{1,0:T(8,128)(2,1)}, bf16[10,512,128]{2,1,0:T(8,128)(2,1)}, f32[...) custom-call(f32[8,128]{1,0:T(8,128)} %maximum_maximum_fusion.refs_0_, ...), custom_call_target="tpu_custom_call" | custom-call | tf_op jit(solution)/shard_map/front/pallas_call | solution.py:542
  76.7 36.7 %feed.1 = (bf16[4,256,1280]{2,1,0:T(8,128)(2,1)}, bf16[4,256,1280]{2,1,0:T(8,128)(2,1)}, bf16[1280,1024]{1,0:T(8,128)(2,1)}, bf16[896,1024]{1,0:T(8,128)(2,1)}, ...) custom-call(bf16[256,1280]{1,0:T(8,128)(2,1)} %get-tuple-element.49.refs_0_, bf16[4,256,1280]{2,1,0:T(8,128)(2,1)} %bitcast.23, ...), custom_call_target="tpu_custom_call" | custom-call | tf_op jit(solution)/shard_map/feed/pallas_call | solution.py:751
  113.4 159.6 %backward.1 = (bf16[1280,896]{1,0:T(8,128)(2,1)}, bf16[1280,896]{1,0:T(8,128)(2,1)}, bf16[896,1280]{1,0:T(8,128)(2,1)}, bf16[320,1280]{1,0:T(8,128)(2,1)}, bf16[...) custom-call(f32[8,1280]{1,0:T(8,128)} %get-tuple-element.41.refs_0_,, ...), custom_call_target="tpu_custom_call" | custom-call | tf_op jit(solution)/shard_map/backward/pallas_call | solution.py:1750
  273.1 1.3 copy.30
  274.3 0.0 copy-start.2
  274.3 0.1 fusion.2
  274.4 0.1 bitcast_convert_fusion
  274.5 1.0 copy.31
  275.5 1.0 copy.32
  276.5 0.0 copy-done.2
  276.5 0.0 copy-start.1
  276.5 2.4 convert_element_type.45
  279.0 0.1 copy-done.1
  279.1 0.0 copy-start
  279.1 2.4 convert_element_type.46
  281.5 0.1 copy-done
  281.7 0.0 copy-start.4
  281.7 2.5 convert_element_type.47
  284.1 0.0 copy-start.3
  284.1 0.0 copy-done.4
  284.1 0.0 copy-start.6
  284.2 1.3 convert_element_type.39
  285.4 0.0 copy-start.5
  285.4 0.1 copy-done.3
  285.6 1.3 convert_element_type.44
  286.8 1.5 dynamic-slice_reduce_fusion
  288.3 0.0 copy-done.6
  288.3 0.8 copy.38
  289.1 0.0 copy-done.5
  289.1 0.8 copy.39
  (2 shorter events, 0.0 us)
Async XLA Ops:
  0.6 5.6 %copy-start.7 = (s32[2,1024]{1,0:T(2,128)S(1)}, s32[2,1024]{1,0:T(2,128)}, u32[]{:S(2)}) copy-start(s32[2,1024]{1,0:T(2,128)} %param.15) | copy-start | bytes 24580
  0.7 5.6 %copy-start.8 = (s32[2]{0:T(128)S(1)}, s32[2]{0:T(128)}, u32[]{:S(2)}) copy-start(s32[2]{0:T(128)} %param.16) | copy-start | bytes 28
  0.7 6.3 %copy-start.9 = (bf16[320]{0:T(512)(128)(2,1)S(1)}, bf16[320]{0:T(512)(128)(2,1)}, u32[]{:S(2)}) copy-start(bf16[320]{0:T(512)(128)(2,1)} %param.17) | copy-start | bytes 1924
  0.7 6.9 %copy-start.10 = (bf16[320]{0:T(512)(128)(2,1)S(1)}, bf16[320]{0:T(512)(128)(2,1)}, u32[]{:S(2)}) copy-start(bf16[320]{0:T(512)(128)(2,1)} %param.22) | copy-start | bytes 1924
  274.3 2.2 copy-start.2
  276.5 2.6 copy-start.1
  279.1 2.6 copy-start
  281.7 2.5 copy-start.4
  284.1 1.4 copy-start.3
  284.1 4.2 %copy-start.6 = (bf16[256,1280]{1,0:T(8,128)(2,1)S(1)}, bf16[256,1280]{1,0:T(8,128)(2,1)}, u32[]{:S(2)}) copy-start(bf16[256,1280]{1,0:T(8,128)(2,1)} %get-tuple-element.62) | copy-start | bytes 1966084
  285.4 3.7 %copy-start.5 = (bf16[256,1280]{1,0:T(8,128)(2,1)S(1)}, bf16[256,1280]{1,0:T(8,128)(2,1)}, u32[]{:S(2)}) copy-start(bf16[256,1280]{1,0:T(8,128)(2,1)} %get-tuple-element.63) | copy-start | bytes 1966084

commit v5 on v4

--- a/solution.py
+++ b/solution.py
@@ -2,6 +2,7 @@
 
 import jax
 import jax.numpy as jnp
+import numpy as np
 from jax import lax
 from jax.experimental import pallas as pl
 from jax.experimental.pallas import tpu as pltpu
@@ -154,22 +155,19 @@
 
 def front_kernel(
     sizes,
-    info_ref,
-    keys_ref,
+    positions_ref,
+    lengths_ref,
     freq_ref,
-    gain_one_ref,
-    gain_two_ref,
+    gains_in,
+    wk_ref,
+    wv_ref,
     x_hbm,
     g_hbm,
     wq_ref,
-    wkv_ref,
     wo_ref,
-    out_attn,
-    out_attn_t,
-    out_n1_t,
-    out_qp,
-    out_mid,
-    out_n2,
+    wg_hbm,
+    wu_hbm,
+    wd_hbm,
     out_gains,
     cos_ref,
     sin_ref,
@@ -179,17 +177,37 @@
     out_kv,
     out_pt,
     out_g,
+    keep_attn,
+    keep_attn_t,
+    keep_n1_t,
+    keep_qp,
+    keep_mid,
+    out_parts,
+    out_back,
+    out_n2_t,
+    out_inner_t,
+    out_dgate,
+    out_dup,
     wq_all,
     wkv_all,
     wo_all,
     kv_all,
+    n2_all,
+    g_all,
+    wg,
+    wu,
+    wd,
+    out_attn,
+    out_attn_t,
+    out_n1_t,
+    out_qp,
+    out_mid,
     norm,
     x_ref,
-    g_ref,
     bias_ref,
+    pt_stage,
     gains_ref,
     gain_zone,
-    pt_stage,
     gain_send,
     gain_recv,
     wq_s,
@@ -206,26 +224,41 @@
     wo_sr,
     g_s,
     g_r,
+    n2_send,
+    n2_recv,
     kv_send,
     kv_recv,
     kv_sib_send,
     kv_sib_recv,
     pt_sem,
+    in_sem,
+    load_sem,
+    keep_sem,
+    part_sem,
+    back_sem,
     out_sem,
 ):
-    shards, line, keys, rows, width = sizes
+    shards, line, keys, rows, width, feed = sizes
     env = Env(shards, line)
     s_id, l_id, c_id = env.s_id, env.l_id, env.c_id
     part = width // shards
     hp = part // 2
     quarter = hp // 2
     blocks = keys // 1024
-    load_x = pltpu.make_async_copy(x_hbm, x_ref, out_sem.at[4])
-    load_g = pltpu.make_async_copy(g_hbm, g_ref, out_sem.at[5])
-    load_x.start()
+    load_g = pltpu.make_async_copy(g_hbm, g_all.at[s_id], in_sem.at[0])
     load_g.start()
-    gains_ref[0:1, :] = gain_one_ref[...].astype(F32)
-    gains_ref[1:2, :] = gain_two_ref[...].astype(F32)
+    loads = [
+        pltpu.make_async_copy(src, dst, load_sem.at[i])
+        for i, (src, dst) in enumerate(((wg_hbm, wg), (wu_hbm, wu), (wd_hbm, wd)))
+    ]
+    for head in range(HK):
+        both = jnp.concatenate(
+            [ref[:, head * HD : head * HD + HD].astype(F32) for ref in (wk_ref, wv_ref)], 1
+        )
+        wkv_all[pl.ds(pl.multiple_of(s_id * part, 16), part), head * 128 : head * 128 + 128] = (
+            both.astype(BF)
+        )
+    gains_ref[0:2, :] = gains_in[...].astype(F32)
     gains_ref[2:8, :] = jnp.zeros((6, part), F32)
     env.barrier(
         [env.sibling]
@@ -233,6 +266,17 @@
         + [env.mate(k) for k in range(1, line)]
     )
 
+    def tokens_of(ref):
+        def block(s, core, first, count):
+            return ref.at[s, pl.ds(first * (rows // 2), count * (rows // 2))]
+
+        return block
+
+    grad_gather = Spread(env, tokens_of(g_all), g_all.at[s_id], (g_s, g_r, None, None), False)
+    n2_gather = Spread(
+        env, tokens_of(n2_all), n2_all.at[s_id], (n2_send, n2_recv, None, None), False
+    )
+
     def rows_of(ref):
         def block(s, core, first, count):
             start = s * part + core * hp + first * quarter
@@ -240,314 +284,449 @@
 
         return block
 
-    def g_rows(s, core, first, count):
-        start = s * rows + first * (rows // 2)
-        return out_g.at[pl.ds(pl.multiple_of(start, 16), count * (rows // 2))]
 
     mine = pl.ds(pl.multiple_of(c_id * hp, 16), hp)
     own = pl.ds(pl.multiple_of(s_id * part, 16), part)
+    kv_mine = pl.ds(pl.multiple_of(s_id * part + c_id * hp, 16), hp)
     kv_gather = Spread(
-        env, rows_of(wkv_all), wkv_ref.at[mine], (wkv_s, wkv_r, wkv_ss, wkv_sr), True
+        env, rows_of(wkv_all), wkv_all.at[kv_mine], (wkv_s, wkv_r, wkv_ss, wkv_sr), True
     )
     q_gather = Spread(env, rows_of(wq_all), wq_ref.at[mine], (wq_s, wq_r, wq_ss, wq_sr), True)
     o_gather = Spread(env, rows_of(wo_all), wo_ref.at[mine], (wo_s, wo_r, wo_ss, wo_sr), True)
-    grad_gather = Spread(env, g_rows, g_ref, (g_s, g_r, None, None), False)
-
-    def gain_copy(k):
-        return env.remote(
-            gains_ref, gain_zone.at[s_id], gain_send.at[k], gain_recv.at[k], env.peer(k)
+    outs = [
+        pltpu.make_async_copy(src, dst, keep_sem.at[i])
+        for i, (src, dst) in enumerate(
+            (
+                (wkv_all, out_wkv),
+                (wq_all, out_wq),
+                (kv_all, out_kv),
+                (wo_all, out_wo),
+                (out_attn, keep_attn),
+                (out_attn_t, keep_attn_t),
+                (out_n1_t, keep_n1_t),
+                (out_qp, keep_qp),
+                (out_mid, keep_mid),
+            )
         )
-
-    for k in range(1, shards):
-        gain_copy(k).start()
-    kv_gather.start()
-    locals_ = [
-        pltpu.make_async_copy(wkv_ref, wkv_all.at[own], out_sem.at[0]),
-        pltpu.make_async_copy(wq_ref, wq_all.at[own], out_sem.at[1]),
-        pltpu.make_async_copy(wo_ref, wo_all.at[own], out_sem.at[2]),
     ]
-    for copy in locals_:
-        copy.start()
-    gain_zone[s_id] = gains_ref[...]
-    lane = lanes_of(128)
-    info = jnp.transpose(info_ref[...])
-    for seq in range(2):
-        angle = info[:, seq : seq + 1] * freq_ref[...]
-        cos_ref[seq * 128 : seq * 128 + 128, :] = jnp.cos(angle)
-        sine = jnp.sin(angle)
-        sin_ref[seq * 128 : seq * 128 + 128, :] = jnp.where(lane % 64 < 32, -sine, sine)
-    load_x.wait()
-    hidden = x_ref[...].astype(F32)
-    scale = lax.rsqrt(jnp.mean(hidden * hidden, -1, keepdims=True) + EPSILON)
-    for k in range(1, shards):
-        gain_copy(k).wait()
-    out_gains[...] = jnp.concatenate([gain_zone[s] for s in range(shards)], 1)
-    norm[...] = (hidden * scale * out_gains[0:1, :]).astype(BF)
-    kv_gather.forward()
-    q_gather.start()
-    for copy in locals_:
-        copy.wait()
-    kv_gather.collect()
-    kv_gather.finish()
-
-    place = l_id * 2 + c_id
-
-    def make_kv(head, carry):
-        block = nn(norm[...], wkv_all[:, pl.ds(pl.multiple_of(head * 128, 128), 128)])
+
+    def attention_part():
+        load_x = pltpu.make_async_copy(x_hbm, x_ref, in_sem.at[3])
+        load_x.start()
+        def gain_copy(k):
+            return env.remote(
+                gains_ref, gain_zone.at[s_id], gain_send.at[k], gain_recv.at[k], env.peer(k)
+            )
+
+        for k in range(1, shards):
+            gain_copy(k).start()
+        kv_gather.start()
+        locals_ = [
+            pltpu.make_async_copy(wq_ref, wq_all.at[own], in_sem.at[1]),
+            pltpu.make_async_copy(wo_ref, wo_all.at[own], in_sem.at[2]),
+        ]
+        for copy in locals_:
+            copy.start()
+        gain_zone[s_id] = gains_ref[...]
+        lane = lanes_of(128)
+        place = pl.ds(pl.multiple_of((l_id * 2 + c_id) * 128, 128), 128)
+        spots = positions_ref[:, place].astype(F32)
+        good = [
+            jnp.where(positions_ref[seq : seq + 1, place] < lengths_ref[seq], 1.0, 0.0).astype(F32)
+            for seq in range(2)
+        ]
+        info = jnp.transpose(jnp.concatenate([spots] + good + [jnp.zeros((4, 128), F32)], 0))
         for seq in range(2):
-            piece = block[seq * 128 : seq * 128 + 128]
-            cos = jnp.where(lane < 64, cos_ref[pl.ds(seq * 128, 128), :], 1.0)
-            sin = jnp.where(lane < 64, sin_ref[pl.ds(seq * 128, 128), :], 0.0)
-            kv_all[seq * HK + head, place] = (piece * cos + swap_halves(piece, lane) * sin).astype(
-                BF
-            )
-        return carry
-
-    lax.fori_loop(0, HK, make_kv, 0)
-
-    def kv_slice(seq, l, c):
-        return kv_all.at[pl.ds(seq * HK, HK), l * 2 + c]
-
-    def kv_move(seq, way, src):
-        piece = kv_slice(seq, src, c_id)
-        to = (s_id, lax.rem(l_id + (1 if way == 0 else line - 1), line), c_id)
-        return env.remote(
-            piece, piece, kv_send.at[seq, way * line + src], kv_recv.at[seq, src], to
-        )
-
-    def kv_sib(seq, src):
-        piece = kv_slice(seq, src, c_id)
-        return env.remote(
-            piece, piece, kv_sib_send.at[seq, src], kv_sib_recv.at[seq, src], env.sibling
-        )
-
-    def kv_onward(seq, way, src):
-        @pl.when((l_id < line - 1) if way == 0 else (l_id > 0))
-        def _():
-            kv_move(seq, way, src).start()
-
-    def kv_start(seq):
-        for way in range(2):
-            kv_onward(seq, way, l_id)
-        kv_sib(seq, l_id).start()
-
-    def kv_step(seq, far):
-        for way in range(2):
-            src = l_id - far if way == 0 else l_id + far
-
-            @pl.when((src >= 0) & (src < line))
-            def _():
-                kv_move(seq, way, src).wait_recv()
-                kv_onward(seq, way, src)
-                kv_sib(seq, src).start()
-
-    def kv_finish(seq):
-        for src in range(line):
-            kv_sib(seq, src).wait()
-
-    def kv_settle(seq):
-        for src in range(line):
-
-            @pl.when((l_id < line - 1) & (src <= l_id))
-            def _():
-                kv_move(seq, 0, src).wait_send()
-
-            @pl.when((l_id > 0) & (src >= l_id))
-            def _():
-                kv_move(seq, 1, src).wait_send()
-
-    kv_start(0)
-    load_g.wait()
-    for seq in range(2):
-        rows_ = pl.ds(seq * 128, 128)
-        g_ref[rows_, :] = (g_ref[rows_, :].astype(F32) * info[:, 2 + seq : 3 + seq]).astype(BF)
-        key_at = jnp.transpose(keys_ref[seq])
-        for tile in range(keys // 128):
-            bias_ref[seq, tile * 128 : tile * 128 + 128, :] = jnp.where(
-                key_at[:, tile : tile + 1] <= info_ref[seq : seq + 1, :], 0.0, NEGATIVE
-            )
-    keep_g = pltpu.make_async_copy(
-        g_ref, out_g.at[pl.ds(pl.multiple_of(s_id * rows, 16), rows)], out_sem.at[4]
-    )
-    keep_g.start()
-    for tile in range(width // 128):
-        piece = norm[:, tile * 128 : tile * 128 + 128].astype(F32)
-        out_n1_t[tile * 128 : tile * 128 + 128, :] = jnp.transpose(piece).astype(BF)
-    q_gather.forward()
-    o_gather.start()
-    kv_step(0, 1)
-    if line == 2:
-        kv_start(1)
-    else:
-        kv_step(0, 2)
-        kv_start(1)
-    q_gather.collect()
-    q_gather.finish()
-
-    def make_q(head, carry):
-        block = nn(norm[...], wq_all[:, pl.ds(pl.multiple_of(head * 256, 256), 256)])
-        for seq in range(2):
-            cos = cos_ref[pl.ds(seq * 128, 128), :]
-            sin = sin_ref[pl.ds(seq * 128, 128), :]
-            for two in range(2):
-                piece = block[seq * 128 : seq * 128 + 128, two * 128 : two * 128 + 128]
-                piece = piece * cos + swap_halves(piece, lane) * sin
-                piece = piece.astype(BF).astype(F32) * (1.0 / math.sqrt(HD))
-                pair = seq * HK + head
-                out_qp[pair, pl.ds(two * 256, 128), :] = jnp.where(lane < 64, piece, 0.0).astype(
+            angle = info[:, seq : seq + 1] * freq_ref[...]
+            cos_ref[seq * 128 : seq * 128 + 128, :] = jnp.cos(angle)
+            sine = jnp.sin(angle)
+            sin_ref[seq * 128 : seq * 128 + 128, :] = jnp.where(lane % 64 < 32, -sine, sine)
+        load_x.wait()
+        hidden = x_ref[...].astype(F32)
+        scale = lax.rsqrt(jnp.mean(hidden * hidden, -1, keepdims=True) + EPSILON)
+        for k in range(1, shards):
+            gain_copy(k).wait()
+        out_gains[...] = jnp.concatenate([gain_zone[s] for s in range(shards)], 1)
+        norm[...] = (hidden * scale * out_gains[0:1, :]).astype(BF)
+        kv_gather.forward()
+        q_gather.start()
+        for copy in locals_:
+            copy.wait()
+        kv_gather.collect()
+        kv_gather.finish()
+
+        spot = l_id * 2 + c_id
+
+        def make_kv(head, carry):
+            block = nn(norm[...], wkv_all[:, pl.ds(pl.multiple_of(head * 128, 128), 128)])
+            for seq in range(2):
+                piece = block[seq * 128 : seq * 128 + 128]
+                cos = jnp.where(lane < 64, cos_ref[pl.ds(seq * 128, 128), :], 1.0)
+                sin = jnp.where(lane < 64, sin_ref[pl.ds(seq * 128, 128), :], 0.0)
+                kv_all[seq * HK + head, spot] = (piece * cos + swap_halves(piece, lane) * sin).astype(
                     BF
                 )
-                out_qp[pair, pl.ds(two * 256 + 128, 128), :] = jnp.where(
-                    lane < 64, pltpu.roll(piece, 64, 1), 0.0
-                ).astype(BF)
-        return carry
-
-    lax.fori_loop(0, HK, make_q, 0)
-
-    def pt_copy(pair, block, slot):
-        span = pl.ds(pl.multiple_of(block * 1024, 1024), 1024)
-        return pltpu.make_async_copy(pt_stage.at[slot], out_pt.at[pair, span], pt_sem.at[slot])
-
-    def keys_of(pair, block):
+            return carry
+
+        lax.fori_loop(0, HK, make_kv, 0)
+
+        def kv_slice(seq, l, c):
+            return kv_all.at[pl.ds(seq * HK, HK), l * 2 + c]
+
+        def kv_move(seq, way, src):
+            piece = kv_slice(seq, src, c_id)
+            to = (s_id, lax.rem(l_id + (1 if way == 0 else line - 1), line), c_id)
+            return env.remote(
+                piece, piece, kv_send.at[seq, way * line + src], kv_recv.at[seq, src], to
+            )
+
+        def kv_sib(seq, src):
+            piece = kv_slice(seq, src, c_id)
+            return env.remote(
+                piece, piece, kv_sib_send.at[seq, src], kv_sib_recv.at[seq, src], env.sibling
+            )
+
+        def kv_onward(seq, way, src):
+            @pl.when((l_id < line - 1) if way == 0 else (l_id > 0))
+            def _():
+                kv_move(seq, way, src).start()
+
+        def kv_start(seq):
+            for way in range(2):
+                kv_onward(seq, way, l_id)
+            kv_sib(seq, l_id).start()
+
+        def kv_step(seq, far):
+            for way in range(2):
+                src = l_id - far if way == 0 else l_id + far
+
+                @pl.when((src >= 0) & (src < line))
+                def _():
+                    kv_move(seq, way, src).wait_recv()
+                    kv_onward(seq, way, src)
+                    kv_sib(seq, src).start()
+
+        def kv_finish(seq):
+            for src in range(line):
+                kv_sib(seq, src).wait()
+
+        def kv_settle(seq):
+            for src in range(line):
+
+                @pl.when((l_id < line - 1) & (src <= l_id))
+                def _():
+                    kv_move(seq, 0, src).wait_send()
+
+                @pl.when((l_id > 0) & (src >= l_id))
+                def _():
+                    kv_move(seq, 1, src).wait_send()
+
+        kv_start(0)
+        for load in loads:
+            load.start()
+        load_g.wait()
+        for seq in range(2):
+            rows_ = pl.ds(seq * 128, 128)
+            g_all[s_id, rows_, :] = (
+                g_all[s_id, rows_, :].astype(F32) * info[:, 2 + seq : 3 + seq]
+            ).astype(BF)
+            for group in range(keys // 1024):
+                some = jnp.concatenate(
+                    [
+                        positions_ref[seq : seq + 1, (group * 8 + t) * 128 : (group * 8 + t + 1) * 128]
+                        for t in range(8)
+                    ],
+                    0,
+                )
+                some = jnp.where(some < lengths_ref[seq], some, 1 << 24)
+                key_at = jnp.transpose(some.astype(F32))
+                for t in range(8):
+                    first = (group * 8 + t) * 128
+                    bias_ref[seq, first : first + 128, :] = jnp.where(
+                        key_at[:, t : t + 1] <= spots[seq : seq + 1, :], 0.0, NEGATIVE
+                    )
+        for tile in range(width // 128):
+            piece = norm[:, tile * 128 : tile * 128 + 128].astype(F32)
+            out_n1_t[tile * 128 : tile * 128 + 128, :] = jnp.transpose(piece).astype(BF)
+        q_gather.forward()
+        o_gather.start()
+        kv_step(0, 1)
+        if line == 2:
+            kv_start(1)
+        else:
+            kv_step(0, 2)
+            kv_start(1)
+        q_gather.collect()
+        q_gather.finish()
+
+        def make_q(head, carry):
+            block = nn(norm[...], wq_all[:, pl.ds(pl.multiple_of(head * 256, 256), 256)])
+            for seq in range(2):
+                cos = cos_ref[pl.ds(seq * 128, 128), :]
+                sin = sin_ref[pl.ds(seq * 128, 128), :]
+                for two in range(2):
+                    piece = block[seq * 128 : seq * 128 + 128, two * 128 : two * 128 + 128]
+                    piece = piece * cos + swap_halves(piece, lane) * sin
+                    piece = piece.astype(BF).astype(F32) * (1.0 / math.sqrt(HD))
+                    pair = seq * HK + head
+                    out_qp[pair, pl.ds(two * 256, 128), :] = jnp.where(lane < 64, piece, 0.0).astype(
+                        BF
+                    )
+                    out_qp[pair, pl.ds(two * 256 + 128, 128), :] = jnp.where(
+                        lane < 64, pltpu.roll(piece, 64, 1), 0.0
+                    ).astype(BF)
+            return carry
+
+        lax.fori_loop(0, HK, make_q, 0)
+
+        def pt_copy(pair, block, slot):
+            span = pl.ds(pl.multiple_of(block * 1024, 1024), 1024)
+            return pltpu.make_async_copy(pt_stage.at[slot], out_pt.at[pair, span], pt_sem.at[slot])
+
+        def keys_of(pair, block):
+            if blocks == 1:
+                return kv_all[pair].reshape(1024, 128)
+            return kv_all[pair, pl.ds(block * 8, 8)].reshape(1024, 128)
+
+        def scores(pair, block):
+            span = pl.ds(pl.multiple_of(block * 1024, 1024), 1024)
+            bias = bias_ref[pair // HK, span, :]
+            return nt(keys_of(pair, block), out_qp[pair]) + jnp.concatenate([bias] * GROUP, 1)
+
+        def attend(pair, carry):
+            if blocks == 1:
+                slot = lax.rem(pair, 2)
+
+                @pl.when(pair >= 2)
+                def _():
+                    pt_copy(pair - 2, 0, slot).wait()
+
+                value = scores(pair, 0)
+                top = jnp.max(value, 0, keepdims=True)
+                weight = jnp.exp(value - top)
+                inverse = 1.0 / jnp.sum(weight, 0, keepdims=True)
+                soft = (weight * inverse).astype(BF)
+                pt_stage[slot] = soft
+                pt_copy(pair, 0, slot).start()
+                mixed = tn(keys_of(pair, 0), soft)[HD:]
+            else:
+
+                def first(block, state):
+                    top, total = state
+                    value = scores(pair, block)
+                    new = jnp.maximum(top, jnp.max(value, 0, keepdims=True))
+                    total = total * jnp.exp(top - new) + jnp.sum(
+                        jnp.exp(value - new), 0, keepdims=True
+                    )
+                    return new, total
+
+                top, total = lax.fori_loop(
+                    0,
+                    blocks,
+                    first,
+                    (jnp.full((1, 512), NEGATIVE, F32), jnp.zeros((1, 512), F32)),
+                )
+                inverse = 1.0 / total
+
+                def second(block, mixed):
+                    pt_stage[0] = (jnp.exp(scores(pair, block) - top) * inverse).astype(BF)
+                    copy = pt_copy(pair, block, 0)
+                    copy.start()
+                    mixed = mixed + tn(keys_of(pair, block), pt_stage[0])[HD:]
+                    copy.wait()
+                    return mixed
+
+                mixed = lax.fori_loop(0, blocks, second, jnp.zeros((HD, 512), F32))
+            seq, head = pair // HK, pair % HK
+            for two in range(2):
+                both = jnp.concatenate(
+                    [
+                        mixed[:, two * 256 : two * 256 + 128],
+                        mixed[:, two * 256 + 128 : two * 256 + 256],
+                    ],
+                    0,
+                )
+                tokens_ = pl.ds(pl.multiple_of(seq * 128, 128), 128)
+                cols = pl.ds(pl.multiple_of(head * 256 + two * 128, 128), 128)
+                out_attn_t[cols, tokens_] = both.astype(BF)
+                out_attn[tokens_, cols] = jnp.transpose(both).astype(BF)
+            return carry
+
+        for far in range(3, line):
+            kv_step(0, far)
+        o_gather.forward()
+        grad_gather.start()
+        kv_step(1, 1)
+        kv_finish(0)
+        lax.fori_loop(0, 2, attend, 0)
+        if line > 2:
+            kv_step(1, 2)
+        lax.fori_loop(2, HK, attend, 0)
+        for far in range(3, line):
+            kv_step(1, far)
+        o_gather.collect()
+        kv_finish(1)
+        lax.fori_loop(HK, 2 * HK, attend, 0)
+        o_gather.finish()
+
+        def project(tile, carry):
+            cols = pl.ds(pl.multiple_of(tile * 256, 256), 256)
+            out_mid[:, cols] = x_ref[:, cols].astype(F32) + nn(out_attn[...], wo_all[:, cols])
+            return carry
+
+        lax.fori_loop(0, width // 256, project, 0)
+        middle = out_mid[...]
+        scale_two = lax.rsqrt(jnp.mean(middle * middle, -1, keepdims=True) + EPSILON)
+        n2_all[s_id] = (middle * scale_two * out_gains[1:2, :]).astype(BF)
+        n2_gather.start()
+        grad_gather.forward()
+        for copy in outs:
+            copy.start()
         if blocks == 1:
-            return kv_all[pair].reshape(1024, 128)
-        return kv_all[pair, pl.ds(block * 8, 8)].reshape(1024, 128)
-
-    def scores(pair, block):
-        span = pl.ds(pl.multiple_of(block * 1024, 1024), 1024)
-        bias = bias_ref[pair // HK, span, :]
-        return nt(keys_of(pair, block), out_qp[pair]) + jnp.concatenate([bias] * GROUP, 1)
-
-    def attend(pair, carry):
-        if blocks == 1:
-            slot = lax.rem(pair, 2)
-
-            @pl.when(pair >= 2)
+            pt_copy(2 * HK - 2, 0, 0).wait()
+            pt_copy(2 * HK - 1, 0, 1).wait()
+
+        def finish():
+            for gather in (kv_gather, q_gather, o_gather):
+                gather.settle()
+            kv_settle(0)
+            kv_settle(1)
+            for copy in outs:
+                copy.wait()
+
+        finishing.append(finish)
+
+    v = pltpu.VMEM
+    finishing = []
+    attention_part()
+
+    def feed_part(inner, dgate, dup, stage, part_stage, n2_t, inner_t):
+        def back_copy(k, slot):
+            return pltpu.make_async_copy(
+                stage.at[slot], out_back.at[peer_of(s_id, shards, k, True)], back_sem.at[slot]
+            )
+
+        def part_copy(k, slot):
+            return pltpu.make_async_copy(
+                part_stage.at[slot], out_parts.at[peer_of(s_id, shards, k, True)], part_sem.at[slot]
+            )
+
+        def outs(k):
+            source = peer_of(s_id, shards, k, True)
+            cols = pl.ds(pl.multiple_of(source * rows, 128), rows)
+            return [
+                pltpu.make_async_copy(n2_t.at[k], out_n2_t.at[:, cols], out_sem.at[k, 0]),
+                pltpu.make_async_copy(inner_t.at[k], out_inner_t.at[:, cols], out_sem.at[k, 1]),
+                pltpu.make_async_copy(dgate.at[source], out_dgate.at[source], out_sem.at[k, 2]),
+                pltpu.make_async_copy(dup.at[source], out_dup.at[source], out_sem.at[k, 3]),
+                pltpu.make_async_copy(g_all.at[source], out_g.at[source], out_sem.at[k, 4]),
+            ]
+
+        def project(k):
+            slot = lax.rem(k, 2)
+
+            @pl.when(k >= 2)
             def _():
-                pt_copy(pair - 2, 0, slot).wait()
-
-            value = scores(pair, 0)
-            top = jnp.max(value, 0, keepdims=True)
-            weight = jnp.exp(value - top)
-            inverse = 1.0 / jnp.sum(weight, 0, keepdims=True)
-            soft = (weight * inverse).astype(BF)
-            pt_stage[slot] = soft
-            pt_copy(pair, 0, slot).start()
-            mixed = tn(keys_of(pair, 0), soft)[HD:]
-        else:
-
-            def first(block, state):
-                top, total = state
-                value = scores(pair, block)
-                new = jnp.maximum(top, jnp.max(value, 0, keepdims=True))
-                total = total * jnp.exp(top - new) + jnp.sum(
-                    jnp.exp(value - new), 0, keepdims=True
-                )
-                return new, total
-
-            top, total = lax.fori_loop(
-                0,
-                blocks,
-                first,
-                (jnp.full((1, 512), NEGATIVE, F32), jnp.zeros((1, 512), F32)),
-            )
-            inverse = 1.0 / total
-
-            def second(block, mixed):
-                pt_stage[0] = (jnp.exp(scores(pair, block) - top) * inverse).astype(BF)
-                copy = pt_copy(pair, block, 0)
+                part_copy(k - 2, slot).wait()
+
+            part_stage[slot] = nn(inner[peer_of(s_id, shards, k, True)], wd[...]).astype(BF)
+            part_copy(k, slot).start()
+
+        def block(k, carry):
+            source = peer_of(s_id, shards, k, True)
+            slot = lax.rem(k, 2)
+            if n2_gather.relay:
+
+                @pl.when(k == 1)
+                def _():
+                    n2_gather.forward()
+
+                @pl.when(k == 3)
+                def _():
+                    n2_gather.collect()
+                    grad_gather.collect()
+
+            else:
+
+                @pl.when(k > 0)
+                def _():
+                    n2_gather.copy(k).wait_recv()
+
+            normed = n2_all[source]
+            gate, upper = nn(normed, wg[...]), nn(normed, wu[...])
+
+            @pl.when(k == 0)
+            def _():
+                loads[2].wait()
+
+            grad = g_all[source]
+            grad_inner = nt(grad, wd[...])
+            sig = 1.0 / (1.0 + jnp.exp(-gate))
+            act = gate * sig
+            inner[source] = (act * upper).astype(BF)
+            dgate[source] = (grad_inner * upper * sig * (1.0 + gate * (1.0 - sig))).astype(BF)
+            dup[source] = (grad_inner * act).astype(BF)
+
+            @pl.when(k >= 2)
+            def _():
+                back_copy(k - 2, slot).wait()
+
+            stage[slot] = (nt(dgate[source], wg[...]) + nt(dup[source], wu[...])).astype(BF)
+            back_copy(k, slot).start()
+            n2_t[k] = jnp.transpose(normed)
+            inner_t[k] = jnp.transpose(inner[source])
+            for copy in outs(k):
                 copy.start()
-                mixed = mixed + tn(keys_of(pair, block), pt_stage[0])[HD:]
+
+            @pl.when(k > 0)
+            def _():
+                project(k - 1)
+
+            return carry
+
+        loads[0].wait()
+        loads[1].wait()
+        lax.fori_loop(0, shards, block, 0)
+        project(shards - 1)
+        for k in range(shards):
+            for copy in outs(k):
                 copy.wait()
-                return mixed
-
-            mixed = lax.fori_loop(0, blocks, second, jnp.zeros((HD, 512), F32))
-        seq, head = pair // HK, pair % HK
-        for two in range(2):
-            both = jnp.concatenate(
-                [
-                    mixed[:, two * 256 : two * 256 + 128],
-                    mixed[:, two * 256 + 128 : two * 256 + 256],
-                ],
-                0,
-            )
-            tokens_ = pl.ds(pl.multiple_of(seq * 128, 128), 128)
-            cols = pl.ds(pl.multiple_of(head * 256 + two * 128, 128), 128)
-            out_attn_t[cols, tokens_] = both.astype(BF)
-            out_attn[tokens_, cols] = jnp.transpose(both).astype(BF)
-        return carry
-
-    for far in range(3, line):
-        kv_step(0, far)
-    o_gather.forward()
-    grad_gather.start()
-    kv_step(1, 1)
-    kv_finish(0)
-    lax.fori_loop(0, 2, attend, 0)
-    if line > 2:
-        kv_step(1, 2)
-    lax.fori_loop(2, HK, attend, 0)
-    for far in range(3, line):
-        kv_step(1, far)
-    o_gather.collect()
-    kv_finish(1)
-    lax.fori_loop(HK, 2 * HK - 2, attend, 0)
-    grad_gather.forward()
-    lax.fori_loop(2 * HK - 2, 2 * HK, attend, 0)
-    outs = [
-        pltpu.make_async_copy(wkv_all, out_wkv, out_sem.at[0]),
-        pltpu.make_async_copy(wq_all, out_wq, out_sem.at[1]),
-        pltpu.make_async_copy(kv_all, out_kv, out_sem.at[2]),
-    ]
-    for copy in outs:
-        copy.start()
-    o_gather.finish()
-    outs.append(pltpu.make_async_copy(wo_all, out_wo, out_sem.at[3]))
-    outs[3].start()
-
-    def project(tile, carry):
-        cols = pl.ds(pl.multiple_of(tile * 256, 256), 256)
-        out_mid[:, cols] = x_ref[:, cols].astype(F32) + nn(out_attn[...], wo_all[:, cols])
-        return carry
-
-    lax.fori_loop(0, width // 256, project, 0)
-    middle = out_mid[...]
-    scale_two = lax.rsqrt(jnp.mean(middle * middle, -1, keepdims=True) + EPSILON)
-    out_n2[...] = (middle * scale_two * out_gains[1:2, :]).astype(BF)
-    if blocks == 1:
-        pt_copy(2 * HK - 2, 0, 0).wait()
-        pt_copy(2 * HK - 1, 0, 1).wait()
-    grad_gather.collect()
-    for gather in (kv_gather, q_gather, o_gather, grad_gather):
-        gather.settle()
-    kv_settle(0)
-    kv_settle(1)
-    keep_g.wait()
-    for copy in outs:
-        copy.wait()
+        n2_gather.settle()
+        grad_gather.settle()
+        for last in (2, 1):
+            part_copy(shards - last, (shards - last) % 2).wait()
+            back_copy(shards - last, (shards - last) % 2).wait()
+
+    pl.run_scoped(
+        feed_part,
+        v((shards, rows, feed), BF),
+        v((shards, rows, feed), BF),
+        v((shards, rows, feed), BF),
+        v((2, rows, width), BF),
+        v((2, rows, width), BF),
+        v((shards, width, rows), BF),
+        v((shards, feed, rows), BF),
+    )
+    finishing[0]()
 
 
 def front_call(shards, line, *arrays):
-    info, keys_at, x, wkv = arrays[0], arrays[1], arrays[5], arrays[8]
+    positions, x, w_gate = arrays[0], arrays[6], arrays[10]
     rows, width = x.shape
-    keys = keys_at.shape[1] * 128
-    kv_width = wkv.shape[1]
+    keys = positions.shape[1]
+    feed = w_gate.shape[1]
+    kv_width = 2 * HK * HD
     dma = pltpu.SemaphoreType.DMA
     v = pltpu.VMEM
     vm = pl.BlockSpec(memory_space=pltpu.VMEM)
+    sm = pl.BlockSpec(memory_space=pltpu.SMEM)
     hbm = pl.BlockSpec(memory_space=pltpu.HBM)
     part = width // shards
     shape = jax.ShapeDtypeStruct
     hops = max(5, shards)
     return pl.pallas_call(
-        lambda *refs: front_kernel((shards, line, keys, rows, width), *refs),
+        lambda *refs: front_kernel((shards, line, keys, rows, width, feed), *refs),
         out_shape=(
-            shape((rows, width), BF),
-            shape((width, rows), BF),
-            shape((width, rows), BF),
-            shape((2 * HK, 512, 128), BF),
-            shape((rows, width), F32),
-            shape((rows, width), BF),
             shape((8, width), F32),
             shape((rows, 128), F32),
             shape((rows, 128), F32),
@@ -556,201 +735,12 @@
             shape((width, width), BF),
             shape((2 * HK, 2 * line, 128, 128), BF),
             shape((2 * HK, keys, 512), BF),
-            shape((shards * rows, width), BF),
-        ),
-        in_specs=[vm] * 5 + [hbm] * 5,
-        out_specs=(*[vm] * 9, *[hbm] * 6),
-        scratch_shapes=[
-            v((width, width), BF),
-            v((width, kv_width), BF),
-            v((width, width), BF),
-            v((2 * HK, 2 * line, 128, 128), BF),
-            v((rows, width), BF),
-            v((rows, width), BF),
-            v((rows, width), BF),
-            v((2, keys, 128), F32),
-            v((8, part), F32),
-            v((shards, 8, part), F32),
-            v((2, 1024, 512), BF),
-            dma((shards,)),
-            dma((shards,)),
-            *[dma((hops,)) for _ in range(12)],
-            dma((hops,)),
-            dma((hops,)),
-            dma((2, 2 * line)),
-            dma((2, line)),
-            dma((2, line)),
-            dma((2, line)),
-            dma((2,)),
-            dma((6,)),
-        ],
-        compiler_params=pltpu.CompilerParams(
-            collective_id=1, has_side_effects=True, vmem_limit_bytes=VMEM_LIMIT
-        ),
-        name="front",
-    )(*arrays)
-
-
-def feed_kernel(
-    sizes,
-    n2_ref,
-    g_hbm,
-    wg_hbm,
-    wu_hbm,
-    wd_hbm,
-    out_parts,
-    out_back,
-    out_n2_t,
-    out_inner_t,
-    out_dgate,
-    out_dup,
-    n2_all,
-    g_all,
-    wg,
-    wu,
-    wd,
-    inner,
-    dgate,
-    dup,
-    stage,
-    part_stage,
-    n2_t,
-    inner_t,
-    load_sem,
-    n2_send,
-    n2_recv,
-    part_sem,
-    back_sem,
-    out_sem,
-):
-    shards, rows, width, feed = sizes
-    env = Env(shards, 1)
-    s_id = env.s_id
-    env.barrier([env.peer(k) for k in range(1, shards)])
-
-    def n2_rows(s, core, first, count):
-        return n2_all.at[s, pl.ds(first * (rows // 2), count * (rows // 2))]
-
-    gather = Spread(env, n2_rows, n2_ref, (n2_send, n2_recv, None, None), False)
-    gather.start()
-    loads = [
-        pltpu.make_async_copy(src, dst, load_sem.at[i])
-        for i, (src, dst) in enumerate(
-            ((wg_hbm, wg), (wu_hbm, wu), (g_hbm, g_all), (wd_hbm, wd))
-        )
-    ]
-    for load in loads:
-        load.start()
-    n2_all[s_id] = n2_ref[...]
-    loads[0].wait()
-    loads[1].wait()
-
-    def back_copy(k, slot):
-        return pltpu.make_async_copy(
-            stage.at[slot], out_back.at[peer_of(s_id, shards, k, True)], back_sem.at[slot]
-        )
-
-    def part_copy(k, slot):
-        return pltpu.make_async_copy(
-            part_stage.at[slot], out_parts.at[peer_of(s_id, shards, k, True)], part_sem.at[slot]
-        )
-
-    def outs(k):
-        source = peer_of(s_id, shards, k, True)
-        cols = pl.ds(pl.multiple_of(source * rows, 128), rows)
-        return [
-            pltpu.make_async_copy(n2_t.at[k], out_n2_t.at[:, cols], out_sem.at[k, 0]),
-            pltpu.make_async_copy(inner_t.at[k], out_inner_t.at[:, cols], out_sem.at[k, 1]),
-            pltpu.make_async_copy(dgate.at[source], out_dgate.at[source], out_sem.at[k, 2]),
-            pltpu.make_async_copy(dup.at[source], out_dup.at[source], out_sem.at[k, 3]),
-        ]
-
-    def project(k):
-        slot = lax.rem(k, 2)
-
-        @pl.when(k >= 2)
-        def _():
-            part_copy(k - 2, slot).wait()
-
-        part_stage[slot] = nn(inner[peer_of(s_id, shards, k, True)], wd[...]).astype(BF)
-        part_copy(k, slot).start()
-
-    def block(k, carry):
-        source = peer_of(s_id, shards, k, True)
-        slot = lax.rem(k, 2)
-        if gather.relay:
-
-            @pl.when(k == 1)
-            def _():
-                gather.forward()
-
-            @pl.when(k == 3)
-            def _():
-                gather.passing(1).wait_recv()
-                gather.passing(2).wait_recv()
-
-        else:
-
-            @pl.when(k > 0)
-            def _():
-                gather.copy(k).wait_recv()
-
-        normed = n2_all[source]
-        gate, upper = nn(normed, wg[...]), nn(normed, wu[...])
-
-        @pl.when(k == 0)
-        def _():
-            loads[2].wait()
-            loads[3].wait()
-
-        grad = g_all[source]
-        grad_inner = nt(grad, wd[...])
-        sig = 1.0 / (1.0 + jnp.exp(-gate))
-        act = gate * sig
-        inner[source] = (act * upper).astype(BF)
-        dgate[source] = (grad_inner * upper * sig * (1.0 + gate * (1.0 - sig))).astype(BF)
-        dup[source] = (grad_inner * act).astype(BF)
-
-        @pl.when(k >= 2)
-        def _():
-            back_copy(k - 2, slot).wait()
-
-        stage[slot] = (nt(dgate[source], wg[...]) + nt(dup[source], wu[...])).astype(BF)
-        back_copy(k, slot).start()
-        n2_t[k] = jnp.transpose(normed)
-        inner_t[k] = jnp.transpose(inner[source])
-        for copy in outs(k):
-            copy.start()
-
-        @pl.when(k > 0)
-        def _():
-            project(k - 1)
-
-        return carry
-
-    lax.fori_loop(0, shards, block, 0)
-    project(shards - 1)
-    for k in range(shards):
-        for copy in outs(k):
-            copy.wait()
-    gather.settle()
-    for last in (2, 1):
-        part_copy(shards - last, (shards - last) % 2).wait()
-        back_copy(shards - last, (shards - last) % 2).wait()
-
-
-def feed_call(shards, n2, grad_all, w_gate, w_up, w_down):
-    rows, width = n2.shape
-    feed = w_gate.shape[1]
-    dma = pltpu.SemaphoreType.DMA
-    v = pltpu.VMEM
-    vm = pl.BlockSpec(memory_space=pltpu.VMEM)
-    hbm = pl.BlockSpec(memory_space=pltpu.HBM)
-    shape = jax.ShapeDtypeStruct
-    hops = max(5, shards)
-    return pl.pallas_call(
-        lambda *refs: feed_kernel((shards, rows, width, feed), *refs),
-        out_shape=(
+            shape((shards, rows, width), BF),
+            shape((rows, width), BF),
+            shape((width, rows), BF),
+            shape((width, rows), BF),
+            shape((2 * HK, 512, 128), BF),
+            shape((rows, width), F32),
             shape((shards, rows, width), BF),
             shape((shards, rows, width), BF),
             shape((width, shards * rows), BF),
@@ -758,33 +748,95 @@
             shape((shards, rows, feed), BF),
             shape((shards, rows, feed), BF),
         ),
-        in_specs=[vm] + [hbm] * 4,
-        out_specs=tuple([hbm] * 6),
+        in_specs=[vm, sm, vm, vm, vm, vm] + [hbm] * 7,
+        out_specs=(*[vm] * 3, *[hbm] * 17),
         scratch_shapes=[
+            v((width, width), BF),
+            v((width, kv_width), BF),
+            v((width, width), BF),
+            v((2 * HK, 2 * line, 128, 128), BF),
             v((shards, rows, width), BF),
             v((shards, rows, width), BF),
             v((width, feed), BF),
             v((width, feed), BF),
             v((feed, width), BF),
-            v((shards, rows, feed), BF),
-            v((shards, rows, feed), BF),
-            v((shards, rows, feed), BF),
-            v((2, rows, width), BF),
-            v((2, rows, width), BF),
-            v((shards, width, rows), BF),
-            v((shards, feed, rows), BF),
+            v((rows, width), BF),
+            v((width, rows), BF),
+            v((width, rows), BF),
+            v((2 * HK, 512, 128), BF),
+            v((rows, width), F32),
+            v((rows, width), BF),
+            v((rows, width), BF),
+            v((2, keys, 128), F32),
+            v((2, 1024, 512), BF),
+            v((8, part), F32),
+            v((shards, 8, part), F32),
+            dma((shards,)),
+            dma((shards,)),
+            *[dma((hops,)) for _ in range(16)],
+            dma((2, 2 * line)),
+            dma((2, line)),
+            dma((2, line)),
+            dma((2, line)),
+            dma((2,)),
             dma((4,)),
-            dma((hops,)),
-            dma((hops,)),
+            dma((3,)),
+            dma((9,)),
             dma((2,)),
             dma((2,)),
-            dma((shards, 4)),
+            dma((shards, 5)),
         ],
         compiler_params=pltpu.CompilerParams(
-            collective_id=2, has_side_effects=True, vmem_limit_bytes=VMEM_LIMIT
+            collective_id=1, has_side_effects=True, vmem_limit_bytes=VMEM_LIMIT
         ),
-        name="feed",
-    )(n2, grad_all, w_gate, w_up, w_down)
+        name="front",
+    )(*arrays)
+
+
+def widen_kernel(count, *refs):
+    src, dst = refs[:count], refs[count : 2 * count]
+    narrow = refs[2 * count : 3 * count]
+    wide = refs[3 * count : 4 * count]
+    load_sem, store_sem = refs[4 * count :]
+    for i in range(count):
+        pltpu.make_async_copy(src[i], narrow[i], load_sem.at[i]).start()
+
+    def piece(i, part, parts):
+        rows = narrow[i].shape[0] // parts
+        span = pl.ds(part * rows, rows)
+        held = wide[i] if dst[i].dtype == F32 else narrow[i]
+        return span, pltpu.make_async_copy(held.at[span], dst[i].at[span], store_sem.at[i, part])
+
+    for i in range(count):
+        pltpu.make_async_copy(src[i], narrow[i], load_sem.at[i]).wait()
+        for part in range(4):
+            span, copy = piece(i, part, 4)
+            if dst[i].dtype == F32:
+                wide[i][span, :] = narrow[i][span, :].astype(F32)
+            copy.start()
+    for i in range(count):
+        for part in range(4):
+            piece(i, part, 4)[1].wait()
+
+
+def widen_call(arrays, types):
+    v = pltpu.VMEM
+    hbm = pl.BlockSpec(memory_space=pltpu.HBM)
+    count = len(arrays)
+    return pl.pallas_call(
+        lambda *refs: widen_kernel(count, *refs),
+        out_shape=tuple(jax.ShapeDtypeStruct(a.shape, t) for a, t in zip(arrays, types)),
+        in_specs=[hbm] * count,
+        out_specs=tuple([hbm] * count),
+        scratch_shapes=[
+            *[v(a.shape, a.dtype) for a in arrays],
+            *[v(a.shape if t == F32 else (16, 128), F32) for a, t in zip(arrays, types)],
+            pltpu.SemaphoreType.DMA((count,)),
+            pltpu.SemaphoreType.DMA((count, 4)),
+        ],
+        compiler_params=pltpu.CompilerParams(vmem_limit_bytes=VMEM_LIMIT),
+        name="widen",
+    )(*arrays)
 
 
 def add_rows(target, parts, rows, step):
@@ -827,7 +879,8 @@
     out_dn,
     out_wo,
     out_wq,
-    out_wkv,
+    out_wk,
+    out_wv,
     out_gain,
     out_dx,
     out_result,
@@ -863,6 +916,8 @@
     gn_z,
     gn_r,
     gn_t,
+    k_nat,
+    gn_out,
     load_sem,
     pt_sem,
     kv_sem,
@@ -907,7 +962,10 @@
     env.barrier([sibling] + peers + mates)
 
     half = width // 2
-    chunks = 12
+    wide_pieces = 8
+    down_pieces = 8 if feed % 128 == 0 else 4
+    chunks = 2 * wide_pieces + down_pieces
+    turns = 12
     slab = 16
     part = width // shards
     own_rows = part // 2
@@ -943,8 +1001,8 @@
 
     def views(index, where):
         if where != "dn":
-            rows_ = half // 4
-            array, piece = (0 if where == "gate" else 1), index % 4
+            rows_ = half // wide_pieces
+            array, piece = (0 if where == "gate" else 1), index % wide_pieces
             array_of = out_gate if where == "gate" else out_up
             span = pl.ds(pl.multiple_of(piece * rows_, 16), rows_)
             bufs = [ref.at[array, span] for ref in (own_gu, got_gu_x, got_gu_r, got_gu_t)]
@@ -954,8 +1012,8 @@
                 return array_of.at[pl.ds(pl.multiple_of(start, 16), rows_)]
 
             return rows_, bufs, out
-        rows_ = feed // 4
-        span = pl.ds(pl.multiple_of((index - 8) * rows_, 16), rows_)
+        rows_ = feed // down_pieces
+        span = pl.ds(pl.multiple_of((index - 2 * wide_pieces) * rows_, 16), rows_)
         bufs = [ref.at[span] for ref in (own_dn, got_dn_x, got_dn_r, got_dn_t)]
 
         def out(core):
@@ -967,11 +1025,11 @@
         def run(index):
             if isinstance(index, int):
                 if 0 <= index < chunks:
-                    action(index, ("gate", "up", "dn")[index // 4])
+                    action(index, ("gate", "up", "dn")[min(2, index // wide_pieces)])
                 return
             for number, where in enumerate(("gate", "up", "dn")):
 
-                @pl.when(index // 4 == number)
+                @pl.when(jnp.minimum(index // wide_pieces, 2) == number)
                 def _():
                     action(index, where)
 
@@ -1025,31 +1083,46 @@
 
     up_end, up_inner, down, settle = [split(f) for f in (up_end, up_inner, down, settle)]
 
+    def of_turns(first, last):
+        return min(2 * first, chunks), min(2 * last, chunks)
+
+    def run_all(action, first, last):
+        if last > first:
+
+            def body(index, carry):
+                action(index)
+                return carry
+
+            lax.fori_loop(first, last, body, 0)
+
     def ends_up(first, last):
         @pl.when(jnp.logical_not(has_outer))
         def _():
-            for index in range(first, last):
-                up_end(index)
-
-    def ring(step, lag=2):
-        @pl.when((step < chunks) & has_outer)
-        def _():
-            up_inner(step)
-
-        @pl.when((step >= lag) & (step < chunks + lag) & is_mid)
-        def _():
-            down(step - lag)
-
-    def ring_down(index):
+            run_all(up_end, *of_turns(first, last))
+
+    def ring(turn, lag=2):
+        for step in (2 * turn, 2 * turn + 1):
+            if step < chunks:
+
+                @pl.when(has_outer)
+                def _():
+                    up_inner(step)
+
+            if 0 <= step - 2 * lag < chunks:
+
+                @pl.when(is_mid)
+                def _():
+                    down(step - 2 * lag)
+
+    def ring_down(turn):
         @pl.when(is_mid)
         def _():
-            down(index)
+            run_all(down, *of_turns(turn, turn + 1))
 
     def ends_down(first, last):
         @pl.when(jnp.logical_not(is_mid))
         def _():
-            for index in range(first, last):
-                down(index)
+            run_all(down, *of_turns(first, last))
 
     def core_send(array, src):
         dst = got_gu_x.at[array] if array < 2 else got_dn_x
@@ -1112,6 +1185,8 @@
         own_back.start()
         stage = []
         for k in range(1, shards):
+            if k == shards - 1:
+                ring(2)
             back_copy(k).wait()
             stage.append(local(b_zone.at[k - 1], g_v.at[k], load_sem.at[k - 1]))
             stage[-1].start()
@@ -1244,7 +1319,7 @@
             def _():
                 remote(mine, came, a_up.at[slot], a_r.at[slot], inner_to).start()
 
-        def line_down(mine, total, slot, count, near, far):
+        def line_down(mine, total, slot, count, ready, outs):
             remote(mine, total, a_up.at[slot], a_t.at[slot], inner_to).wait()
 
             @pl.when(is_mid)
@@ -1255,18 +1330,22 @@
             def _():
                 remote(total, total, a_down.at[slot], a_t.at[slot], outer_to).start()
 
-            if far is not None:
-                remote(total, near, a_sib_send.at[slot], a_sib_recv.at[slot], sibling).start()
-            local(total, near, a_local.at[slot]).start()
-
-        def line_settle(total, slot, near, far):
+            if ready is not None:
+                ready()
+            for src, near, far, box in outs:
+                if far is not None:
+                    remote(src, near, a_sib_send.at[box], a_sib_recv.at[box], sibling).start()
+                local(src, near, a_local.at[box]).start()
+
+        def line_settle(total, slot, outs):
             @pl.when(has_outer)
             def _():
                 remote(total, total, a_down.at[slot], a_t.at[slot], outer_to).wait_send()
 
-            if far is not None:
-                remote(total, far, a_sib_send.at[slot], a_sib_recv.at[slot], sibling).wait()
-            local(total, near, a_local.at[slot]).wait()
+            for src, near, far, box in outs:
+                if far is not None:
+                    remote(src, far, a_sib_send.at[box], a_sib_recv.at[box], sibling).wait()
+                local(src, near, a_local.at[box]).wait()
 
         lane = lanes_of(128)
         dproj[...] = gm[...].astype(BF)
@@ -1303,7 +1382,7 @@
 
         lax.fori_loop(0, HK, spread, 0)
         load_wq.start()
-        ring(2)
+        ring(3)
 
         def weight_grad(left, right, grad, count):
             def body(s, carry):
@@ -1496,28 +1575,57 @@
         far = (1 - c_id) * own_rows
         pieces = 2 if own_rows % 32 == 0 else 1
 
-        def jobs_of(box, came, total, out, slot):
+        def jobs_of(box, came, total, slot, outs_of):
             count = own_rows // pieces
             result = []
             for piece in range(pieces):
                 span = pl.ds(piece * count, count)
+
+                def rows_at(out, start, piece=piece):
+                    return out.at[pl.ds(pl.multiple_of(start + piece * count, 16), count)]
+
+                ready, outs = outs_of(total.at[span], span, slot + piece, rows_at)
                 result.append(
-                    (
-                        box.at[s_id, span],
-                        came.at[span],
-                        total.at[span],
-                        slot + piece,
-                        count,
-                        out.at[pl.ds(pl.multiple_of(near + piece * count, 16), count)],
-                        out.at[pl.ds(pl.multiple_of(far + piece * count, 16), count)],
-                    )
+                    (box.at[s_id, span], came.at[span], total.at[span], slot + piece, count)
+                    + (ready, outs)
                 )
             return result
 
-        o_jobs = jobs_of(o_x, o_r, o_t, out_wo, 0)
-        q_jobs = jobs_of(q_x, q_r, q_t, out_wq, 2)
-        k_jobs = jobs_of(k_x, k_r, k_t, out_wkv, 4)
-        gain_job = [(gn_x, gn_r, gn_t, 6, 8, out_gain, None)]
+        def plain(out):
+            def outs_of(total, span, slot, rows_at):
+                return None, [(total, rows_at(out, near), rows_at(out, far), slot)]
+
+            return outs_of
+
+        def unpacked(total, span, slot, rows_at):
+            def ready():
+                value = total[...].astype(F32)
+                for half_, first in ((0, 0), (1, HD)):
+                    k_nat[half_, span, :] = jnp.concatenate(
+                        [
+                            value[:, head * 128 + first : head * 128 + first + HD]
+                            for head in range(HK)
+                        ],
+                        1,
+                    ).astype(BF)
+
+            outs = [
+                (k_nat.at[half_, span], rows_at(out, near), rows_at(out, far), slot + 3 * half_)
+                for half_, out in ((0, out_wk), (1, out_wv))
+            ]
+            return ready, outs
+
+        def own_gain():
+            value = gn_t[...]
+            chosen = value[:, 0:part]
+            for s in range(1, shards):
+                chosen = jnp.where(s_id == s, value[:, s * part : (s + 1) * part], chosen)
+            gn_out[...] = chosen
+
+        o_jobs = jobs_of(o_x, o_r, o_t, 0, plain(out_wo))
+        q_jobs = jobs_of(q_x, q_r, q_t, 2, plain(out_wq))
+        k_jobs = jobs_of(k_x, k_r, k_t, 4, unpacked)
+        gain_job = [(gn_x, gn_r, gn_t, 6, 8, own_gain, [(gn_out, out_gain, None, 6)])]
         jobs = o_jobs + q_jobs + gain_job + k_jobs
 
         def first_up(some):
@@ -1534,15 +1642,15 @@
                 line_up(mine, came, total, slot, count)
 
         def job_down(job):
-            mine, _, total, slot, count, to, other = job
-            line_down(mine, total, slot, count, to, other)
+            mine, _, total, slot, count, ready, outs = job
+            line_down(mine, total, slot, count, ready, outs)
 
         lax.fori_loop(0, 2 * blocks, attend, 0)
+        ring(4)
         scatter_part(g_buf, o_x, o_z, 0)
-        ring(3)
         lax.fori_loop(2 * blocks, HK * blocks, attend, 0)
         dkv_core_copy(0).start()
-        ring(4)
+        ring(5)
         lax.fori_loop(HK * blocks, (HK + 2) * blocks, attend, 0)
         dkv_scatter(0)
         lax.fori_loop((HK + 2) * blocks, total_steps, attend, 0)
@@ -1555,12 +1663,11 @@
                     cos = cosine[where[0], :]
                     sin = sine[where[0], :]
                     dq[where] = (piece * cos - swap_halves(piece, lane) * sin).astype(dq.dtype)
-        ring(5)
+        ring(6)
         weight_grad(n1_t_ref, dq, g_buf, shards)
         core_part(g_buf, q_x, 1).start()
         dkv_scatter(1)
-        ends_up(7, chunks)
-        ring(6)
+        ends_up(7, turns)
         ring_down(5)
         dkv_hops(0)
         scatter_part(g_buf, q_x, q_z, 1)
@@ -1572,6 +1679,7 @@
         load_wkv.wait()
         back = nt(dq[...], w_buf[...])
         ends_down(0, 3)
+        ring(7, 8)
         dkv_gather(0)
         dkv_gather(1)
         g_kv = g_buf.at[:, :, pl.ds(0, 2 * HK * HD)]
@@ -1579,7 +1687,7 @@
         core_part(g_kv, k_x, 2).start()
         back = back + nt(dkv_own[...], wkv_buf[...])
         scatter_part(g_kv, k_x, k_z, 2)
-        ring(7, 8)
+        ring(8, 1)
         hidden = x_ref[...].astype(F32)
         scale = lax.rsqrt(jnp.mean(hidden * hidden, -1, keepdims=True) + EPSILON)
         scaled = back * gains_ref[0:1, :]
@@ -1587,11 +1695,13 @@
         gn_own[2:8, :] = jnp.zeros((6, width), F32)
         gain_core = remote(gn_own, gn_x, g_core.at[6], g_core.at[7], sibling)
         gain_core.start()
-        out_dx[...] = (
+        x_ref[...] = (
             gm[...]
             + scale * scaled
             - hidden * (scale * scale * scale) * jnp.mean(scaled * hidden, -1, keepdims=True)
         ).astype(BF)
+        keep_dx = local(x_ref, out_dx, late_sem.at[1])
+        keep_dx.start()
         gain_core.wait()
         gn_own[...] = gn_own[...] + gn_x[...]
 
@@ -1625,7 +1735,6 @@
 
         @pl.when(has_outer)
         def _():
-            ring(8, 1)
             ring(9, 1)
             gather_part(q_x, q_z, 1)
             ring(10, 1)
@@ -1634,37 +1743,52 @@
             ring(11, 1)
 
         ends_down(3, 8)
+        def finish_result():
+            for k in range(1, shards):
+                part_copy(k).wait()
+            result = mid_ref[...]
+            for first in range(0, shards, 4):
+                stage = [
+                    local(
+                        parts_hbm.at[s_id] if k == 0 else p_zone.at[k - 1],
+                        w_buf.at[pl.ds((k - first) * rows, rows)],
+                        load_sem.at[k - first],
+                    )
+                    for k in range(first, min(shards, first + 4))
+                ]
+                for copy in stage:
+                    copy.start()
+                for k, copy in enumerate(stage):
+                    copy.wait()
+                    result = result + w_buf[k * rows : (k + 1) * rows, :].astype(F32)
+            dproj[...] = result.astype(BF)
+            local(dproj, out_result, late_sem.at[2]).start()
+
         todo = list(jobs)
         done = [todo.pop(0)]
         job_up(done[-1])
-        ring(chunks, 1)
-        ends_down(8, chunks)
+        ring(turns, 1)
+        ends_down(8, turns)
+
+        @pl.when(jnp.logical_not(has_outer))
+        def _():
+            finish_result()
+
         for job in todo:
             job_up(job)
             done.append(job)
             job_down(done.pop(0))
         for job in done:
             job_down(job)
-        for k in range(1, shards):
-            part_copy(k).wait()
-        result = mid_ref[...]
-        for first in range(0, shards, 4):
-            stage = [
-                local(
-                    parts_hbm.at[s_id] if k == 0 else p_zone.at[k - 1],
-                    w_buf.at[pl.ds((k - first) * rows, rows)],
-                    load_sem.at[k - first],
-                )
-                for k in range(first, min(shards, first + 4))
-            ]
-            for copy in stage:
-                copy.start()
-            for k, copy in enumerate(stage):
-                copy.wait()
-                result = result + w_buf[k * rows : (k + 1) * rows, :].astype(F32)
-        out_result[...] = result.astype(BF)
-        for _, _, total, slot, _, to, other in jobs:
-            line_settle(total, slot, to, other)
+
+        @pl.when(has_outer)
+        def _():
+            finish_result()
+
+        for _, _, total, slot, _, _, outs in jobs:
+            line_settle(total, slot, outs)
+        keep_dx.wait()
+        local(dproj, out_result, late_sem.at[2]).wait()
 
     pl.run_scoped(
         attention,
@@ -1732,18 +1856,20 @@
         v((shards - 1, 8, width), F32),
         v((8, width), F32),
         v((8, width), F32),
+        v((2, own_rows, HK * HD), BF),
+        v((8, part), F32),
         dma((max(6, shards),)),
         dma((2,)),
         dma((2,)),
         dma((6,)),
-        *[dma((12,)) for _ in range(7)],
+        *[dma((24,)) for _ in range(7)],
         dma((4,)),
         dma((2, 2 * line)),
         dma((2, 2 * line)),
         dma((8,)),
         dma((4, shards - 1)),
         dma((4, shards - 1)),
-        *[dma((7,)) for _ in range(7)],
+        *[dma((9,)) for _ in range(7)],
         *[dma((shards - 1,)) for _ in range(4)],
         dma((9,)),
     ]
@@ -1755,15 +1881,16 @@
             shape((feed, width), BF),
             shape((part, width), BF),
             shape((part, width), BF),
-            shape((part, kv_width), BF),
-            shape((8, width), F32),
+            shape((part, HK * HD), BF),
+            shape((part, HK * HD), BF),
+            shape((8, part), F32),
             shape((rows, width), BF),
             shape((rows, width), BF),
             shape((shards - 1, rows, width), BF),
             shape((shards - 1, rows, width), BF),
         ),
         in_specs=[vm] * 3 + [hbm] * 18,
-        out_specs=(*[hbm] * 7, vm, vm, hbm, hbm),
+        out_specs=tuple([hbm] * 12),
         scratch_shapes=scratch,
         compiler_params=pltpu.CompilerParams(
             collective_id=3, has_side_effects=True, vmem_limit_bytes=VMEM_LIMIT
@@ -1790,25 +1917,10 @@
     seqs, stretch, width = tokens.shape
     shards, line = lax.axis_size("shard"), lax.axis_size("line")
     rows = seqs * stretch
-    rank = lax.axis_index("line") * 2 + lax.axis_index("core")
-    places = lax.dynamic_slice_in_dim(positions, rank * stretch, stretch, 1)
-    valid = (places < lengths[:, None]).astype(F32)
-    info = jnp.concatenate([places.astype(F32), valid, jnp.zeros((4, stretch), F32)], 0)
-    keys_at = jnp.where(positions < lengths[:, None], positions, 1 << 24).astype(F32)
-    frequency = ROPE_BASE ** (-jnp.arange(HD // 2, dtype=F32) * 2.0 / HD)
-    frequency = jnp.concatenate([frequency] * 4)[None]
-    w_kv = jnp.stack(
-        [w_key.reshape(-1, HK, HD), w_value.reshape(-1, HK, HD)], 2
-    ).reshape(-1, 2 * HK * HD)
-    span = attn_gain.shape[0]
+    frequency = ROPE_BASE ** (-np.arange(HD // 2, dtype=np.float32) * 2.0 / HD)
+    frequency = np.tile(frequency, 4)[None].astype(np.float32)
     x = tokens.reshape(rows, width)
     (
-        attn,
-        attn_t,
-        norm_t,
-        packed_q,
-        middle,
-        norm_two,
         gains,
         cos_wide,
         sin_wide,
@@ -1817,67 +1929,89 @@
         out_all,
         packed_kv,
         soft,
-        grad_low_all,
+        grad_all,
+        attn,
+        attn_t,
+        norm_t,
+        packed_q,
+        middle,
+        parts,
+        back,
+        norm_all_t,
+        inner_t,
+        grad_gate,
+        grad_up,
     ) = front_call(
         shards,
         line,
-        info,
-        keys_at.reshape(seqs, -1, 128),
+        positions,
+        lengths,
         frequency,
-        attn_gain[None],
-        mlp_gain[None],
+        jnp.stack([attn_gain, mlp_gain]),
+        w_key,
+        w_value,
         x,
         cotangent.reshape(rows, width),
         w_query,
-        w_kv,
         w_out,
+        w_gate,
+        w_up,
+        w_down,
     )
-    packed_kv = packed_kv.reshape(seqs * HK, -1, 128)
-    grad_low_all = grad_low_all.reshape(shards, rows, width)
-    parts, back, norm_all_t, inner_t, grad_gate, grad_up = feed_call(
-        shards, norm_two, grad_low_all, w_gate, w_up, w_down
+    (
+        sum_gate,
+        sum_up,
+        sum_down,
+        sum_out,
+        sum_query,
+        sum_key,
+        sum_value,
+        sum_gain,
+        grad_input,
+        result,
+        _,
+        _,
+    ) = backward_call(
+        shards,
+        line,
+        gains,
+        cos_wide,
+        sin_wide,
+        attn,
+        attn_t,
+        packed_q,
+        norm_t,
+        x,
+        middle,
+        parts,
+        back,
+        norm_all_t,
+        grad_all,
+        inner_t,
+        grad_gate,
+        grad_up,
+        out_all,
+        wq_all,
+        wkv_all,
+        soft,
+        packed_kv.reshape(seqs * HK, -1, 128),
     )
-    sum_gate, sum_up, sum_down, sum_out, sum_query, sum_kv, sum_gain, grad_input, result, _, _ = (
-        backward_call(
-            shards,
-            line,
-            gains,
-            cos_wide,
-            sin_wide,
-            attn,
-            attn_t,
-            packed_q,
-            norm_t,
-            x,
-            middle,
-            parts,
-            back,
-            norm_all_t,
-            grad_low_all,
-            inner_t,
-            grad_gate,
-            grad_up,
-            out_all,
-            wq_all,
-            wkv_all,
-            soft,
-            packed_kv,
-        )
-    )
-    sum_kv = sum_kv.reshape(-1, HK, 2, HD)
-    sum_gain = lax.dynamic_slice_in_dim(sum_gain, lax.axis_index("shard") * span, span, 1)
+    arrays = [sum_gate, sum_up, sum_down, sum_query, sum_out, sum_key, sum_value]
+    arrays = widen_call(arrays + [grad_input, result], [F32] * 7 + [BF] * 2)
+    sum_gate, sum_up, sum_down, sum_query, sum_out, sum_key, sum_value = arrays[:7]
+    grad_input, result = arrays[7:]
     return (
         result.reshape(seqs, stretch, width),
         grad_input.reshape(seqs, stretch, width),
         sum_gain[0],
-        sum_query.astype(F32),
-        sum_kv[:, :, 0].reshape(-1, HK * HD).astype(F32),
-        sum_kv[:, :, 1].reshape(-1, HK * HD).astype(F32),
-        sum_out.astype(F32),
+        sum_query,
+        sum_key,
+        sum_value,
+        sum_out,
         sum_gain[1],
-        sum_gate.astype(F32),
-        sum_up.astype(F32),
-        sum_down.astype(F32),
+        sum_gate,
+        sum_up,
+        sum_down,
     )
 
 

time: 291 us -> 259 us (0.89)
  other arithmetic: 12.9 us -> 0.57 us
  local copies, waits for them, and re-layouts: 12 us -> 2.75 us
  Pallas kernels: 264 us -> 255 us
    pallas_call x1, Pallas kernels: 68 us -> 98.1 us  [front_call(): pl.pallas_call(lambda *refs: front_kernel((shards, line, keys, rows, widt...]
    pallas_call x1, Pallas kernels: 36.7 us -> 9.63 us  [widen_call(): pl.pallas_call(lambda *refs: widen_kernel(count, *refs), out_shape=tuple(...]
    pallas_call x1, Pallas kernels: 160 us -> 147 us  [backward_call(): pl.pallas_call(lambda *refs: backward_kernel(sizes, *refs), out_shape=(sh...]
    convert_element_type x8 -> x0, other arithmetic: 11.5 us -> none  [the longest x1 2.48 us: per_device(): sum_down.astype(F32)]
    unnamed x29 -> x0, local copies, waits for them, and re-layouts: 6.97 us -> none
where the time goes in v5:
time: 259 us
  Pallas kernels  255 us (98%)
  local copies, waits for them, and re-layouts  2.75 us (1%)
    pallas_call x1, Pallas kernels, backward_call(): pl.pallas_call(lambda *refs: backward_kernel(sizes, *refs), out_shape=(sh...  147 us
    pallas_call x1, Pallas kernels, front_call(): pl.pallas_call(lambda *refs: front_kernel((shards, line, keys, rows, widt...  98.1 us
    pallas_call x1, Pallas kernels, widen_call(): pl.pallas_call(lambda *refs: widen_kernel(count, *refs), out_shape=tuple(...  9.63 us

profile of v5, /device:TPU:0, one launch (start us, length us, event | category | flops | bytes accessed | tf_op | source)
XLA Modules:
  0.0 259.0 jit_solution(4733458928923444399)
XLA Ops:
  0.6 0.7 stack.9
  1.3 0.7 stack.10
  2.0 0.6 pad_maximum_fusion.refs_3_
  2.6 98.1 %front.1 = (f32[8,1280]{1,0:T(8,128)}, f32[256,128]{1,0:T(8,128)}, f32[256,128]{1,0:T(8,128)}, bf16[1280,1280]{1,0:T(8,128)(2,1)}, bf16[1280,640]{1,0:T(8,128)(2...) custom-call(s32[2,1024]{1,0:T(2,128)} %refs_0_.1, ...), custom_call_target="tpu_custom_call" | custom-call | tf_op jit(solution)/shard_map/front/pallas_call | solution.py:727
  100.6 147.1 %backward.1 = (bf16[1280,896]{1,0:T(8,128)(2,1)}, bf16[1280,896]{1,0:T(8,128)(2,1)}, bf16[896,1280]{1,0:T(8,128)(2,1)}, bf16[320,1280]{1,0:T(8,128)(2,1)}, bf16[...) custom-call(f32[8,1280]{1,0:T(8,128)} %get-tuple-element.50.refs_0_,, ...), custom_call_target="tpu_custom_call" | custom-call | tf_op jit(solution)/shard_map/backward/pallas_call | solution.py:1876
  247.7 1.4 slice_reduce_fusion
  249.1 9.6 %widen.1 = (f32[1280,896]{1,0:T(8,128)}, f32[1280,896]{1,0:T(8,128)}, f32[896,1280]{1,0:T(8,128)}, f32[320,1280]{1,0:T(8,128)}, f32[320,1280]{1,0:T(8,128)}, /*i...) custom-call(bf16[1280,896]{1,0:T(8,128)(2,1)} %get-tuple-element.70.refs_0_, ...), custom_call_target="tpu_custom_call" | custom-call | tf_op jit(solution)/shard_map/widen/pallas_call | solution.py:826

commit v6 on v5

--- a/solution.py
+++ b/solution.py
@@ -158,7 +158,8 @@
     positions_ref,
     lengths_ref,
     freq_ref,
-    gains_in,
+    gain_one_ref,
+    gain_two_ref,
     wk_ref,
     wv_ref,
     x_hbm,
@@ -182,7 +183,7 @@
     keep_n1_t,
     keep_qp,
     keep_mid,
-    out_parts,
+    out_inner,
     out_back,
     out_n2_t,
     out_inner_t,
@@ -258,7 +259,8 @@
         wkv_all[pl.ds(pl.multiple_of(s_id * part, 16), part), head * 128 : head * 128 + 128] = (
             both.astype(BF)
         )
-    gains_ref[0:2, :] = gains_in[...].astype(F32)
+    gains_ref[0:1, :] = gain_one_ref[...].astype(F32).reshape(1, part)
+    gains_ref[1:2, :] = gain_two_ref[...].astype(F32).reshape(1, part)
     gains_ref[2:8, :] = jnp.zeros((6, part), F32)
     env.barrier(
         [env.sibling]
@@ -600,15 +602,10 @@
     finishing = []
     attention_part()
 
-    def feed_part(inner, dgate, dup, stage, part_stage, n2_t, inner_t):
+    def feed_part(inner, dgate, dup, stage, grads, n2_t, inner_t):
         def back_copy(k, slot):
             return pltpu.make_async_copy(
                 stage.at[slot], out_back.at[peer_of(s_id, shards, k, True)], back_sem.at[slot]
-            )
-
-        def part_copy(k, slot):
-            return pltpu.make_async_copy(
-                part_stage.at[slot], out_parts.at[peer_of(s_id, shards, k, True)], part_sem.at[slot]
             )
 
         def outs(k):
@@ -620,23 +617,30 @@
                 pltpu.make_async_copy(dgate.at[source], out_dgate.at[source], out_sem.at[k, 2]),
                 pltpu.make_async_copy(dup.at[source], out_dup.at[source], out_sem.at[k, 3]),
                 pltpu.make_async_copy(g_all.at[source], out_g.at[source], out_sem.at[k, 4]),
+                pltpu.make_async_copy(inner.at[source], out_inner.at[source], out_sem.at[k, 5]),
             ]
-
-        def project(k):
-            slot = lax.rem(k, 2)
-
-            @pl.when(k >= 2)
-            def _():
-                part_copy(k - 2, slot).wait()
-
-            part_stage[slot] = nn(inner[peer_of(s_id, shards, k, True)], wd[...]).astype(BF)
-            part_copy(k, slot).start()
 
         def block(k, carry):
             source = peer_of(s_id, shards, k, True)
             slot = lax.rem(k, 2)
             if n2_gather.relay:
 
+                @pl.when(k == 0)
+                def _():
+                    loads[2].wait()
+
+                @pl.when(k == 3)
+                def _():
+                    grad_gather.collect()
+
+                def grad_of(other, carry):
+                    grads[other] = nt(g_all[peer_of(s_id, shards, other, True)], wd[...])
+                    return carry
+
+                first = jnp.where(k == 0, 0, jnp.where(k == 1, 1, 3))
+                last = jnp.where(k == 0, 1, jnp.where(k == 3, 4, 3))
+                lax.fori_loop(first, last, grad_of, 0)
+
                 @pl.when(k == 1)
                 def _():
                     n2_gather.forward()
@@ -644,28 +648,35 @@
                 @pl.when(k == 3)
                 def _():
                     n2_gather.collect()
-                    grad_gather.collect()
 
             else:
+
+                @pl.when(k == 0)
+                def _():
+                    loads[2].wait()
 
                 @pl.when(k > 0)
                 def _():
                     n2_gather.copy(k).wait_recv()
 
+                grads[0] = nt(g_all[source], wd[...])
+
             normed = n2_all[source]
+            n2_t[k] = jnp.transpose(normed)
+            copies = outs(k)
+            copies[0].start()
+            copies[4].start()
             gate, upper = nn(normed, wg[...]), nn(normed, wu[...])
-
-            @pl.when(k == 0)
-            def _():
-                loads[2].wait()
-
-            grad = g_all[source]
-            grad_inner = nt(grad, wd[...])
+            grad_inner = grads[k if n2_gather.relay else 0]
             sig = 1.0 / (1.0 + jnp.exp(-gate))
             act = gate * sig
             inner[source] = (act * upper).astype(BF)
             dgate[source] = (grad_inner * upper * sig * (1.0 + gate * (1.0 - sig))).astype(BF)
             dup[source] = (grad_inner * act).astype(BF)
+            for index in (2, 3, 5):
+                copies[index].start()
+            inner_t[k] = jnp.transpose(inner[source])
+            copies[1].start()
 
             @pl.when(k >= 2)
             def _():
@@ -673,28 +684,17 @@
 
             stage[slot] = (nt(dgate[source], wg[...]) + nt(dup[source], wu[...])).astype(BF)
             back_copy(k, slot).start()
-            n2_t[k] = jnp.transpose(normed)
-            inner_t[k] = jnp.transpose(inner[source])
-            for copy in outs(k):
-                copy.start()
-
-            @pl.when(k > 0)
-            def _():
-                project(k - 1)
-
             return carry
 
         loads[0].wait()
         loads[1].wait()
         lax.fori_loop(0, shards, block, 0)
-        project(shards - 1)
         for k in range(shards):
             for copy in outs(k):
                 copy.wait()
         n2_gather.settle()
         grad_gather.settle()
         for last in (2, 1):
-            part_copy(shards - last, (shards - last) % 2).wait()
             back_copy(shards - last, (shards - last) % 2).wait()
 
     pl.run_scoped(
@@ -703,7 +703,7 @@
         v((shards, rows, feed), BF),
         v((shards, rows, feed), BF),
         v((2, rows, width), BF),
-        v((2, rows, width), BF),
+        v((shards if shards == 4 else 1, rows, feed), F32),
         v((shards, width, rows), BF),
         v((shards, feed, rows), BF),
     )
@@ -711,7 +711,7 @@
 
 
 def front_call(shards, line, *arrays):
-    positions, x, w_gate = arrays[0], arrays[6], arrays[10]
+    positions, x, w_gate = arrays[0], arrays[7], arrays[11]
     rows, width = x.shape
     keys = positions.shape[1]
     feed = w_gate.shape[1]
@@ -741,14 +741,14 @@
             shape((width, rows), BF),
             shape((2 * HK, 512, 128), BF),
             shape((rows, width), F32),
-            shape((shards, rows, width), BF),
+            shape((shards, rows, feed), BF),
             shape((shards, rows, width), BF),
             shape((width, shards * rows), BF),
             shape((feed, shards * rows), BF),
             shape((shards, rows, feed), BF),
             shape((shards, rows, feed), BF),
         ),
-        in_specs=[vm, sm, vm, vm, vm, vm] + [hbm] * 7,
+        in_specs=[vm, sm, vm, vm, vm, vm, vm] + [hbm] * 7,
         out_specs=(*[vm] * 3, *[hbm] * 17),
         scratch_shapes=[
             v((width, width), BF),
@@ -784,7 +784,7 @@
             dma((9,)),
             dma((2,)),
             dma((2,)),
-            dma((shards, 5)),
+            dma((shards, 6)),
         ],
         compiler_params=pltpu.CompilerParams(
             collective_id=1, has_side_effects=True, vmem_limit_bytes=VMEM_LIMIT
@@ -793,11 +793,14 @@
     )(*arrays)
 
 
-def widen_kernel(count, *refs):
+def widen_kernel(count, gain_ref, *refs):
     src, dst = refs[:count], refs[count : 2 * count]
-    narrow = refs[2 * count : 3 * count]
-    wide = refs[3 * count : 4 * count]
-    load_sem, store_sem = refs[4 * count :]
+    out_one, out_two = refs[2 * count : 2 * count + 2]
+    refs = refs[2 * count + 2 :]
+    narrow, wide = refs[:count], refs[count : 2 * count]
+    load_sem, store_sem = refs[2 * count :]
+    out_one[...] = gain_ref[0:1, :].reshape(out_one.shape)
+    out_two[...] = gain_ref[1:2, :].reshape(out_two.shape)
     for i in range(count):
         pltpu.make_async_copy(src[i], narrow[i], load_sem.at[i]).start()
 
@@ -805,7 +808,7 @@
         rows = narrow[i].shape[0] // parts
         span = pl.ds(part * rows, rows)
         held = wide[i] if dst[i].dtype == F32 else narrow[i]
-        return span, pltpu.make_async_copy(held.at[span], dst[i].at[span], store_sem.at[i, part])
+        return span, pltpu.make_async_copy(held.at[span], dst[i].at[span], store_sem.at[i])
 
     for i in range(count):
         pltpu.make_async_copy(src[i], narrow[i], load_sem.at[i]).wait()
@@ -815,28 +818,29 @@
                 wide[i][span, :] = narrow[i][span, :].astype(F32)
             copy.start()
     for i in range(count):
-        for part in range(4):
-            piece(i, part, 4)[1].wait()
-
-
-def widen_call(arrays, types):
+        piece(i, 0, 1)[1].wait()
+
+
+def widen_call(gains, arrays, types):
     v = pltpu.VMEM
     hbm = pl.BlockSpec(memory_space=pltpu.HBM)
+    vm = pl.BlockSpec(memory_space=pltpu.VMEM)
     count = len(arrays)
     return pl.pallas_call(
         lambda *refs: widen_kernel(count, *refs),
-        out_shape=tuple(jax.ShapeDtypeStruct(a.shape, t) for a, t in zip(arrays, types)),
-        in_specs=[hbm] * count,
-        out_specs=tuple([hbm] * count),
+        out_shape=tuple(jax.ShapeDtypeStruct(a.shape, t) for a, t in zip(arrays, types))
+        + (jax.ShapeDtypeStruct(gains.shape[1:], F32),) * 2,
+        in_specs=[vm] + [hbm] * count,
+        out_specs=tuple([hbm] * count) + (vm, vm),
         scratch_shapes=[
             *[v(a.shape, a.dtype) for a in arrays],
             *[v(a.shape if t == F32 else (16, 128), F32) for a, t in zip(arrays, types)],
             pltpu.SemaphoreType.DMA((count,)),
-            pltpu.SemaphoreType.DMA((count, 4)),
+            pltpu.SemaphoreType.DMA((count,)),
         ],
         compiler_params=pltpu.CompilerParams(vmem_limit_bytes=VMEM_LIMIT),
         name="widen",
-    )(*arrays)
+    )(gains, *arrays)
 
 
 def add_rows(target, parts, rows, step):
@@ -862,7 +866,8 @@
     n1_t_hbm,
     x_hbm,
     mid_hbm,
-    parts_hbm,
+    inner_hbm,
+    wd_hbm,
     back_hbm,
     n2_t_hbm,
     g_hbm,
@@ -884,6 +889,7 @@
     out_gain,
     out_dx,
     out_result,
+    parts_hbm,
     p_zone,
     b_zone,
     w_buf,
@@ -959,8 +965,6 @@
     outer_to = (s_id, jnp.where(has_outer, l_id - toward, l_id + toward), c_id)
     peers = [env.peer(k) for k in range(1, shards)]
     mates = [env.mate(k) for k in range(1, line)]
-    env.barrier([sibling] + peers + mates)
-
     half = width // 2
     wide_pieces = 8
     down_pieces = 8 if feed % 128 == 0 else 4
@@ -988,13 +992,10 @@
         return remote(
             parts_hbm.at[peer_of(s_id, shards, k, False)],
             p_zone.at[k - 1],
-            p_send.at[k - 1],
-            p_recv.at[k - 1],
+            p_send.at[0],
+            p_recv.at[0],
             peers[k - 1],
         )
-
-    for k in range(1, shards):
-        back_copy(k).start()
 
     def local(src, dst, sem):
         return pltpu.make_async_copy(src, dst, sem)
@@ -1011,7 +1012,7 @@
                 start = core * half + piece * rows_
                 return array_of.at[pl.ds(pl.multiple_of(start, 16), rows_)]
 
-            return rows_, bufs, out
+            return rows_, bufs, out, array
         rows_ = feed // down_pieces
         span = pl.ds(pl.multiple_of((index - 2 * wide_pieces) * rows_, 16), rows_)
         bufs = [ref.at[span] for ref in (own_dn, got_dn_x, got_dn_r, got_dn_t)]
@@ -1019,7 +1020,7 @@
         def out(core):
             return out_dn.at[span, pl.ds(pl.multiple_of(core * half, 128), half)]
 
-        return rows_, bufs, out
+        return rows_, bufs, out, 2
 
     def split(action):
         def run(index):
@@ -1036,28 +1037,28 @@
         return run
 
     def up_end(index, where):
-        count, (mine, extra, came, total), _ = views(index, where)
+        count, (mine, extra, came, total), _, array = views(index, where)
         add_rows(mine, [mine, extra], count, slab)
-        send_up(index, mine, came, total)
+        send_up(index, mine, came, total, array)
 
     def up_inner(index, where):
-        count, (mine, extra, came, total), _ = views(index, where)
-        remote(mine, came, up_send.at[index], r_recv.at[index], inner_to).wait_recv()
+        count, (mine, extra, came, total), _, array = views(index, where)
+        remote(mine, came, up_send.at[array], r_recv.at[index], inner_to).wait_recv()
         add_rows(mine, [mine, extra, came], count, slab)
-        send_up(index, mine, came, total)
-
-    def send_up(index, mine, came, total):
+        send_up(index, mine, came, total, array)
+
+    def send_up(index, mine, came, total, array):
         @pl.when(is_mid)
         def _():
-            remote(mine, total, up_send.at[index], t_recv.at[index], inner_to).start()
+            remote(mine, total, up_send.at[array], t_recv.at[index], inner_to).start()
 
         @pl.when(jnp.logical_not(is_mid))
         def _():
-            remote(mine, came, up_send.at[index], r_recv.at[index], inner_to).start()
+            remote(mine, came, up_send.at[array], r_recv.at[index], inner_to).start()
 
     def down(index, where):
-        count, (mine, _, _, total), out = views(index, where)
-        remote(mine, total, up_send.at[index], t_recv.at[index], inner_to).wait_recv()
+        count, (mine, _, _, total), out, array = views(index, where)
+        remote(mine, total, up_send.at[array], t_recv.at[index], inner_to).wait_recv()
 
         @pl.when(is_mid)
         def _():
@@ -1065,23 +1066,35 @@
 
         @pl.when(has_outer)
         def _():
-            remote(total, total, down_send.at[index], t_recv.at[index], outer_to).start()
-
-        remote(total, out(c_id), sib_send.at[index], sib_recv.at[index], sibling).start()
-        local(total, out(c_id), local_sem.at[index]).start()
-
-    def settle(index, where):
-        _, (mine, _, _, total), out = views(index, where)
-        remote(mine, total, up_send.at[index], t_recv.at[index], inner_to).wait_send()
+            remote(total, total, down_send.at[array], t_recv.at[index], outer_to).start()
+
+        remote(total, out(c_id), sib_send.at[array], sib_recv.at[array], sibling).start()
+        local(total, out(c_id), local_sem.at[array]).start()
+
+    def settle(array):
+        if array < 2:
+            mine, total = own_gu.at[array], got_gu_t.at[array]
+            out_of = (out_gate, out_up)[array]
+            outs = [
+                out_of.at[pl.ds(pl.multiple_of(core * half, 16), half)]
+                for core in (c_id, 1 - c_id)
+            ]
+        else:
+            mine, total = own_dn, got_dn_t
+            outs = [
+                out_dn.at[:, pl.ds(pl.multiple_of(core * half, 128), half)]
+                for core in (c_id, 1 - c_id)
+            ]
+        remote(mine, total, up_send.at[array], t_recv.at[0], inner_to).wait_send()
 
         @pl.when(has_outer)
         def _():
-            remote(total, total, down_send.at[index], t_recv.at[index], outer_to).wait_send()
-
-        remote(total, out(1 - c_id), sib_send.at[index], sib_recv.at[index], sibling).wait()
-        local(total, out(c_id), local_sem.at[index]).wait()
-
-    up_end, up_inner, down, settle = [split(f) for f in (up_end, up_inner, down, settle)]
+            remote(total, total, down_send.at[array], t_recv.at[0], outer_to).wait_send()
+
+        remote(total, outs[1], sib_send.at[array], sib_recv.at[array], sibling).wait()
+        local(total, outs[0], local_sem.at[array]).wait()
+
+    up_end, up_inner, down = [split(f) for f in (up_end, up_inner, down)]
 
     def of_turns(first, last):
         return min(2 * first, chunks), min(2 * last, chunks)
@@ -1124,6 +1137,16 @@
         def _():
             run_all(down, *of_turns(first, last))
 
+    def first_send(src, part_):
+        span = pl.ds(part_ * (half // 2), half // 2)
+        return remote(
+            src.at[0, span],
+            got_gu_x.at[0, span],
+            core_sem.at[3 * part_],
+            core_sem.at[6 + part_],
+            sibling,
+        )
+
     def core_send(array, src):
         dst = got_gu_x.at[array] if array < 2 else got_dn_x
         return remote(src, dst, core_sem.at[array], core_sem.at[3 + array], sibling)
@@ -1132,7 +1155,9 @@
 
     load_mid = local(mid_hbm, mid_ref, late_sem.at[0])
 
-    def feed_grads(g_v, g_own, dgate_v, dup_v, wide_t, near_t, inner_t, far_gu, far_dn):
+    def feed_grads(
+        g_v, g_own, dgate_v, dup_v, wide_t, near_t, inner_t, far_gu, far_dn, inner_v, wd_v, stage_v
+    ):
         loads = [
             local(src, dst, load_sem.at[i])
             for i, (src, dst) in enumerate(
@@ -1155,24 +1180,35 @@
         load_own.start()
         load_mid.start()
         load_wo.start()
+        load_inner = local(inner_hbm, inner_v, late_sem.at[4])
+        load_wd = local(wd_hbm, wd_v, late_sem.at[5])
+        load_inner.start()
+        load_wd.start()
+        env.barrier([sibling] + peers + mates)
+        for k in range(1, shards):
+            back_copy(k).start()
 
         def flat(ref):
             return ref[...].reshape(tokens, ref.shape[2])
 
         loads[0].wait()
         loads[1].wait()
-        far_gu[0] = nn(wide_t[...], flat(dgate_v)).astype(BF)
-        core_send(0, far_gu.at[0]).start()
-        load_near.wait()
-        own_gu[0] = nn(near_t[...], flat(dgate_v)).astype(BF)
-        core_send(0, far_gu.at[0]).wait()
-        ends_up(0, 4)
+        split_at = half // 2
+        for part_ in range(2):
+            span = pl.ds(part_ * split_at, split_at)
+            far_gu[0, span, :] = nn(wide_t[span, :], flat(dgate_v)).astype(BF)
+            first_send(far_gu, part_).start()
+            if part_ == 0:
+                load_near.wait()
+            own_gu[0, span, :] = nn(near_t[span, :], flat(dgate_v)).astype(BF)
+            first_send(far_gu, part_).wait()
+            ends_up(2 * part_, 2 * part_ + 2)
         loads[2].wait()
         far_gu[1] = nn(wide_t[...], flat(dup_v)).astype(BF)
         core_send(1, far_gu.at[1]).start()
         own_gu[1] = nn(near_t[...], flat(dup_v)).astype(BF)
         core_send(1, far_gu.at[1]).wait()
-        ends_up(4, 7)
+        ends_up(4, 8)
         loads[3].wait()
         loads[4].wait()
         far_dn[...] = nn(inner_t[...], g_v[:, :, far_half].reshape(tokens, half)).astype(BF)
@@ -1180,6 +1216,24 @@
         own_dn[...] = nn(inner_t[...], g_v[:, :, near_half].reshape(tokens, half)).astype(BF)
         ring(0)
         core_send(2, far_dn).wait()
+        load_inner.wait()
+        load_wd.wait()
+
+        def part_keep(k):
+            return local(stage_v.at[k % 2], parts_hbm.at[k], late_sem.at[6 + k % 2])
+
+        def project(k, carry):
+            @pl.when(k >= 2)
+            def _():
+                part_keep(k - 2).wait()
+
+            stage_v[k % 2] = nn(inner_v[k], wd_v[...]).astype(BF)
+            part_keep(k).start()
+            return carry
+
+        lax.fori_loop(0, shards, project, 0)
+        for k in range(shards - 2, shards):
+            part_keep(k).wait()
         ring(1)
         own_back = local(back_hbm.at[s_id], g_v.at[0], load_sem.at[shards - 1])
         own_back.start()
@@ -1219,6 +1273,9 @@
         v((feed, tokens), BF),
         v((2, half, feed), BF),
         v((feed, half), BF),
+        v((shards, rows, feed), BF),
+        v((feed, width), BF),
+        v((2, rows, width), BF),
     )
 
     def attention(
@@ -1290,14 +1347,13 @@
             return remote(
                 box.at[peer_of(s_id, shards, k, False)],
                 zone.at[k - 1],
-                g_send.at[slot, k - 1],
-                g_recv.at[slot, k - 1],
+                g_send.at[slot],
+                g_recv.at[slot],
                 peers[k - 1],
             )
 
         def gather_part(box, zone, slot):
-            for k in range(1, shards):
-                scatter_copy(box, zone, slot, k).wait()
+            remote(zone, zone, g_send.at[slot], g_recv.at[slot], peers[0]).wait()
             add_rows(
                 box.at[s_id],
                 [box.at[s_id]] + [zone.at[k] for k in range(shards - 1)],
@@ -1305,22 +1361,22 @@
                 slab,
             )
 
-        def line_up(mine, came, total, slot, count):
+        def line_up(mine, came, total, slot, count, group):
             @pl.when(has_outer)
             def _():
-                remote(mine, came, a_up.at[slot], a_r.at[slot], inner_to).wait_recv()
+                remote(mine, came, a_up.at[group], a_r.at[slot], inner_to).wait_recv()
                 add_rows(mine, [mine, came], count, slab if mine.dtype == BF else 8)
 
             @pl.when(is_mid)
             def _():
-                remote(mine, total, a_up.at[slot], a_t.at[slot], inner_to).start()
+                remote(mine, total, a_up.at[group], a_t.at[slot], inner_to).start()
 
             @pl.when(jnp.logical_not(is_mid))
             def _():
-                remote(mine, came, a_up.at[slot], a_r.at[slot], inner_to).start()
-
-        def line_down(mine, total, slot, count, ready, outs):
-            remote(mine, total, a_up.at[slot], a_t.at[slot], inner_to).wait()
+                remote(mine, came, a_up.at[group], a_r.at[slot], inner_to).start()
+
+        def line_down(mine, total, slot, count, group, ready, outs):
+            remote(mine, total, a_up.at[group], a_t.at[slot], inner_to).wait_recv()
 
             @pl.when(is_mid)
             def _():
@@ -1328,7 +1384,7 @@
 
             @pl.when(has_outer)
             def _():
-                remote(total, total, a_down.at[slot], a_t.at[slot], outer_to).start()
+                remote(total, total, a_down.at[group], a_t.at[slot], outer_to).start()
 
             if ready is not None:
                 ready()
@@ -1337,10 +1393,12 @@
                     remote(src, near, a_sib_send.at[box], a_sib_recv.at[box], sibling).start()
                 local(src, near, a_local.at[box]).start()
 
-        def line_settle(total, slot, outs):
+        def line_settle(mine, total, group, outs):
+            remote(mine, total, a_up.at[group], a_t.at[0], inner_to).wait_send()
+
             @pl.when(has_outer)
             def _():
-                remote(total, total, a_down.at[slot], a_t.at[slot], outer_to).wait_send()
+                remote(total, total, a_down.at[group], a_t.at[0], outer_to).wait_send()
 
             for src, near, far, box in outs:
                 if far is not None:
@@ -1493,7 +1551,7 @@
             return remote(
                 dkv_x.at[pl.ds(seq * HK, HK), dest],
                 dkv_z.at[seq, way, dest],
-                dkv_send.at[seq, way * line + dest],
+                dkv_send.at[seq, 0],
                 dkv_recv.at[seq, way * line + dest],
                 to,
             )
@@ -1533,15 +1591,9 @@
                 for k in range(1, line):
                     dkv_copy(seq, k).wait()
                 return
+            sent = dkv_x.at[pl.ds(seq * HK, HK), pl.ds(0, line - 1)]
+            remote(sent, sent, dkv_send.at[seq, 0], dkv_recv.at[seq, 0], mates[0]).wait_send()
             for dest in range(line):
-
-                @pl.when(l_id < dest)
-                def _():
-                    dkv_hop(seq, 0, dest).wait_send()
-
-                @pl.when(l_id > dest)
-                def _():
-                    dkv_hop(seq, 1, dest).wait_send()
 
                 @pl.when((l_id == dest) & (l_id > 0))
                 def _():
@@ -1573,44 +1625,57 @@
 
         near = c_id * own_rows
         far = (1 - c_id) * own_rows
-        pieces = 2 if own_rows % 32 == 0 else 1
-
-        def jobs_of(box, came, total, slot, outs_of):
+        pieces = 5
+
+        def rows_at(out, start, first, count):
+            return out.at[pl.ds(pl.multiple_of(start + first, 16), count)]
+
+        def jobs_of(box, came, total, group, outs_of):
             count = own_rows // pieces
             result = []
             for piece in range(pieces):
                 span = pl.ds(piece * count, count)
-
-                def rows_at(out, start, piece=piece):
-                    return out.at[pl.ds(pl.multiple_of(start + piece * count, 16), count)]
-
-                ready, outs = outs_of(total.at[span], span, slot + piece, rows_at)
+                ready, outs = outs_of(total, piece * count, count)
                 result.append(
-                    (box.at[s_id, span], came.at[span], total.at[span], slot + piece, count)
-                    + (ready, outs)
+                    (box.at[s_id, span], came.at[span], total.at[span], group * pieces + piece)
+                    + (count, group, ready, outs)
                 )
             return result
 
-        def plain(out):
-            def outs_of(total, span, slot, rows_at):
-                return None, [(total, rows_at(out, near), rows_at(out, far), slot)]
+        def plain(out, box):
+            def outs_of(total, first, count):
+                return None, [
+                    (
+                        total.at[pl.ds(first, count)],
+                        rows_at(out, near, first, count),
+                        rows_at(out, far, first, count),
+                        box,
+                    )
+                ]
 
             return outs_of
 
-        def unpacked(total, span, slot, rows_at):
+        def unpacked(total, first, count):
+            span = pl.ds(first, count)
+
             def ready():
-                value = total[...].astype(F32)
-                for half_, first in ((0, 0), (1, HD)):
+                value = total[span, :].astype(F32)
+                for half_, start in ((0, 0), (1, HD)):
                     k_nat[half_, span, :] = jnp.concatenate(
                         [
-                            value[:, head * 128 + first : head * 128 + first + HD]
+                            value[:, head * 128 + start : head * 128 + start + HD]
                             for head in range(HK)
                         ],
                         1,
                     ).astype(BF)
 
             outs = [
-                (k_nat.at[half_, span], rows_at(out, near), rows_at(out, far), slot + 3 * half_)
+                (
+                    k_nat.at[half_, span],
+                    rows_at(out, near, first, count),
+                    rows_at(out, far, first, count),
+                    2 + half_,
+                )
                 for half_, out in ((0, out_wk), (1, out_wv))
             ]
             return ready, outs
@@ -1622,28 +1687,28 @@
                 chosen = jnp.where(s_id == s, value[:, s * part : (s + 1) * part], chosen)
             gn_out[...] = chosen
 
-        o_jobs = jobs_of(o_x, o_r, o_t, 0, plain(out_wo))
-        q_jobs = jobs_of(q_x, q_r, q_t, 2, plain(out_wq))
-        k_jobs = jobs_of(k_x, k_r, k_t, 4, unpacked)
-        gain_job = [(gn_x, gn_r, gn_t, 6, 8, own_gain, [(gn_out, out_gain, None, 6)])]
+        o_jobs = jobs_of(o_x, o_r, o_t, 0, plain(out_wo, 0))
+        q_jobs = jobs_of(q_x, q_r, q_t, 1, plain(out_wq, 1))
+        k_jobs = jobs_of(k_x, k_r, k_t, 2, unpacked)
+        gain_job = [
+            (gn_x, gn_r, gn_t, 3 * pieces, 8, 3, own_gain, [(gn_out, out_gain, None, 4)])
+        ]
         jobs = o_jobs + q_jobs + gain_job + k_jobs
 
         def first_up(some):
             @pl.when(jnp.logical_not(has_outer))
             def _():
-                for mine, came, total, slot, count, _, _ in some:
-                    line_up(mine, came, total, slot, count)
+                for job in some:
+                    line_up(*job[:6])
 
         def job_up(job):
-            mine, came, total, slot, count, _, _ = job
-
             @pl.when(has_outer)
             def _():
-                line_up(mine, came, total, slot, count)
+                line_up(*job[:6])
 
         def job_down(job):
-            mine, _, total, slot, count, ready, outs = job
-            line_down(mine, total, slot, count, ready, outs)
+            mine, _, total, slot, count, group, ready, outs = job
+            line_down(mine, total, slot, count, group, ready, outs)
 
         lax.fori_loop(0, 2 * blocks, attend, 0)
         ring(4)
@@ -1667,19 +1732,20 @@
         weight_grad(n1_t_ref, dq, g_buf, shards)
         core_part(g_buf, q_x, 1).start()
         dkv_scatter(1)
-        ends_up(7, turns)
-        ring_down(5)
+        ends_up(8, turns)
+        ring(7)
+        ring_down(6)
         dkv_hops(0)
         scatter_part(g_buf, q_x, q_z, 1)
         gather_part(o_x, o_z, 0)
         first_up(o_jobs)
         dkv_hops(1)
-        ring_down(6)
+        ring_down(7)
         load_wq.wait()
         load_wkv.wait()
         back = nt(dq[...], w_buf[...])
         ends_down(0, 3)
-        ring(7, 8)
+        ring(8, 16)
         dkv_gather(0)
         dkv_gather(1)
         g_kv = g_buf.at[:, :, pl.ds(0, 2 * HK * HD)]
@@ -1687,7 +1753,7 @@
         core_part(g_kv, k_x, 2).start()
         back = back + nt(dkv_own[...], wkv_buf[...])
         scatter_part(g_kv, k_x, k_z, 2)
-        ring(8, 1)
+        ring(9, 1)
         hidden = x_ref[...].astype(F32)
         scale = lax.rsqrt(jnp.mean(hidden * hidden, -1, keepdims=True) + EPSILON)
         scaled = back * gains_ref[0:1, :]
@@ -1707,7 +1773,7 @@
 
         def gain_copy(k):
             return remote(
-                gn_own, gn_z.at[k - 1], g_send.at[3, k - 1], g_recv.at[3, k - 1], peers[k - 1]
+                gn_own, gn_z.at[k - 1], g_send.at[3], g_recv.at[3], peers[k - 1]
             )
 
         for k in range(1, shards):
@@ -1716,8 +1782,7 @@
             part_copy(k).start()
 
         def gather_gain():
-            for k in range(1, shards):
-                gain_copy(k).wait()
+            remote(gn_z, gn_z, g_send.at[3], g_recv.at[3], peers[0]).wait()
             total = gn_own[...]
             for k in range(shards - 1):
                 total = total + gn_z[k]
@@ -1726,26 +1791,21 @@
         @pl.when(jnp.logical_not(has_outer))
         def _():
             gather_part(q_x, q_z, 1)
-            for mine, came, total, slot, count, _, _ in q_jobs:
-                line_up(mine, came, total, slot, count)
+            for job in q_jobs:
+                line_up(*job[:6])
             gather_gain()
             gather_part(k_x, k_z, 2)
-            for mine, came, total, slot, count, _, _ in gain_job + k_jobs:
-                line_up(mine, came, total, slot, count)
+            for job in gain_job + k_jobs:
+                line_up(*job[:6])
 
         @pl.when(has_outer)
         def _():
-            ring(9, 1)
-            gather_part(q_x, q_z, 1)
             ring(10, 1)
-            gather_gain()
-            gather_part(k_x, k_z, 2)
             ring(11, 1)
 
         ends_down(3, 8)
         def finish_result():
-            for k in range(1, shards):
-                part_copy(k).wait()
+            remote(p_zone, p_zone, p_send.at[0], p_recv.at[0], peers[0]).wait()
             result = mid_ref[...]
             for first in range(0, shards, 4):
                 stage = [
@@ -1765,18 +1825,38 @@
             local(dproj, out_result, late_sem.at[2]).start()
 
         todo = list(jobs)
-        done = [todo.pop(0)]
-        job_up(done[-1])
-        ring(turns, 1)
+        done = []
+
+        def next_up():
+            done.append(todo.pop(0))
+            job_up(done[-1])
+
+        def last_chunk(index):
+            @pl.when(is_mid)
+            def _():
+                down(index)
+
+        next_up()
+        next_up()
+        last_chunk(2 * turns - 2)
+        next_up()
+        last_chunk(2 * turns - 1)
+        next_up()
+
+        @pl.when(has_outer)
+        def _():
+            gather_part(q_x, q_z, 1)
+            gather_gain()
+            gather_part(k_x, k_z, 2)
+
         ends_down(8, turns)
 
         @pl.when(jnp.logical_not(has_outer))
         def _():
             finish_result()
 
-        for job in todo:
-            job_up(job)
-            done.append(job)
+        while todo:
+            next_up()
             job_down(done.pop(0))
         for job in done:
             job_down(job)
@@ -1785,8 +1865,22 @@
         def _():
             finish_result()
 
-        for _, _, total, slot, _, _, outs in jobs:
-            line_settle(total, slot, outs)
+        whole = [
+            (o_x.at[s_id], o_t, [(o_t, out_wo, 0)]),
+            (q_x.at[s_id], q_t, [(q_t, out_wq, 1)]),
+            (k_x.at[s_id], k_t, [(k_nat.at[0], out_wk, 2), (k_nat.at[1], out_wv, 3)]),
+        ]
+        for group, (mine, total, outs) in enumerate(whole):
+            line_settle(
+                mine,
+                total,
+                group,
+                [
+                    (src, rows_at(out, near, 0, own_rows), rows_at(out, far, 0, own_rows), box)
+                    for src, out, box in outs
+                ],
+            )
+        line_settle(gn_x, gn_t, 3, [(gn_out, out_gain, None, 4)])
         keep_dx.wait()
         local(dproj, out_result, late_sem.at[2]).wait()
 
@@ -1809,15 +1903,12 @@
         v((rows, width), BF),
     )
 
-    def last(index, carry):
-        settle(index)
-        return carry
-
-    lax.fori_loop(0, chunks, last, 0)
+    for array in range(3):
+        settle(array)
 
 
 def backward_call(shards, line, *arrays):
-    x, kv, gate = arrays[7], arrays[-1], arrays[14]
+    x, kv, gate = arrays[7], arrays[-1], arrays[15]
     rows, width = x.shape
     keys = kv.shape[1]
     feed = gate.shape[2]
@@ -1861,16 +1952,28 @@
         dma((max(6, shards),)),
         dma((2,)),
         dma((2,)),
-        dma((6,)),
-        *[dma((24,)) for _ in range(7)],
+        dma((8,)),
+        dma((3,)),
+        dma((24,)),
+        dma((24,)),
+        *[dma((3,)) for _ in range(4)],
         dma((4,)),
-        dma((2, 2 * line)),
+        dma((2, 1 if line == 4 else line)),
         dma((2, 2 * line)),
         dma((8,)),
-        dma((4, shards - 1)),
-        dma((4, shards - 1)),
-        *[dma((9,)) for _ in range(7)],
-        *[dma((shards - 1,)) for _ in range(4)],
+        dma((4,)),
+        dma((4,)),
+        dma((4,)),
+        dma((16,)),
+        dma((16,)),
+        dma((4,)),
+        dma((4,)),
+        dma((4,)),
+        dma((5,)),
+        dma((1,)),
+        dma((1,)),
+        dma((shards - 1,)),
+        dma((shards - 1,)),
         dma((9,)),
     ]
     return pl.pallas_call(
@@ -1886,11 +1989,12 @@
             shape((8, part), F32),
             shape((rows, width), BF),
             shape((rows, width), BF),
+            shape((shards, rows, width), BF),
             shape((shards - 1, rows, width), BF),
             shape((shards - 1, rows, width), BF),
         ),
-        in_specs=[vm] * 3 + [hbm] * 18,
-        out_specs=tuple([hbm] * 12),
+        in_specs=[vm] * 3 + [hbm] * 19,
+        out_specs=tuple([hbm] * 13),
         scratch_shapes=scratch,
         compiler_params=pltpu.CompilerParams(
             collective_id=3, has_side_effects=True, vmem_limit_bytes=VMEM_LIMIT
@@ -1935,7 +2039,7 @@
         norm_t,
         packed_q,
         middle,
-        parts,
+        inner,
         back,
         norm_all_t,
         inner_t,
@@ -1947,7 +2051,8 @@
         positions,
         lengths,
         frequency,
-        jnp.stack([attn_gain, mlp_gain]),
+        attn_gain,
+        mlp_gain,
         w_key,
         w_value,
         x,
@@ -1971,6 +2076,7 @@
         result,
         _,
         _,
+        _,
     ) = backward_call(
         shards,
         line,
@@ -1983,7 +2089,8 @@
         norm_t,
         x,
         middle,
-        parts,
+        inner,
+        w_down,
         back,
         norm_all_t,
         grad_all,
@@ -1997,18 +2104,18 @@
         packed_kv.reshape(seqs * HK, -1, 128),
     )
     arrays = [sum_gate, sum_up, sum_down, sum_query, sum_out, sum_key, sum_value]
-    arrays = widen_call(arrays + [grad_input, result], [F32] * 7 + [BF] * 2)
+    arrays = widen_call(sum_gain, arrays + [grad_input, result], [F32] * 7 + [BF] * 2)
     sum_gate, sum_up, sum_down, sum_query, sum_out, sum_key, sum_value = arrays[:7]
-    grad_input, result = arrays[7:]
+    grad_input, result, gain_one, gain_two = arrays[7:]
     return (
         result.reshape(seqs, stretch, width),
         grad_input.reshape(seqs, stretch, width),
-        sum_gain[0],
+        gain_one,
         sum_query,
         sum_key,
         sum_value,
         sum_out,
-        sum_gain[1],
+        gain_two,
         sum_gate,
         sum_up,
         sum_down,

time: 259 us -> 250 us (0.965)
  Pallas kernels: 255 us -> 249 us
  local copies, waits for them, and re-layouts: 2.75 us -> 0 us
    pallas_call x1, Pallas kernels: 147 us -> 142 us  [backward_call(): pl.pallas_call(lambda *refs: backward_kernel(sizes, *refs), out_shape=(sh...]
where the time goes in v6:
time: 250 us
  Pallas kernels  249 us (100%)
    pallas_call x1, Pallas kernels, backward_call(): pl.pallas_call(lambda *refs: backward_kernel(sizes, *refs), out_shape=(sh...  142 us
    pallas_call x1, Pallas kernels, front_call(): pl.pallas_call(lambda *refs: front_kernel((shards, line, keys, rows, widt...  95.7 us
    pallas_call x1, Pallas kernels, widen_call(): pl.pallas_call(lambda *refs: widen_kernel(count, *refs), out_shape=tuple(...  10.7 us

profile of v6, /device:TPU:0, one launch (start us, length us, event | category | flops | bytes accessed | tf_op | source)
XLA Modules:
  0.0 249.6 jit_solution(7389515022560743146)
XLA Ops:
  0.6 95.7 %front.1 = (f32[8,1280]{1,0:T(8,128)}, f32[256,128]{1,0:T(8,128)}, f32[256,128]{1,0:T(8,128)}, bf16[1280,1280]{1,0:T(8,128)(2,1)}, bf16[1280,640]{1,0:T(8,128)(2...) custom-call(s32[2,1024]{1,0:T(2,128)} %refs_0_.1, ...), custom_call_target="tpu_custom_call" | custom-call | tf_op jit(solution)/shard_map/front/pallas_call | solution.py:727
  96.4 142.3 %backward.1 = (bf16[1280,896]{1,0:T(8,128)(2,1)}, bf16[1280,896]{1,0:T(8,128)(2,1)}, bf16[896,1280]{1,0:T(8,128)(2,1)}, bf16[320,1280]{1,0:T(8,128)(2,1)}, bf16[...) custom-call(f32[8,1280]{1,0:T(8,128)} %get-tuple-element.52.refs_0_,, ...), custom_call_target="tpu_custom_call" | custom-call | tf_op jit(solution)/shard_map/backward/pallas_call | solution.py:1979
  238.7 10.7 %widen.1 = (f32[1280,896]{1,0:T(8,128)}, f32[1280,896]{1,0:T(8,128)}, f32[896,1280]{1,0:T(8,128)}, f32[320,1280]{1,0:T(8,128)}, f32[320,1280]{1,0:T(8,128)}, /*i...) custom-call(f32[8,320]{1,0:T(8,128)} %get-tuple-element.72.refs_0_, ...), custom_call_target="tpu_custom_call" | custom-call | tf_op jit(solution)/shard_map/widen/pallas_call | solution.py:829

commit v7 on v6

--- a/solution.py
+++ b/solution.py
@@ -59,8 +59,9 @@
 
 
 class Spread:
-    def __init__(self, env, block, source, sems, shared):
+    def __init__(self, env, block, source, sems, shared, size):
         self.env, self.block, self.source, self.shared = env, block, source, shared
+        self.size = size
         self.send, self.recv, self.sib_send, self.sib_recv = sems
         self.relay = env.shards == 4
 
@@ -69,7 +70,7 @@
         return env.remote(
             self.source,
             self.block(env.s_id, env.c_id, 0, 2),
-            self.send.at[k],
+            self.send.at[0],
             self.recv.at[k],
             env.peer(k),
         )
@@ -78,7 +79,7 @@
         env = self.env
         piece = self.block(env.origin(k), env.c_id, k - 1, 1)
         return env.remote(
-            piece, piece, self.send.at[2 + k], self.recv.at[2 + k], env.peer(3 - k)
+            piece, piece, self.send.at[0], self.recv.at[2 + k], env.peer(3 - k)
         )
 
     def direct(self):
@@ -91,7 +92,7 @@
     def sib_copy(self, k):
         piece = self.block(self.env.origin(k), self.env.c_id, 0, 2)
         return self.env.remote(
-            piece, piece, self.sib_send.at[k], self.sib_recv.at[k], self.env.sibling
+            piece, piece, self.sib_send.at[0], self.sib_recv.at[k], self.env.sibling
         )
 
     def forward(self):
@@ -115,13 +116,13 @@
                 self.sib_copy(k).wait_recv()
 
     def settle(self):
-        for k in self.direct():
-            self.copy(k).wait_send()
-            if self.relay:
-                self.passing(k).wait_send()
+        env = self.env
+        piece = self.size(env.shards - 1)
+        env.remote(piece, piece, self.send.at[0], self.recv.at[0], env.peer(1)).wait_send()
         if self.shared:
-            for k in range(1, self.env.shards):
-                self.sib_copy(k).wait_send()
+            env.remote(
+                piece, piece, self.sib_send.at[0], self.sib_recv.at[0], env.sibling
+            ).wait_send()
 
 
 class Env:
@@ -146,11 +147,17 @@
     def mate(self, k):
         return (self.s_id, lax.rem(self.l_id + k, self.line), self.c_id)
 
-    def barrier(self, others):
+    def greet(self, others):
         barrier = pltpu.get_barrier_semaphore()
         for other in others:
             pl.semaphore_signal(barrier, inc=1, device_id=other, device_id_type=BY_MESH)
-        pl.semaphore_wait(barrier, len(others))
+
+    def meet(self, others):
+        pl.semaphore_wait(pltpu.get_barrier_semaphore(), len(others))
+
+    def barrier(self, others):
+        self.greet(others)
+        self.meet(others)
 
 
 def front_kernel(
@@ -274,9 +281,27 @@
 
         return block
 
-    grad_gather = Spread(env, tokens_of(g_all), g_all.at[s_id], (g_s, g_r, None, None), False)
+    def first_tokens(ref):
+        return lambda count: ref.at[pl.ds(0, count)]
+
+    def first_rows(ref):
+        return lambda count: ref.at[pl.ds(0, count * hp)]
+
+    grad_gather = Spread(
+        env,
+        tokens_of(g_all),
+        g_all.at[s_id],
+        (g_s, g_r, None, None),
+        False,
+        first_tokens(g_all),
+    )
     n2_gather = Spread(
-        env, tokens_of(n2_all), n2_all.at[s_id], (n2_send, n2_recv, None, None), False
+        env,
+        tokens_of(n2_all),
+        n2_all.at[s_id],
+        (n2_send, n2_recv, None, None),
+        False,
+        first_tokens(n2_all),
     )
 
     def rows_of(ref):
@@ -291,10 +316,29 @@
     own = pl.ds(pl.multiple_of(s_id * part, 16), part)
     kv_mine = pl.ds(pl.multiple_of(s_id * part + c_id * hp, 16), hp)
     kv_gather = Spread(
-        env, rows_of(wkv_all), wkv_all.at[kv_mine], (wkv_s, wkv_r, wkv_ss, wkv_sr), True
+        env,
+        rows_of(wkv_all),
+        wkv_all.at[kv_mine],
+        (wkv_s, wkv_r, wkv_ss, wkv_sr),
+        True,
+        first_rows(wkv_all),
     )
-    q_gather = Spread(env, rows_of(wq_all), wq_ref.at[mine], (wq_s, wq_r, wq_ss, wq_sr), True)
-    o_gather = Spread(env, rows_of(wo_all), wo_ref.at[mine], (wo_s, wo_r, wo_ss, wo_sr), True)
+    q_gather = Spread(
+        env,
+        rows_of(wq_all),
+        wq_ref.at[mine],
+        (wq_s, wq_r, wq_ss, wq_sr),
+        True,
+        first_rows(wq_all),
+    )
+    o_gather = Spread(
+        env,
+        rows_of(wo_all),
+        wo_ref.at[mine],
+        (wo_s, wo_r, wo_ss, wo_sr),
+        True,
+        first_rows(wo_all),
+    )
     outs = [
         pltpu.make_async_copy(src, dst, keep_sem.at[i])
         for i, (src, dst) in enumerate(
@@ -385,7 +429,7 @@
         def kv_sib(seq, src):
             piece = kv_slice(seq, src, c_id)
             return env.remote(
-                piece, piece, kv_sib_send.at[seq, src], kv_sib_recv.at[seq, src], env.sibling
+                piece, piece, kv_sib_send.at[seq], kv_sib_recv.at[seq], env.sibling
             )
 
         def kv_onward(seq, way, src):
@@ -409,8 +453,10 @@
                     kv_sib(seq, src).start()
 
         def kv_finish(seq):
-            for src in range(line):
-                kv_sib(seq, src).wait()
+            piece = kv_all.at[pl.ds(seq * HK, HK), pl.ds(0, line)]
+            env.remote(
+                piece, piece, kv_sib_send.at[seq], kv_sib_recv.at[seq], env.sibling
+            ).wait()
 
         def kv_settle(seq):
             for src in range(line):
@@ -612,12 +658,12 @@
             source = peer_of(s_id, shards, k, True)
             cols = pl.ds(pl.multiple_of(source * rows, 128), rows)
             return [
-                pltpu.make_async_copy(n2_t.at[k], out_n2_t.at[:, cols], out_sem.at[k, 0]),
-                pltpu.make_async_copy(inner_t.at[k], out_inner_t.at[:, cols], out_sem.at[k, 1]),
-                pltpu.make_async_copy(dgate.at[source], out_dgate.at[source], out_sem.at[k, 2]),
-                pltpu.make_async_copy(dup.at[source], out_dup.at[source], out_sem.at[k, 3]),
-                pltpu.make_async_copy(g_all.at[source], out_g.at[source], out_sem.at[k, 4]),
-                pltpu.make_async_copy(inner.at[source], out_inner.at[source], out_sem.at[k, 5]),
+                pltpu.make_async_copy(n2_t.at[k], out_n2_t.at[:, cols], out_sem.at[0]),
+                pltpu.make_async_copy(inner_t.at[k], out_inner_t.at[:, cols], out_sem.at[1]),
+                pltpu.make_async_copy(dgate.at[source], out_dgate.at[source], out_sem.at[2]),
+                pltpu.make_async_copy(dup.at[source], out_dup.at[source], out_sem.at[3]),
+                pltpu.make_async_copy(g_all.at[source], out_g.at[source], out_sem.at[4]),
+                pltpu.make_async_copy(inner.at[source], out_inner.at[source], out_sem.at[5]),
             ]
 
         def block(k, carry):
@@ -689,9 +735,11 @@
         loads[0].wait()
         loads[1].wait()
         lax.fori_loop(0, shards, block, 0)
-        for k in range(shards):
-            for copy in outs(k):
-                copy.wait()
+        whole = ((g_all, out_g), (inner, out_inner), (dgate, out_dgate), (dup, out_dup))
+        for index, (src, dst) in zip((4, 5, 2, 3), whole):
+            pltpu.make_async_copy(src, dst, out_sem.at[index]).wait()
+        pltpu.make_async_copy(out_n2_t, out_n2_t, out_sem.at[0]).wait()
+        pltpu.make_async_copy(out_inner_t, out_inner_t, out_sem.at[1]).wait()
         n2_gather.settle()
         grad_gather.settle()
         for last in (2, 1):
@@ -773,18 +821,19 @@
             v((shards, 8, part), F32),
             dma((shards,)),
             dma((shards,)),
-            *[dma((hops,)) for _ in range(16)],
+            *[dma((n,)) for n in (1, hops, 1, shards) * 3],
+            *[dma((n,)) for n in (1, hops) * 2],
             dma((2, 2 * line)),
             dma((2, line)),
-            dma((2, line)),
-            dma((2, line)),
+            dma((2,)),
+            dma((2,)),
             dma((2,)),
             dma((4,)),
             dma((3,)),
             dma((9,)),
             dma((2,)),
             dma((2,)),
-            dma((shards, 6)),
+            dma((6,)),
         ],
         compiler_params=pltpu.CompilerParams(
             collective_id=1, has_side_effects=True, vmem_limit_bytes=VMEM_LIMIT
@@ -928,6 +977,7 @@
     pt_sem,
     kv_sem,
     core_sem,
+    first_sem,
     up_send,
     r_recv,
     t_recv,
@@ -965,6 +1015,7 @@
     outer_to = (s_id, jnp.where(has_outer, l_id - toward, l_id + toward), c_id)
     peers = [env.peer(k) for k in range(1, shards)]
     mates = [env.mate(k) for k in range(1, line)]
+    env.greet([sibling] + peers + mates)
     half = width // 2
     wide_pieces = 8
     down_pieces = 8 if feed % 128 == 0 else 4
@@ -1100,13 +1151,11 @@
         return min(2 * first, chunks), min(2 * last, chunks)
 
     def run_all(action, first, last):
-        if last > first:
-
-            def body(index, carry):
-                action(index)
-                return carry
-
-            lax.fori_loop(first, last, body, 0)
+        def body(index, carry):
+            action(index)
+            return carry
+
+        lax.fori_loop(first, last, body, 0)
 
     def ends_up(first, last):
         @pl.when(jnp.logical_not(has_outer))
@@ -1137,13 +1186,16 @@
         def _():
             run_all(down, *of_turns(first, last))
 
+    def quarter_span(part_):
+        return pl.ds(pl.multiple_of(part_ * (half // 4), 16), half // 4)
+
     def first_send(src, part_):
-        span = pl.ds(part_ * (half // 2), half // 2)
+        span = quarter_span(part_)
         return remote(
             src.at[0, span],
             got_gu_x.at[0, span],
-            core_sem.at[3 * part_],
-            core_sem.at[6 + part_],
+            first_sem.at[part_],
+            first_sem.at[4 + part_],
             sibling,
         )
 
@@ -1184,25 +1236,39 @@
         load_wd = local(wd_hbm, wd_v, late_sem.at[5])
         load_inner.start()
         load_wd.start()
-        env.barrier([sibling] + peers + mates)
-        for k in range(1, shards):
-            back_copy(k).start()
 
         def flat(ref):
             return ref[...].reshape(tokens, ref.shape[2])
 
         loads[0].wait()
         loads[1].wait()
-        split_at = half // 2
-        for part_ in range(2):
-            span = pl.ds(part_ * split_at, split_at)
+
+        def quarter(part_, carry):
+            span = quarter_span(part_)
             far_gu[0, span, :] = nn(wide_t[span, :], flat(dgate_v)).astype(BF)
+
+            @pl.when(part_ == 0)
+            def _():
+                env.meet([sibling] + peers + mates)
+
             first_send(far_gu, part_).start()
-            if part_ == 0:
+
+            @pl.when(part_ == 0)
+            def _():
+                for k in range(1, shards):
+                    back_copy(k).start()
                 load_near.wait()
+
             own_gu[0, span, :] = nn(near_t[span, :], flat(dgate_v)).astype(BF)
             first_send(far_gu, part_).wait()
-            ends_up(2 * part_, 2 * part_ + 2)
+
+            @pl.when(jnp.logical_not(has_outer))
+            def _():
+                run_all(up_end, part_ * wide_pieces // 4, (part_ + 1) * wide_pieces // 4)
+
+            return carry
+
+        lax.fori_loop(0, 4, quarter, 0)
         loads[2].wait()
         far_gu[1] = nn(wide_t[...], flat(dup_v)).astype(BF)
         core_send(1, far_gu.at[1]).start()
@@ -1365,7 +1431,7 @@
             @pl.when(has_outer)
             def _():
                 remote(mine, came, a_up.at[group], a_r.at[slot], inner_to).wait_recv()
-                add_rows(mine, [mine, came], count, slab if mine.dtype == BF else 8)
+                add_rows(mine, [mine, came], count, slab if mine.dtype == BF else 2)
 
             @pl.when(is_mid)
             def _():
@@ -1380,7 +1446,7 @@
 
             @pl.when(is_mid)
             def _():
-                add_rows(total, [mine, total], count, slab if mine.dtype == BF else 8)
+                add_rows(total, [mine, total], count, slab if mine.dtype == BF else 2)
 
             @pl.when(has_outer)
             def _():
@@ -1556,25 +1622,24 @@
                 to,
             )
 
-        def dkv_hops(seq):
+        def dkv_hops(seq, outward):
             if not hops:
                 return
             low = l_id < line // 2
-            for first in (True, False):
-                for step in range(1, line):
-                    for way, dest in ((0, line - step), (1, step - 1)):
-                        ahead = (
-                            (l_id > 0) & (l_id < dest)
-                            if way == 0
-                            else (l_id < line - 1) & (l_id > dest)
-                        )
-                        turn_now = low if first == (way == 0) else jnp.logical_not(low)
-
-                        @pl.when(ahead & turn_now)
-                        def _():
-                            dkv_hop(seq, way, dest).wait_recv()
-                            dkv_take(seq, way, dest)
-                            dkv_hop(seq, way, dest).start()
+            for step in range(1, line):
+                for way, dest in ((0, line - step), (1, step - 1)):
+                    ahead = (
+                        (l_id > 0) & (l_id < dest)
+                        if way == 0
+                        else (l_id < line - 1) & (l_id > dest)
+                    )
+                    turn_now = jnp.logical_not(low) if outward == (way == 0) else low
+
+                    @pl.when(ahead & turn_now)
+                    def _():
+                        dkv_hop(seq, way, dest).wait_recv()
+                        dkv_take(seq, way, dest)
+                        dkv_hop(seq, way, dest).start()
 
         def dkv_take(seq, way, dest):
             def body(head, carry):
@@ -1691,7 +1756,7 @@
         q_jobs = jobs_of(q_x, q_r, q_t, 1, plain(out_wq, 1))
         k_jobs = jobs_of(k_x, k_r, k_t, 2, unpacked)
         gain_job = [
-            (gn_x, gn_r, gn_t, 3 * pieces, 8, 3, own_gain, [(gn_out, out_gain, None, 4)])
+            (gn_x, gn_r, gn_t, 3 * pieces, 2, 3, own_gain, [(gn_out, out_gain, None, 4)])
         ]
         jobs = o_jobs + q_jobs + gain_job + k_jobs
 
@@ -1733,13 +1798,16 @@
         core_part(g_buf, q_x, 1).start()
         dkv_scatter(1)
         ends_up(8, turns)
-        ring(7)
+        ring(7, 16)
+        dkv_hops(0, False)
+        scatter_part(g_buf, q_x, q_z, 1)
+        ring_down(5)
         ring_down(6)
-        dkv_hops(0)
-        scatter_part(g_buf, q_x, q_z, 1)
+        dkv_hops(1, False)
         gather_part(o_x, o_z, 0)
         first_up(o_jobs)
-        dkv_hops(1)
+        dkv_hops(0, True)
+        dkv_hops(1, True)
         ring_down(7)
         load_wq.wait()
         load_wkv.wait()
@@ -1758,7 +1826,6 @@
         scale = lax.rsqrt(jnp.mean(hidden * hidden, -1, keepdims=True) + EPSILON)
         scaled = back * gains_ref[0:1, :]
         gn_own[0:1, :] = jnp.sum(back * hidden * scale, 0, keepdims=True)
-        gn_own[2:8, :] = jnp.zeros((6, width), F32)
         gain_core = remote(gn_own, gn_x, g_core.at[6], g_core.at[7], sibling)
         gain_core.start()
         x_ref[...] = (
@@ -1942,16 +2009,17 @@
         *boxes(width),
         *boxes(width),
         *boxes(kv_width),
-        v((8, width), F32),
-        v((8, width), F32),
-        v((shards - 1, 8, width), F32),
-        v((8, width), F32),
-        v((8, width), F32),
+        v((2, width), F32),
+        v((2, width), F32),
+        v((shards - 1, 2, width), F32),
+        v((2, width), F32),
+        v((2, width), F32),
         v((2, own_rows, HK * HD), BF),
-        v((8, part), F32),
+        v((2, part), F32),
         dma((max(6, shards),)),
         dma((2,)),
         dma((2,)),
+        dma((6,)),
         dma((8,)),
         dma((3,)),
         dma((24,)),
@@ -1986,7 +2054,7 @@
             shape((part, width), BF),
             shape((part, HK * HD), BF),
             shape((part, HK * HD), BF),
-            shape((8, part), F32),
+            shape((2, part), F32),
             shape((rows, width), BF),
             shape((rows, width), BF),
             shape((shards, rows, width), BF),

time: 250 us -> 249 us (level)
  no operation moved by 1% of the time
where the time goes in v7:
time: 249 us; the launch traced here: 248 us
  Pallas kernels  247 us (99%)
    pallas_call x1, Pallas kernels, backward_call(): pl.pallas_call(lambda *refs: backward_kernel(sizes, *refs), out_shape=(sh...  142 us
    pallas_call x1, Pallas kernels, front_call(): pl.pallas_call(lambda *refs: front_kernel((shards, line, keys, rows, widt...  95.1 us
    pallas_call x1, Pallas kernels, widen_call(): pl.pallas_call(lambda *refs: widen_kernel(count, *refs), out_shape=tuple(...  10.7 us

profile of v7, /device:TPU:0, one launch (start us, length us, event | category | flops | bytes accessed | tf_op | source)
XLA Modules:
  0.0 248.3 jit_solution(16067086356186578778)
XLA Ops:
  0.6 95.1 %front.1 = (f32[8,1280]{1,0:T(8,128)}, f32[256,128]{1,0:T(8,128)}, f32[256,128]{1,0:T(8,128)}, bf16[1280,1280]{1,0:T(8,128)(2,1)}, bf16[1280,640]{1,0:T(8,128)(2...) custom-call(s32[2,1024]{1,0:T(2,128)} %refs_0_.1, ...), custom_call_target="tpu_custom_call" | custom-call | tf_op jit(solution)/shard_map/front/pallas_call | solution.py:775
  95.8 141.7 %backward.1 = (bf16[1280,896]{1,0:T(8,128)(2,1)}, bf16[1280,896]{1,0:T(8,128)(2,1)}, bf16[896,1280]{1,0:T(8,128)(2,1)}, bf16[320,1280]{1,0:T(8,128)(2,1)}, bf16[...) custom-call(f32[8,1280]{1,0:T(8,128)} %get-tuple-element.52.refs_0_,, ...), custom_call_target="tpu_custom_call" | custom-call | tf_op jit(solution)/shard_map/backward/pallas_call | solution.py:2047
  237.5 10.7 %widen.1 = (f32[1280,896]{1,0:T(8,128)}, f32[1280,896]{1,0:T(8,128)}, f32[896,1280]{1,0:T(8,128)}, f32[320,1280]{1,0:T(8,128)}, f32[320,1280]{1,0:T(8,128)}, /*i...) custom-call(f32[2,320]{1,0:T(2,128)} %get-tuple-element.72.refs_0_, ...), custom_call_target="tpu_custom_call" | custom-call | tf_op jit(solution)/shard_map/widen/pallas_call | solution.py:878
